TPU v7x, 128 devices: a whole 4x4x4 slice. The times are simulated.
128 devices in a mesh: ctx: 32 (over z, x, core), exp: 4 (over y).
Axes of the slice: x: 4, y: 4, z: 4, core: 2. Of those that a mesh axis runs over, the one named last changes fastest.
Arguments:
- queries: bfloat16 [4096, 4096], P('ctx', 'exp'), may hold values from -5 to 5
- keys: bfloat16 [4096, 1024], P('ctx', 'exp'), may hold values from -5 to 5
- values: bfloat16 [4096, 1024], P('ctx', 'exp'), may hold values from -6 to 6
- resid_in: bfloat16 [4096, 4096], P(('ctx', 'exp')), may hold values from -6 to 6
- span_order: int32 [64], replicated, may hold values from 0 to 63, each once
- out_weight: bfloat16 [4096, 4096], P('exp'), may hold values from -0.09375 to 0.09375
- norm_gain: float32 [4096], replicated, may hold values from 0.25 to 1.75
- router: float32 [4096, 4], replicated, may hold values from -0.09375 to 0.09375
- expert_ids: int32 [4096, 2], P(('ctx', 'exp')), may hold values from 0 to 3, all different within a row; in each aligned block of 32 rows (0 to 31, 32 to 63, ...) at most 16 rows name the same one
- w_gate: bfloat16 [4, 4096, 14336], P('exp', None, 'ctx'), may hold values from -0.09375 to 0.09375
- w_up: bfloat16 [4, 4096, 14336], P('exp', None, 'ctx'), may hold values from -0.09375 to 0.09375
- w_down: bfloat16 [4, 14336, 4096], P('exp', 'ctx'), may hold values from -0.046875 to 0.046875
Outputs:
- mixed: bfloat16 [4096, 4096], P(('ctx', 'exp'))
Inputs may be any that keep to these rules, and one draw needn't show every extreme that they name: `expert_ids`: A token's 2 ids differ. In every aligned block of 32 tokens, each of the 4 experts is named by exactly 16 tokens. `span_order`: each span number appears once.
All inputs are finite; a program needn't handle non-finite values.
Results may differ from a plain program's by a relative error of at most 0.012.
Values may be sent and summed in bfloat16 or wider, within the bound.
No kernel may reach another device: no remote copies, remote signals or barrier semaphores. Data moves between devices by JAX's collectives and lax.ppermute only.
A program may use at most 128 MiB of HBM per device.

v0:
```python
import math

import jax
import jax.numpy as jnp
from jax import lax
from jax.experimental import pallas as pl
from jax.experimental.pallas import tpu as pltpu
from jax.sharding import PartitionSpec as P

HEAD_SIZE = 128
SPAN = 64
RING = 4
NEVER = -1e30

f32 = jnp.float32
bf16 = jnp.bfloat16
i32 = jnp.int32


def ctx_index_of(z, x, core):
    return (z % RING) * 8 + (x % RING) * 2 + core


def ring_pairs(phase, step):
    pairs = []
    for z in range(RING):
        for x in range(RING):
            for core in range(2):
                along_x = (core == 0) == (phase == 1)
                target = ctx_index_of(z, x + step, core) if along_x else ctx_index_of(z + step, x, core)
                pairs.append((ctx_index_of(z, x, core), target))
    return pairs


RINGS = {(phase, step): ring_pairs(phase, step) for phase in (1, 2) for step in (1, -1, 2)}
SWAP = [(i, i ^ 1) for i in range(32)]


def shift(a, phase, step):
    return lax.ppermute(a, "ctx", RINGS[phase, step])


def swap(a):
    return lax.ppermute(a, "ctx", SWAP)


def shift_exp(a, step):
    return lax.ppermute(a, "exp", [(i, (i + step) % 4) for i in range(4)])


def join(*parts):
    return jnp.concatenate(parts, axis=0)


def total(*terms):
    return sum(t.astype(f32) for t in terms).astype(bf16)


def positions_of(span_ids, span_order):
    matches = span_ids[:, None] == jnp.arange(span_order.shape[0], dtype=i32)[None, :]
    starts = jnp.sum(jnp.where(matches, span_order[None, :], 0), axis=1) * SPAN
    return (starts[:, None] + jnp.arange(SPAN, dtype=i32)[None, :]).reshape(-1)


def attend_blocks(q_ref, qpos_ref, kpos_ref, kv_refs, old, m_ref, l_ref, acc_ref):
    tok = q_ref.shape[0]
    kv_heads = kv_refs[0].shape[1] // (2 * HEAD_SIZE)
    cluster = q_ref.shape[1] // HEAD_SIZE // kv_heads
    rows = cluster * tok
    slope = math.log2(math.e) / math.sqrt(HEAD_SIZE)
    masks = []
    for n, kv in enumerate(kv_refs):
        keep = kpos_ref[n : n + 1, :] <= qpos_ref[:, 0:1]
        masks.append(jnp.where(keep, 0.0, NEVER))
    for h in range(kv_heads):
        q = jnp.concatenate(
            [q_ref[:, (h * cluster + g) * HEAD_SIZE : (h * cluster + g + 1) * HEAD_SIZE] for g in range(cluster)],
            axis=0,
        )
        at = pl.ds(h * rows, rows)
        if old is not None:
            m = jnp.max(old[0][at, :], axis=1, keepdims=True)
            l = jnp.max(old[1][at, :], axis=1, keepdims=True)
            acc = old[2][at, :]
        for n, kv in enumerate(kv_refs):
            k = kv[:, h * HEAD_SIZE : (h + 1) * HEAD_SIZE]
            v = kv[:, (kv_heads + h) * HEAD_SIZE : (kv_heads + h + 1) * HEAD_SIZE]
            s = lax.dot_general(q, k, (((1,), (1,)), ((), ())), preferred_element_type=f32)
            s = (s.reshape(cluster, tok, -1) * slope + masks[n][None]).reshape(rows, -1)
            top = jnp.max(s, axis=1, keepdims=True)
            if old is None and n == 0:
                m = top
                p = jnp.exp2(s - m)
                l = jnp.sum(p, axis=1, keepdims=True)
                acc = jnp.dot(p.astype(bf16), v, preferred_element_type=f32)
            else:
                new = jnp.maximum(m, top)
                fade = jnp.exp2(m - new)
                p = jnp.exp2(s - new)
                l = l * fade + jnp.sum(p, axis=1, keepdims=True)
                acc = acc * fade + jnp.dot(p.astype(bf16), v, preferred_element_type=f32)
                m = new
        m_ref[at, :] = jnp.broadcast_to(m, (rows, HEAD_SIZE))
        l_ref[at, :] = jnp.broadcast_to(l, (rows, HEAD_SIZE))
        acc_ref[at, :] = acc


def vmem_spec():
    return pl.BlockSpec(memory_space=pltpu.VMEM)


def attend_cost(q, kvs):
    work = q.shape[0] * q.shape[1] * sum(kv.shape[0] for kv in kvs)
    return pl.CostEstimate(flops=8 * work, transcendentals=work // HEAD_SIZE, bytes_accessed=4 << 20)


def attend_part(q, qpos, kpos, kvs, state):
    heads = q.shape[1] // HEAD_SIZE
    rows = heads * q.shape[0]
    first = state is None

    def kernel(*refs):
        q_ref, qpos_ref, kpos_ref = refs[:3]
        kv_refs = refs[3 : 3 + len(kvs)]
        m_ref, l_ref, acc_ref = refs[-3:]
        old = None if first else refs[3 + len(kvs) : 6 + len(kvs)]
        attend_blocks(q_ref, qpos_ref, kpos_ref, kv_refs, old, m_ref, l_ref, acc_ref)

    operands = (q, qpos, kpos, *kvs) + (() if first else tuple(state))
    shape = jax.ShapeDtypeStruct((rows, HEAD_SIZE), f32)
    return pl.pallas_call(
        kernel,
        out_shape=(shape, shape, shape),
        in_specs=[vmem_spec()] * len(operands),
        out_specs=(vmem_spec(),) * 3,
        cost_estimate=attend_cost(q, kvs),
        compiler_params=pltpu.CompilerParams(vmem_limit_bytes=40 << 20),
        name="attend_part",
    )(*operands)


def attend_last(mine, q, qpos, kpos, kvs, state, out_weight):
    tok = q.shape[0]
    heads = q.shape[1] // HEAD_SIZE
    rows = heads * tok
    sub = tok // 4
    width = out_weight.shape[1]

    def kernel(mine_ref, *refs):
        q_ref, qpos_ref, kpos_ref = refs[:3]
        kv_refs = refs[3 : 3 + len(kvs)]
        old = refs[3 + len(kvs) : 6 + len(kvs)]
        weight_hbm = refs[6 + len(kvs)]
        outs = refs[7 + len(kvs) : 11 + len(kvs)]
        m_ref, l_ref, acc_ref, weight, attended, ordered, sem = refs[11 + len(kvs) :]
        fetch = pltpu.make_async_copy(weight_hbm, weight, sem)
        fetch.start()
        attend_blocks(q_ref, qpos_ref, kpos_ref, kv_refs, old, m_ref, l_ref, acc_ref)
        for h in range(heads):
            at = pl.ds(h * tok, tok)
            attended[:, h * HEAD_SIZE : (h + 1) * HEAD_SIZE] = (acc_ref[at, :] / l_ref[at, :]).astype(bf16)
        for r in range(4):
            start = pl.multiple_of(lax.rem(mine_ref[0] + r, 4) * sub, sub)
            ordered[r * sub : (r + 1) * sub, :] = attended[pl.ds(start, sub), :]
        fetch.wait()
        for n in range(4):
            at = pl.ds(n * (width // 4), width // 4)
            product = jnp.dot(ordered[...], weight[:, at], preferred_element_type=f32)
            for r in range(4):
                outs[r][:, at] = product[r * sub : (r + 1) * sub].astype(outs[r].dtype)

    operands = (q, qpos, kpos, *kvs, *state)
    return pl.pallas_call(
        kernel,
        out_shape=tuple(jax.ShapeDtypeStruct((sub, width), t) for t in (f32, bf16, bf16, bf16)),
        in_specs=[pl.BlockSpec(memory_space=pltpu.SMEM)]
        + [vmem_spec()] * len(operands)
        + [pl.BlockSpec(memory_space=pl.ANY)],
        out_specs=(vmem_spec(),) * 4,
        scratch_shapes=[
            pltpu.VMEM((rows, HEAD_SIZE), f32),
            pltpu.VMEM((rows, HEAD_SIZE), f32),
            pltpu.VMEM((rows, HEAD_SIZE), f32),
            pltpu.VMEM(out_weight.shape, bf16),
            pltpu.VMEM((tok, q.shape[1]), bf16),
            pltpu.VMEM((tok, q.shape[1]), bf16),
            pltpu.SemaphoreType.DMA,
        ],
        cost_estimate=attend_cost(q, kvs),
        compiler_params=pltpu.CompilerParams(vmem_limit_bytes=40 << 20),
        name="attend_last",
    )(mine, *operands, out_weight)


def expert_rows(pieces, own, other):
    hid, depth = own[0].shape
    width = own[2].shape[1]
    chunks = 4
    deep, wide = depth // chunks, width // chunks
    sizes = [p.shape[0] for p in pieces]
    rows = sum(sizes)
    count = len(pieces)
    starts = [sum(sizes[:i]) for i in range(count)]

    def kernel(*refs):
        ins, refs = refs[:count], refs[count:]
        (ga, ua, da, gb, ub, db), refs = refs[:6], refs[6:]
        outs, refs = refs[:count], refs[count:]
        x, w, dw, sums, hidden, out, x_sems, w_sems, d_sems, out_sems = refs

        def first_copies(k):
            at = pl.ds(pl.multiple_of(k * deep, deep), deep)
            for i, ref in enumerate((ga, gb, ua, ub)):
                yield pltpu.make_async_copy(ref.at[:, at], w.at[k, pl.ds(i * hid, hid), :], w_sems.at[k, i])
            for i, ref in enumerate(ins):
                yield pltpu.make_async_copy(
                    ref.at[:, at], x.at[k, pl.ds(starts[i], sizes[i]), :], x_sems.at[k, i]
                )

        def last_copies(n):
            at = pl.ds(pl.multiple_of(n * wide, wide), wide)
            for i, ref in enumerate((da, db)):
                yield pltpu.make_async_copy(ref.at[:, at], dw.at[n, pl.ds(i * hid, hid), :], d_sems.at[n, i])

        def out_copies(n):
            at = pl.ds(pl.multiple_of(n * wide, wide), wide)
            for i, ref in enumerate(outs):
                yield pltpu.make_async_copy(
                    out.at[n, pl.ds(starts[i], sizes[i]), :], ref.at[:, at], out_sems.at[n, i]
                )

        for k in range(chunks):
            for copy in first_copies(k):
                copy.start()
        for n in range(chunks):
            for copy in last_copies(n):
                copy.start()
        sums[...] = jnp.zeros_like(sums)

        @pl.loop(0, chunks)
        def _(k):
            for copy in first_copies(k):
                copy.wait()
            sums[...] += lax.dot_general(x[k], w[k], (((1,), (1,)), ((), ())), preferred_element_type=f32)

        hidden[...] = (jax.nn.silu(sums[:, : 2 * hid]) * sums[:, 2 * hid :]).astype(bf16)

        @pl.loop(0, chunks)
        def _(n):
            for copy in last_copies(n):
                copy.wait()
            out[n] = jnp.dot(hidden[...], dw[n], preferred_element_type=f32).astype(bf16)
            for copy in out_copies(n):
                copy.start()

        for n in range(chunks):
            for copy in out_copies(n):
                copy.wait()

    anywhere = pl.BlockSpec(memory_space=pl.ANY)
    return pl.pallas_call(
        kernel,
        out_shape=tuple(jax.ShapeDtypeStruct((size, width), bf16) for size in sizes),
        in_specs=[anywhere] * (count + 6),
        out_specs=(anywhere,) * count,
        scratch_shapes=[
            pltpu.VMEM((chunks, rows, deep), bf16),
            pltpu.VMEM((chunks, 4 * hid, deep), bf16),
            pltpu.VMEM((chunks, 2 * hid, wide), bf16),
            pltpu.VMEM((rows, 4 * hid), f32),
            pltpu.VMEM((rows, 2 * hid), bf16),
            pltpu.VMEM((chunks, rows, wide), bf16),
            pltpu.SemaphoreType.DMA((chunks, count)),
            pltpu.SemaphoreType.DMA((chunks, 4)),
            pltpu.SemaphoreType.DMA((chunks, 2)),
            pltpu.SemaphoreType.DMA((chunks, count)),
        ],
        cost_estimate=pl.CostEstimate(
            flops=12 * rows * depth * hid, transcendentals=2 * rows * hid, bytes_accessed=12 * depth * hid
        ),
        compiler_params=pltpu.CompilerParams(vmem_limit_bytes=(26 << 20) + rows * (32 << 10)),
        name="expert_rows",
    )(*pieces, *own, *other)


def layer(
    queries,
    keys,
    values,
    resid_in,
    span_order,
    out_weight,
    norm_gain,
    router,
    expert_ids,
    w_gate,
    w_up,
    w_down,
):
    me = lax.axis_index("ctx")
    mine = lax.axis_index("exp").astype(i32)
    my_z, my_x, my_core = me // 8, (me // 2) % RING, me % 2

    kv = jnp.concatenate((keys, values), axis=1)
    near = join(kv, shift(kv, 1, 1), shift(kv, 1, -1), shift(kv, 1, 2))
    left, right = shift(near, 2, 1), shift(near, 2, -1)
    far = shift(near, 2, 2)

    def block_positions(seconds):
        spans = []
        for second in seconds:
            for core in (my_core, 1 - my_core):
                a = jnp.array([0, -1, 1, 2], i32)
                z = jnp.where(core == 0, my_z + second, my_z + a) % RING
                x = jnp.where(core == 0, my_x + a, my_x + second) % RING
                block = z * 8 + x * 2 + core
                spans.append((block[:, None] * 2 + jnp.arange(2, dtype=i32)[None, :]).reshape(-1))
        return positions_of(jnp.concatenate(spans), span_order).reshape(2 * len(seconds), -1)

    query_pos = positions_of(me * 2 + jnp.arange(2, dtype=i32), span_order)
    query_pos = jnp.broadcast_to(query_pos[:, None], (query_pos.shape[0], HEAD_SIZE))
    near_other, far_other = swap(near), swap(far)
    left_other, right_other = swap(left), swap(right)
    state = attend_part(queries, query_pos, block_positions((0,)), (near, near_other), None)
    state = attend_part(
        queries,
        query_pos,
        block_positions((-1, 1)),
        (left, left_other, right, right_other),
        state,
    )
    sum0, sum1, sum2, sum3 = attend_last(
        mine.reshape(1), queries, query_pos, block_positions((2,)), (far, far_other), state, out_weight
    )

    sub = resid_in.shape[0]
    back2, back1, back3 = shift_exp(sum2, 2), shift_exp(sum1, 1), shift_exp(sum3, 3)
    own_sum = (sum0 + back2.astype(f32)) + (back1.astype(f32) + back3.astype(f32))
    stream = (resid_in.astype(f32) + own_sum).astype(bf16)
    stream_wide = stream.astype(f32)
    mean_square = jnp.mean(stream_wide * stream_wide, axis=-1, keepdims=True)
    normed = (stream_wide * lax.rsqrt(mean_square + 1e-05) * norm_gain).astype(bf16)
    logits = jnp.dot(normed.astype(f32), router, precision=lax.Precision.HIGHEST)
    experts = router.shape[1]
    expert_axis = (mine + jnp.arange(experts, dtype=i32)) % experts
    picked = expert_ids[:, :, None] == jnp.arange(experts, dtype=i32)[None, None, :]
    chosen = jnp.sum(jnp.where(picked, logits[:, None, :], 0.0), axis=-1)
    mixing = jax.nn.softmax(chosen, axis=-1)
    picked = expert_ids[:, :, None] == expert_axis[None, None, :]
    token_weight = jnp.sum(jnp.where(picked, mixing[:, :, None], 0.0), axis=1)
    routed = jnp.any(picked, axis=1)
    rank_of = jnp.cumsum(routed.astype(i32), axis=0) - 1
    slot_count = sub * expert_ids.shape[1] // experts
    slot_axis = jnp.arange(slot_count, dtype=i32)
    placing = jnp.logical_and(routed.T[:, None, :], rank_of.T[:, None, :] == slot_axis[None, :, None])
    outgoing = jnp.dot(
        placing.reshape(experts * slot_count, sub).astype(bf16), normed, preferred_element_type=f32
    ).astype(bf16)
    o0, o1, o2, o3 = (outgoing[i * slot_count : (i + 1) * slot_count] for i in range(4))
    rows = join(o0, shift_exp(o1, 1), shift_exp(o2, 2), shift_exp(o3, 3))

    own = (w_gate[0].T, w_up[0].T, w_down[0])
    other = tuple(swap(w) for w in own)
    n0 = join(rows, shift(rows, 1, 1))
    n1 = join(shift(rows, 1, -1), shift(rows, 1, 2))
    l0, r0 = shift(n0, 2, 1), shift(n0, 2, -1)
    r1, l1 = shift(n1, 2, -1), shift(n1, 2, 1)
    f0, f1 = shift(l0, 2, 1), shift(r1, 2, -1)

    n0, n1 = expert_rows((n0, n1), own, other)
    l0, l1, r0, r1 = expert_rows((l0, l1, r0, r1), own, other)
    f0, f1 = expert_rows((f0, f1), own, other)

    u1, v0 = shift(l1, 2, -1), shift(r0, 2, 1)
    q0, q1 = shift(f0, 2, -1), shift(f1, 2, 1)
    u0, v1 = shift(total(l0, q0), 2, -1), shift(total(r1, q1), 2, 1)
    n0, n1 = total(n0, u0, v0), total(n1, u1, v1)
    part = rows.shape[0]
    back = (shift(n0[part:], 1, -1), shift(n1[:part], 1, 1), shift(n1[part:], 1, 2))
    own_rows = total(n0[:part], *back)

    r0, r1, r2, r3 = (own_rows[i * slot_count : (i + 1) * slot_count] for i in range(4))
    returned = join(r0, shift_exp(r1, 3), shift_exp(r2, 2), shift_exp(r3, 1))
    coefficient = placing.astype(f32) * token_weight.T[:, None, :]
    combined = jnp.einsum("est,esd->td", coefficient, returned.reshape(experts, slot_count, -1).astype(f32))
    return (stream_wide + combined).astype(bf16)


def solution(mesh):
    placed = (
        P("ctx", "exp"),
        P("ctx", "exp"),
        P("ctx", "exp"),
        P(("ctx", "exp"), None),
        P(),
        P("exp", None),
        P(),
        P(),
        P(("ctx", "exp"), None),
        P("exp", None, "ctx"),
        P("exp", None, "ctx"),
        P("exp", "ctx", None),
    )
    return jax.shard_map(layer, mesh=mesh, in_specs=placed, out_specs=P(("ctx", "exp"), None), check_vma=False)
```

profile of v0, /device:TPU:0, one launch (start us, length us, event | category | flops | bytes accessed | tf_op | source)
XLA Modules:
  0.0 219.0 jit_solution(7029101720422587128)
XLA Ops:
  1.7 1.6 collective-permute-start
  3.3 1.6 collective-permute-start.1
  5.0 1.9 collective-permute-start.2
  11.5 2.1 collective-permute-start.5
  13.6 2.2 %collective-permute-start.7 = (bf16[512,512]{1,0:T(8,128)(2,1)S(1)}, bf16[512,512]{1,0:T(8,128)(2,1)S(1)}, u32[]{:S(2)}, u32[]{:S(2)}) collective-permute-start(bf16[512,512]{1,0:T(8,128)(2,1)S(1)} %pad_maximum_fusion.refs_3_), channel_id=1, source_target_pairs={{0,96},{4,28},{8,104},{12,4},{16,112},{20,12},{24,120},{28,20},{32... | collective-permute-start | bytes 1572872 | tf_op jit(solution)/shard_map/ppermute | solution.py:40
  16.7 1.9 collective-permute-start.3
  18.8 4.0 %collective-permute-done.5.refs_3_ = bf16[512,512]{1,0:T(8,128)(2,1)S(1)} collective-permute-done((bf16[512,512]{1,0:T(8,128)(2,1)S(1)}, bf16[512,512]{1,0:T(8,128)(2,1)S(1)}, u32[]{:S(2)}, u32[]{:S(2)}) %collective-permute-start.5) | collective-permute-done | bytes 524320 | tf_op jit(solution)/shard_map/ppermute | solution.py:40
  22.9 5.3 %collective-permute-done.7.refs_5_ = bf16[512,512]{1,0:T(8,128)(2,1)S(1)} collective-permute-done((bf16[512,512]{1,0:T(8,128)(2,1)S(1)}, bf16[512,512]{1,0:T(8,128)(2,1)S(1)}, u32[]{:S(2)}, u32[]{:S(2)}) %collective-permute-start.7) | collective-permute-done | bytes 524320 | tf_op jit(solution)/shard_map/ppermute | solution.py:40
  28.1 1.8 collective-permute-done.3.refs_3_
  31.0 1.7 attend_part.2
  32.7 3.7 %attend_part.3 = (f32[1024,128]{1,0:T(8,128)S(1)}, f32[1024,128]{1,0:T(8,128)S(1)}, f32[1024,128]{1,0:T(8,128)S(1)}) custom-call(bf16[128,1024]{1,0:T(8,128)(2,1)S(1)} %copy-done.9, s32[128,128]{1,0:T(8,128)S(1)} %broadcast_in_dim.96.refs_1_, s32[4,512]{1,0:T(4,128)S(1)} %broadcast_add_fusion.refs_2_, bf16[512,512]{1,0:T(8,128)(2,1)S(1)} %collective-permute-done.5.refs_3_, ...), custom_call_target="tpu_custom_call" | custom-call | flops 2147483648 | bytes 4194304 | tf_op jit(solution)/shard_map/attend_part/pallas_call | solution.py:131
  36.5 3.8 %attend_last.1 = (f32[32,4096]{1,0:T(8,128)S(1)}, bf16[32,4096]{1,0:T(8,128)(2,1)S(1)}, bf16[32,4096]{1,0:T(8,128)(2,1)S(1)}, bf16[32,4096]{1,0:T(8,128)(2,1)S(1)}) custom-call(s32[1]{0:T(128)} %bitcast.mine_ref, bf16[128,1024]{1,0:T(8,128)(2,1)S(1)} %copy-done.9, s32[128,128]{1,0:T(8,128)S(1)} %broadcast_in_dim.96.refs_1_, ...), custom_call_target="tpu_custom_call" | custom-call | flops 1073741824 | bytes 4194304 | tf_op jit(solution)/shard_map/attend_last/pallas_call | solution.py:173
  40.3 3.3 %collective-permute-start.10 = (bf16[32,4096]{1,0:T(8,128)(2,1)S(1)}, bf16[32,4096]{1,0:T(8,128)(2,1)S(1)}, u32[]{:S(2)}, u32[]{:S(2)}) collective-permute-start(bf16[32,4096]{1,0:T(8,128)(2,1)S(1)} %get-tuple-element.30), channel_id=1, source_target_pairs={{0,2},{1,3},{2,0},{3,1},{4,6},{5,7},{6,4},{7,5},{8,10},{9,11},{10,... | collective-permute-start | bytes 786440 | tf_op jit(solution)/shard_map/ppermute | solution.py:48
  44.3 2.6 %collective-permute-start.12 = (bf16[32,4096]{1,0:T(8,128)(2,1)S(1)}, bf16[32,4096]{1,0:T(8,128)(2,1)S(1)}, u32[]{:S(2)}, u32[]{:S(2)}) collective-permute-start(bf16[32,4096]{1,0:T(8,128)(2,1)S(1)} %get-tuple-element.32), channel_id=1, source_target_pairs={{0,3},{1,0},{2,1},{3,2},{4,7},{5,4},{6,5},{7,6},{8,11},{9,8},{10,9... | collective-permute-start | bytes 786440 | tf_op jit(solution)/shard_map/ppermute | solution.py:48
  47.3 3.8 %collective-permute-done.10 = bf16[32,4096]{1,0:T(8,128)(2,1)S(1)} collective-permute-done((bf16[32,4096]{1,0:T(8,128)(2,1)S(1)}, bf16[32,4096]{1,0:T(8,128)(2,1)S(1)}, u32[]{:S(2)}, u32[]{:S(2)}) %collective-permute-start.10) | collective-permute-done | bytes 262176 | tf_op jit(solution)/shard_map/ppermute | solution.py:48
  51.1 5.1 %collective-permute-done.11 = bf16[32,4096]{1,0:T(8,128)(2,1)S(1)} collective-permute-done((bf16[32,4096]{1,0:T(8,128)(2,1)S(1)}, bf16[32,4096]{1,0:T(8,128)(2,1)S(1)}, u32[]{:S(2)}, u32[]{:S(2)}) %collective-permute-start.11) | collective-permute-done | bytes 262176 | tf_op jit(solution)/shard_map/ppermute | solution.py:48
  57.3 1.4 collective-permute-start.13
  58.8 2.7 %collective-permute-start.14 = (bf16[16,4096]{1,0:T(8,128)(2,1)S(1)}, bf16[16,4096]{1,0:T(8,128)(2,1)S(1)}, u32[]{:S(2)}, u32[]{:S(2)}) collective-permute-start(bf16[16,4096]{1,0:T(8,128)(2,1)S(1)} %get-tuple-element.54), channel_id=1, source_target_pairs={{0,2},{1,3},{2,0},{3,1},{4,6},{5,7},{6,4},{7,5},{8,10},{9,11},{10,... | collective-permute-start | bytes 393224 | tf_op jit(solution)/shard_map/ppermute | solution.py:48
  63.7 4.0 %collective-permute-done.14 = bf16[16,4096]{1,0:T(8,128)(2,1)S(1)} collective-permute-done((bf16[16,4096]{1,0:T(8,128)(2,1)S(1)}, bf16[16,4096]{1,0:T(8,128)(2,1)S(1)}, u32[]{:S(2)}, u32[]{:S(2)}) %collective-permute-start.14) | collective-permute-done | bytes 131104 | tf_op jit(solution)/shard_map/ppermute | solution.py:48
  67.8 1.8 collective-permute-start.17
  70.5 6.8 %collective-permute-done.17 = bf16[64,4096]{1,0:T(8,128)(2,1)S(1)} collective-permute-done((bf16[64,4096]{1,0:T(8,128)(2,1)S(1)}, bf16[64,4096]{1,0:T(8,128)(2,1)S(1)}, u32[]{:S(2)}, u32[]{:S(2)}) %collective-permute-start.17) | collective-permute-done | bytes 524320 | tf_op jit(solution)/shard_map/ppermute | solution.py:40
  77.6 2.7 %collective-permute-done.18 = bf16[64,4096]{1,0:T(8,128)(2,1)S(1)} collective-permute-done((bf16[64,4096]{1,0:T(8,128)(2,1)S(1)}, bf16[64,4096]{1,0:T(8,128)(2,1)S(1)}, u32[]{:S(2)}, u32[]{:S(2)}) %collective-permute-start.18) | collective-permute-done | bytes 524320 | tf_op jit(solution)/shard_map/ppermute | solution.py:40
  80.3 2.2 %collective-permute-start.25 = (bf16[128,4096]{1,0:T(8,128)(2,1)S(1)}, bf16[128,4096]{1,0:T(8,128)(2,1)S(1)}, u32[]{:S(2)}, u32[]{:S(2)}) collective-permute-start(bf16[128,4096]{1,0:T(8,128)(2,1)S(1)} %constant_dynamic-update-slice_fusion.7.refs_1_), channel_id=1, source_target_pairs={{0,96},{4,28},{8,104},{12,4},{16,112},{20,12},{24,120},{28,20},{32... | collective-permute-start | bytes 3145736 | tf_op jit(solution)/shard_map/ppermute | solution.py:40
  82.5 5.1 %collective-permute-done.16 = bf16[64,4096]{1,0:T(8,128)(2,1)S(1)} collective-permute-done((bf16[64,4096]{1,0:T(8,128)(2,1)S(1)}, bf16[64,4096]{1,0:T(8,128)(2,1)S(1)}, u32[]{:S(2)}, u32[]{:S(2)}) %collective-permute-start.16) | collective-permute-done | bytes 524320 | tf_op jit(solution)/shard_map/ppermute | solution.py:40
  87.7 1.5 collective-permute-start.22
  89.1 6.0 %collective-permute-done.25.refs_3_ = bf16[128,4096]{1,0:T(8,128)(2,1)S(1)} collective-permute-done((bf16[128,4096]{1,0:T(8,128)(2,1)S(1)}, bf16[128,4096]{1,0:T(8,128)(2,1)S(1)}, u32[]{:S(2)}, u32[]{:S(2)}) %collective-permute-start.25) | collective-permute-done | bytes 1048608 | tf_op jit(solution)/shard_map/ppermute | solution.py:40
  95.2 3.3 %collective-permute-start.27 = (bf16[128,4096]{1,0:T(8,128)(2,1)S(1)}, bf16[128,4096]{1,0:T(8,128)(2,1)S(1)}, u32[]{:S(2)}, u32[]{:S(2)}) collective-permute-start(bf16[128,4096]{1,0:T(8,128)(2,1)S(1)} %collective-permute-done.25.refs_3_), channel_id=1, source_target_pairs={{0,96},{4,28},{8,104},{12,4},{16,112},{20,12},{24,120},{28,20},{32... | collective-permute-start | bytes 3145736 | tf_op jit(solution)/shard_map/ppermute | solution.py:40
  98.5 5.2 %collective-permute-done.22.refs_0_ = bf16[128,4096]{1,0:T(8,128)(2,1)S(1)} collective-permute-done((bf16[128,4096]{1,0:T(8,128)(2,1)S(1)}, bf16[128,4096]{1,0:T(8,128)(2,1)S(1)}, u32[]{:S(2)}, u32[]{:S(2)}) %collective-permute-start.22) | collective-permute-done | bytes 1048608 | tf_op jit(solution)/shard_map/ppermute | solution.py:40
  104.0 3.2 %collective-permute-start.24 = (bf16[128,4096]{1,0:T(8,128)(2,1)S(1)}, bf16[128,4096]{1,0:T(8,128)(2,1)S(1)}, u32[]{:S(2)}, u32[]{:S(2)}) collective-permute-start(bf16[128,4096]{1,0:T(8,128)(2,1)S(1)} %constant_dynamic-update-slice_fusion.2.refs_0_), channel_id=1, source_target_pairs={{0,96},{4,28},{8,104},{12,4},{16,112},{20,12},{24,120},{28,20},{32... | collective-permute-start | bytes 3145736 | tf_op jit(solution)/shard_map/ppermute | solution.py:40
  107.2 3.7 %collective-permute-done.27.refs_1_ = bf16[128,4096]{1,0:T(8,128)(2,1)S(1)} collective-permute-done((bf16[128,4096]{1,0:T(8,128)(2,1)S(1)}, bf16[128,4096]{1,0:T(8,128)(2,1)S(1)}, u32[]{:S(2)}, u32[]{:S(2)}) %collective-permute-start.27) | collective-permute-done | bytes 1048608 | tf_op jit(solution)/shard_map/ppermute | solution.py:40
  110.9 8.9 %collective-permute-done.26.refs_0_ = bf16[128,4096]{1,0:T(8,128)(2,1)S(1)} collective-permute-done((bf16[128,4096]{1,0:T(8,128)(2,1)S(1)}, bf16[128,4096]{1,0:T(8,128)(2,1)S(1)}, u32[]{:S(2)}, u32[]{:S(2)}) %collective-permute-start.26) | collective-permute-done | bytes 1048608 | tf_op jit(solution)/shard_map/ppermute | solution.py:40
  119.8 2.0 copy-done.4
  121.8 10.5 %expert_rows.5 = (bf16[128,4096]{1,0:T(8,128)(2,1)}, bf16[128,4096]{1,0:T(8,128)(2,1)}) custom-call(bf16[128,4096]{1,0:T(8,128)(2,1)S(1)} %collective-permute-done.26.refs_0_, bf16[128,4096]{1,0:T(8,128)(2,1)S(1)} %collective-permute-done.27.refs_1_, bf16[448,4096]{1,0:T(8,128)(2,1)S(1)} %bitcast.29, bf16[448,4096]{1,0:T(8,128)(2,1)S(1)} %bitcast.34, ...), custom_call_target="tpu_custom_call" | custom-call | flops 5637144576 | bytes 22020096 | tf_op jit(solution)/shard_map/expert_rows/pallas_call | solution.py:261
  132.4 2.0 collective-permute-start.33
  138.8 17.2 %expert_rows.4 = (bf16[128,4096]{1,0:T(8,128)(2,1)S(1)}, bf16[128,4096]{1,0:T(8,128)(2,1)S(1)}, bf16[128,4096]{1,0:T(8,128)(2,1)}, bf16[128,4096]{1,0:T(8,128)(2,1)S(1)}) custom-call(bf16[128,4096]{1,0:T(8,128)(2,1)S(1)} %collective-permute-done.22.refs_0_, bf16[128,4096]{1,0:T(8,128)(2,1)S(1)} %copy-done.11, bf16[128,4096]{1,0:T(8,128)(2,1)S(1)} %copy-done.13, ...), custom_call_target="tpu_custom_call" | custom-call | flops 11274289152 | bytes 22020096 | tf_op jit(solution)/shard_map/expert_rows/pallas_call | solution.py:261
  156.2 3.2 %collective-permute-start.32 = (bf16[128,4096]{1,0:T(8,128)(2,1)S(1)}, bf16[128,4096]{1,0:T(8,128)(2,1)S(1)}, u32[]{:S(2)}, u32[]{:S(2)}) collective-permute-start(bf16[128,4096]{1,0:T(8,128)(2,1)S(1)} %get-tuple-element.38), channel_id=1, source_target_pairs={{0,96},{4,28},{8,104},{12,4},{16,112},{20,12},{24,120},{28,20},{32... | collective-permute-start | bytes 3145736 | tf_op jit(solution)/shard_map/ppermute | solution.py:40
  160.0 2.3 %collective-permute-start.34 = (bf16[128,4096]{1,0:T(8,128)(2,1)S(1)}, bf16[128,4096]{1,0:T(8,128)(2,1)S(1)}, u32[]{:S(2)}, u32[]{:S(2)}) collective-permute-start(bf16[128,4096]{1,0:T(8,128)(2,1)S(1)} %add_convert_fusion.1), channel_id=1, source_target_pairs={{0,32},{4,12},{8,40},{12,20},{16,48},{20,28},{24,56},{28,4},{32,64... | collective-permute-start | bytes 3145736 | tf_op jit(solution)/shard_map/ppermute | solution.py:40
  162.3 2.0 copy-done.5
  164.4 9.8 %expert_rows.3 = (bf16[128,4096]{1,0:T(8,128)(2,1)S(1)}, bf16[128,4096]{1,0:T(8,128)(2,1)S(1)}) custom-call(bf16[128,4096]{1,0:T(8,128)(2,1)S(1)} %constant_dynamic-update-slice_fusion.2.refs_0_, bf16[128,4096]{1,0:T(8,128)(2,1)S(1)} %constant_dynamic-update-slice_fusion.7.refs_1_, bf16[448,4096]{1,0:T(8,128)(2,1)S(1)} %bitcast.31, ...), custom_call_target="tpu_custom_call" | custom-call | flops 5637144576 | bytes 22020096 | tf_op jit(solution)/shard_map/expert_rows/pallas_call | solution.py:261
  174.2 8.7 %collective-permute-done.29 = bf16[128,4096]{1,0:T(8,128)(2,1)S(1)} collective-permute-done((bf16[128,4096]{1,0:T(8,128)(2,1)S(1)}, bf16[128,4096]{1,0:T(8,128)(2,1)S(1)}, u32[]{:S(2)}, u32[]{:S(2)}) %collective-permute-start.29) | collective-permute-done | bytes 1048608 | tf_op jit(solution)/shard_map/ppermute | solution.py:40
  183.4 1.6 collective-permute-start.31
  188.6 4.1 %collective-permute-done.31 = bf16[64,4096]{1,0:T(8,128)(2,1)S(1)} collective-permute-done((bf16[64,4096]{1,0:T(8,128)(2,1)S(1)}, bf16[64,4096]{1,0:T(8,128)(2,1)S(1)}, u32[]{:S(2)}, u32[]{:S(2)}) %collective-permute-start.31) | collective-permute-done | bytes 524320 | tf_op jit(solution)/shard_map/ppermute | solution.py:40
  192.7 10.2 %collective-permute-done.35 = bf16[64,4096]{1,0:T(8,128)(2,1)S(1)} collective-permute-done((bf16[64,4096]{1,0:T(8,128)(2,1)}, bf16[64,4096]{1,0:T(8,128)(2,1)S(1)}, u32[]{:S(2)}, u32[]{:S(2)}) %collective-permute-start.35) | collective-permute-done | bytes 524320 | tf_op jit(solution)/shard_map/ppermute | solution.py:40
  203.2 2.2 %collective-permute-start.37 = (bf16[16,4096]{1,0:T(8,128)(2,1)S(1)}, bf16[16,4096]{1,0:T(8,128)(2,1)S(1)}, u32[]{:S(2)}, u32[]{:S(2)}) collective-permute-start(bf16[16,4096]{1,0:T(8,128)(2,1)S(1)} %get-tuple-element.50), channel_id=1, source_target_pairs={{0,3},{1,0},{2,1},{3,2},{4,7},{5,4},{6,5},{7,6},{8,11},{9,8},{10,9... | collective-permute-start | bytes 393224 | tf_op jit(solution)/shard_map/ppermute | solution.py:48
  205.4 6.5 %collective-permute-start.38 = (bf16[16,4096]{1,0:T(8,128)(2,1)S(1)}, bf16[16,4096]{1,0:T(8,128)(2,1)S(1)}, u32[]{:S(2)}, u32[]{:S(2)}) collective-permute-start(bf16[16,4096]{1,0:T(8,128)(2,1)S(1)} %get-tuple-element.49), channel_id=1, source_target_pairs={{0,2},{1,3},{2,0},{3,1},{4,6},{5,7},{6,4},{7,5},{8,10},{9,11},{10,... | collective-permute-start | bytes 393224 | tf_op jit(solution)/shard_map/ppermute | solution.py:48
  211.9 1.3 collective-permute-start.39
  213.3 1.5 collective-permute-done.38
  214.8 3.2 %collective-permute-done.39 = bf16[16,4096]{1,0:T(8,128)(2,1)S(1)} collective-permute-done((bf16[16,4096]{1,0:T(8,128)(2,1)S(1)}, bf16[16,4096]{1,0:T(8,128)(2,1)S(1)}, u32[]{:S(2)}, u32[]{:S(2)}) %collective-permute-start.39) | collective-permute-done | bytes 131104 | tf_op jit(solution)/shard_map/ppermute | solution.py:48
  (156 shorter events, 25.2 us)
Async XLA Ops:
  0.0 188.2 %copy-start = (f32[4096,4]{0,1:T(4,128)S(1)}, f32[4096,4]{0,1:T(4,128)}, u32[]{:S(2)}) copy-start(f32[4096,4]{0,1:T(4,128)} %param.27) | copy-start | bytes 196612
  1.7 9.4 %collective-permute-start = (bf16[128,512]{1,0:T(8,128)(2,1)S(1)}, bf16[128,512]{1,0:T(8,128)(2,1)S(1)}, u32[]{:S(2)}, u32[]{:S(2)}) collective-permute-start(bf16[128,512]{1,0:T(8,128)(2,1)S(1)} %constant_dynamic-update-slice_fusion), channel_id=1, source_target_pairs={{0,8},{4,36},{8,16},{12,44},{16,24},{20,52},{24,0},{28,60},{32,40}... | collective-permute-start | bytes 393224 | tf_op jit(solution)/shard_map/ppermute | solution.py:40
  3.3 7.8 %collective-permute-start.1 = (bf16[128,512]{1,0:T(8,128)(2,1)S(1)}, bf16[128,512]{1,0:T(8,128)(2,1)S(1)}, u32[]{:S(2)}, u32[]{:S(2)}) collective-permute-start(bf16[128,512]{1,0:T(8,128)(2,1)S(1)} %constant_dynamic-update-slice_fusion), channel_id=1, source_target_pairs={{0,24},{4,100},{8,0},{12,108},{16,8},{20,116},{24,16},{28,124},{32... | collective-permute-start | bytes 393224 | tf_op jit(solution)/shard_map/ppermute | solution.py:40
  5.0 6.5 %collective-permute-start.2 = (bf16[128,512]{1,0:T(8,128)(2,1)S(1)}, bf16[128,512]{1,0:T(8,128)(2,1)S(1)}, u32[]{:S(2)}, u32[]{:S(2)}) collective-permute-start(bf16[128,512]{1,0:T(8,128)(2,1)S(1)} %constant_dynamic-update-slice_fusion), channel_id=1, source_target_pairs={{0,16},{4,68},{8,24},{12,76},{16,0},{20,84},{24,8},{28,92},{32,48}... | collective-permute-start | bytes 393224 | tf_op jit(solution)/shard_map/ppermute | solution.py:40
  11.5 11.4 %collective-permute-start.5 = (bf16[512,512]{1,0:T(8,128)(2,1)S(1)}, bf16[512,512]{1,0:T(8,128)(2,1)S(1)}, u32[]{:S(2)}, u32[]{:S(2)}) collective-permute-start(bf16[512,512]{1,0:T(8,128)(2,1)S(1)} %pad_maximum_fusion.refs_3_), channel_id=1, source_target_pairs={{0,32},{4,12},{8,40},{12,20},{16,48},{20,28},{24,56},{28,4},{32,64... | collective-permute-start | bytes 1572872 | tf_op jit(solution)/shard_map/ppermute | solution.py:40
  13.6 14.6 %collective-permute-start.7 = (bf16[512,512]{1,0:T(8,128)(2,1)S(1)}, bf16[512,512]{1,0:T(8,128)(2,1)S(1)}, u32[]{:S(2)}, u32[]{:S(2)}) collective-permute-start(bf16[512,512]{1,0:T(8,128)(2,1)S(1)} %pad_maximum_fusion.refs_3_), channel_id=1, source_target_pairs={{0,96},{4,28},{8,104},{12,4},{16,112},{20,12},{24,120},{28,20},{32... | collective-permute-start | bytes 1572872 | tf_op jit(solution)/shard_map/ppermute | solution.py:40
  16.7 13.2 %collective-permute-start.3 = (bf16[512,512]{1,0:T(8,128)(2,1)S(1)}, bf16[512,512]{1,0:T(8,128)(2,1)S(1)}, u32[]{:S(2)}, u32[]{:S(2)}) collective-permute-start(bf16[512,512]{1,0:T(8,128)(2,1)S(1)} %pad_maximum_fusion.refs_3_), channel_id=1, source_target_pairs={{0,64},{4,20},{8,72},{12,28},{16,80},{20,4},{24,88},{28,12},{32,96... | collective-permute-start | bytes 1572872 | tf_op jit(solution)/shard_map/ppermute | solution.py:40
  18.8 11.2 %collective-permute-start.9 = (bf16[512,512]{1,0:T(8,128)(2,1)S(1)}, bf16[512,512]{1,0:T(8,128)(2,1)S(1)}, u32[]{:S(2)}, u32[]{:S(2)}) collective-permute-start(bf16[512,512]{1,0:T(8,128)(2,1)S(1)} %pad_maximum_fusion.refs_3_), channel_id=1, source_target_pairs={{0,4},{4,0},{8,12},{12,8},{16,20},{20,16},{24,28},{28,24},{32,36},... | collective-permute-start | bytes 1572872 | tf_op jit(solution)/shard_map/ppermute | solution.py:44
  22.9 9.8 %collective-permute-start.6 = (bf16[512,512]{1,0:T(8,128)(2,1)S(1)}, bf16[512,512]{1,0:T(8,128)(2,1)S(1)}, u32[]{:S(2)}, u32[]{:S(2)}) collective-permute-start(bf16[512,512]{1,0:T(8,128)(2,1)S(1)} %collective-permute-done.5.refs_3_), channel_id=1, source_target_pairs={{0,4},{4,0},{8,12},{12,8},{16,20},{20,16},{24,28},{28,24},{32,36},... | collective-permute-start | bytes 1572872 | tf_op jit(solution)/shard_map/ppermute | solution.py:44
  28.1 4.6 %collective-permute-start.8 = (bf16[512,512]{1,0:T(8,128)(2,1)S(1)}, bf16[512,512]{1,0:T(8,128)(2,1)S(1)}, u32[]{:S(2)}, u32[]{:S(2)}) collective-permute-start(bf16[512,512]{1,0:T(8,128)(2,1)S(1)} %collective-permute-done.7.refs_5_), channel_id=1, source_target_pairs={{0,4},{4,0},{8,12},{12,8},{16,20},{20,16},{24,28},{28,24},{32,36},... | collective-permute-start | bytes 1572872 | tf_op jit(solution)/shard_map/ppermute | solution.py:44
  29.9 6.5 %collective-permute-start.4 = (bf16[512,512]{1,0:T(8,128)(2,1)S(1)}, bf16[512,512]{1,0:T(8,128)(2,1)S(1)}, u32[]{:S(2)}, u32[]{:S(2)}) collective-permute-start(bf16[512,512]{1,0:T(8,128)(2,1)S(1)} %collective-permute-done.3.refs_3_), channel_id=1, source_target_pairs={{0,4},{4,0},{8,12},{12,8},{16,20},{20,16},{24,28},{28,24},{32,36},... | collective-permute-start | bytes 1572872 | tf_op jit(solution)/shard_map/ppermute | solution.py:44
  36.4 10.4 %copy-start.18 = (s32[32,2]{0,1:T(2,128)S(1)}, s32[32,2]{0,1:T(2,128)}, u32[]{:S(2)}) copy-start(s32[32,2]{0,1:T(2,128)} %param.28) | copy-start | bytes 772
  36.5 20.2 %copy-start.16 = (bf16[32,4096]{1,0:T(8,128)(2,1)S(1)}, bf16[32,4096]{1,0:T(8,128)(2,1)}, u32[]{:S(2)}) copy-start(bf16[32,4096]{1,0:T(8,128)(2,1)} %param.23) | copy-start | bytes 786436
  36.5 20.4 %copy-start.17 = (f32[4096]{0:T(1024)S(1)}, f32[4096]{0:T(1024)}, u32[]{:S(2)}) copy-start(f32[4096]{0:T(1024)} %param.26) | copy-start | bytes 49156
  40.3 10.8 %collective-permute-start.10 = (bf16[32,4096]{1,0:T(8,128)(2,1)S(1)}, bf16[32,4096]{1,0:T(8,128)(2,1)S(1)}, u32[]{:S(2)}, u32[]{:S(2)}) collective-permute-start(bf16[32,4096]{1,0:T(8,128)(2,1)S(1)} %get-tuple-element.30), channel_id=1, source_target_pairs={{0,2},{1,3},{2,0},{3,1},{4,6},{5,7},{6,4},{7,5},{8,10},{9,11},{10,... | collective-permute-start | bytes 786440 | tf_op jit(solution)/shard_map/ppermute | solution.py:48
  43.6 12.6 %collective-permute-start.11 = (bf16[32,4096]{1,0:T(8,128)(2,1)S(1)}, bf16[32,4096]{1,0:T(8,128)(2,1)S(1)}, u32[]{:S(2)}, u32[]{:S(2)}) collective-permute-start(bf16[32,4096]{1,0:T(8,128)(2,1)S(1)} %get-tuple-element.31), channel_id=1, source_target_pairs={{0,1},{1,2},{2,3},{3,0},{4,5},{5,6},{6,7},{7,4},{8,9},{9,10},{10,1... | collective-permute-start | bytes 786440 | tf_op jit(solution)/shard_map/ppermute | solution.py:48
  44.3 12.3 %collective-permute-start.12 = (bf16[32,4096]{1,0:T(8,128)(2,1)S(1)}, bf16[32,4096]{1,0:T(8,128)(2,1)S(1)}, u32[]{:S(2)}, u32[]{:S(2)}) collective-permute-start(bf16[32,4096]{1,0:T(8,128)(2,1)S(1)} %get-tuple-element.32), channel_id=1, source_target_pairs={{0,3},{1,0},{2,1},{3,2},{4,7},{5,4},{6,5},{7,6},{8,11},{9,8},{10,9... | collective-permute-start | bytes 786440 | tf_op jit(solution)/shard_map/ppermute | solution.py:48
  47.2 14.8 %copy-start.1 = (bf16[1,4096,448]{1,2,0:T(8,128)(2,1)S(1)}, bf16[1,4096,448]{1,2,0:T(8,128)(2,1)}, u32[]{:S(2)}) copy-start(bf16[1,4096,448]{1,2,0:T(8,128)(2,1)} %param.29) | copy-start | bytes 11010052
  57.3 6.4 %collective-permute-start.13 = (bf16[16,4096]{1,0:T(8,128)(2,1)S(1)}, bf16[16,4096]{1,0:T(8,128)(2,1)S(1)}, u32[]{:S(2)}, u32[]{:S(2)}) collective-permute-start(bf16[16,4096]{1,0:T(8,128)(2,1)S(1)} %get-tuple-element.55), channel_id=1, source_target_pairs={{0,1},{1,2},{2,3},{3,0},{4,5},{5,6},{6,7},{7,4},{8,9},{9,10},{10,1... | collective-permute-start | bytes 393224 | tf_op jit(solution)/shard_map/ppermute | solution.py:48
  58.8 8.9 %collective-permute-start.14 = (bf16[16,4096]{1,0:T(8,128)(2,1)S(1)}, bf16[16,4096]{1,0:T(8,128)(2,1)S(1)}, u32[]{:S(2)}, u32[]{:S(2)}) collective-permute-start(bf16[16,4096]{1,0:T(8,128)(2,1)S(1)} %get-tuple-element.54), channel_id=1, source_target_pairs={{0,2},{1,3},{2,0},{3,1},{4,6},{5,7},{6,4},{7,5},{8,10},{9,11},{10,... | collective-permute-start | bytes 393224 | tf_op jit(solution)/shard_map/ppermute | solution.py:48
  61.5 6.2 %collective-permute-start.15 = (bf16[16,4096]{1,0:T(8,128)(2,1)S(1)}, bf16[16,4096]{1,0:T(8,128)(2,1)S(1)}, u32[]{:S(2)}, u32[]{:S(2)}) collective-permute-start(bf16[16,4096]{1,0:T(8,128)(2,1)S(1)} %get-tuple-element.53), channel_id=1, source_target_pairs={{0,3},{1,0},{2,1},{3,2},{4,7},{5,4},{6,5},{7,6},{8,11},{9,8},{10,9... | collective-permute-start | bytes 393224 | tf_op jit(solution)/shard_map/ppermute | solution.py:48
  62.1 41.9 %collective-permute-start.19 = (bf16[448,4096]{1,0:T(8,128)(2,1)S(1)}, bf16[448,4096]{1,0:T(8,128)(2,1)S(1)}, u32[]{:S(2)}, u32[]{:S(2)}) collective-permute-start(bf16[448,4096]{1,0:T(8,128)(2,1)S(1)} %bitcast.28), channel_id=1, source_target_pairs={{0,4},{4,0},{8,12},{12,8},{16,20},{20,16},{24,28},{28,24},{32,36},... | collective-permute-start | bytes 11010056 | tf_op jit(solution)/shard_map/ppermute | solution.py:44
  62.1 41.9 %collective-permute-start.20 = (bf16[448,4096]{1,0:T(8,128)(2,1)}, bf16[448,4096]{1,0:T(8,128)(2,1)S(1)}, u32[]{:S(2)}, u32[]{:S(2)}) collective-permute-start(bf16[448,4096]{1,0:T(8,128)(2,1)} %bitcast.32), channel_id=1, source_target_pairs={{0,4},{4,0},{8,12},{12,8},{16,20},{20,16},{24,28},{28,24},{32,36},... | collective-permute-start | bytes 11010056 | tf_op jit(solution)/shard_map/ppermute | solution.py:44
  63.7 43.5 %collective-permute-start.21 = (bf16[448,4096]{1,0:T(8,128)(2,1)}, bf16[448,4096]{1,0:T(8,128)(2,1)S(1)}, u32[]{:S(2)}, u32[]{:S(2)}) collective-permute-start(bf16[448,4096]{1,0:T(8,128)(2,1)} %bitcast.36), channel_id=1, source_target_pairs={{0,4},{4,0},{8,12},{12,8},{16,20},{20,16},{24,28},{28,24},{32,36},... | collective-permute-start | bytes 11010056 | tf_op jit(solution)/shard_map/ppermute | solution.py:44
  67.8 52.0 %copy-start.2 = (bf16[1,4096,448]{1,2,0:T(8,128)(2,1)S(1)}, bf16[1,4096,448]{1,2,0:T(8,128)(2,1)}, u32[]{:S(2)}) copy-start(bf16[1,4096,448]{1,2,0:T(8,128)(2,1)} %param.30) | copy-start | bytes 11010052
  67.8 9.5 %collective-permute-start.17 = (bf16[64,4096]{1,0:T(8,128)(2,1)S(1)}, bf16[64,4096]{1,0:T(8,128)(2,1)S(1)}, u32[]{:S(2)}, u32[]{:S(2)}) collective-permute-start(bf16[64,4096]{1,0:T(8,128)(2,1)S(1)} %pad_maximum_fusion.1), channel_id=1, source_target_pairs={{0,24},{4,100},{8,0},{12,108},{16,8},{20,116},{24,16},{28,124},{32... | collective-permute-start | bytes 1572872 | tf_op jit(solution)/shard_map/ppermute | solution.py:40
  69.6 10.7 %collective-permute-start.18 = (bf16[64,4096]{1,0:T(8,128)(2,1)S(1)}, bf16[64,4096]{1,0:T(8,128)(2,1)S(1)}, u32[]{:S(2)}, u32[]{:S(2)}) collective-permute-start(bf16[64,4096]{1,0:T(8,128)(2,1)S(1)} %pad_maximum_fusion.1), channel_id=1, source_target_pairs={{0,16},{4,68},{8,24},{12,76},{16,0},{20,84},{24,8},{28,92},{32,48}... | collective-permute-start | bytes 1572872 | tf_op jit(solution)/shard_map/ppermute | solution.py:40
  77.2 10.4 %collective-permute-start.16 = (bf16[64,4096]{1,0:T(8,128)(2,1)S(1)}, bf16[64,4096]{1,0:T(8,128)(2,1)S(1)}, u32[]{:S(2)}, u32[]{:S(2)}) collective-permute-start(bf16[64,4096]{1,0:T(8,128)(2,1)S(1)} %pad_maximum_fusion.1), channel_id=1, source_target_pairs={{0,8},{4,36},{8,16},{12,44},{16,24},{20,52},{24,0},{28,60},{32,40}... | collective-permute-start | bytes 1572872 | tf_op jit(solution)/shard_map/ppermute | solution.py:40
  80.3 14.9 %collective-permute-start.25 = (bf16[128,4096]{1,0:T(8,128)(2,1)S(1)}, bf16[128,4096]{1,0:T(8,128)(2,1)S(1)}, u32[]{:S(2)}, u32[]{:S(2)}) collective-permute-start(bf16[128,4096]{1,0:T(8,128)(2,1)S(1)} %constant_dynamic-update-slice_fusion.7.refs_1_), channel_id=1, source_target_pairs={{0,96},{4,28},{8,104},{12,4},{16,112},{20,12},{24,120},{28,20},{32... | collective-permute-start | bytes 3145736 | tf_op jit(solution)/shard_map/ppermute | solution.py:40
  87.7 16.1 %collective-permute-start.22 = (bf16[128,4096]{1,0:T(8,128)(2,1)S(1)}, bf16[128,4096]{1,0:T(8,128)(2,1)S(1)}, u32[]{:S(2)}, u32[]{:S(2)}) collective-permute-start(bf16[128,4096]{1,0:T(8,128)(2,1)S(1)} %constant_dynamic-update-slice_fusion.2.refs_0_), channel_id=1, source_target_pairs={{0,32},{4,12},{8,40},{12,20},{16,48},{20,28},{24,56},{28,4},{32,64... | collective-permute-start | bytes 3145736 | tf_op jit(solution)/shard_map/ppermute | solution.py:40
  95.2 15.7 %collective-permute-start.27 = (bf16[128,4096]{1,0:T(8,128)(2,1)S(1)}, bf16[128,4096]{1,0:T(8,128)(2,1)S(1)}, u32[]{:S(2)}, u32[]{:S(2)}) collective-permute-start(bf16[128,4096]{1,0:T(8,128)(2,1)S(1)} %collective-permute-done.25.refs_3_), channel_id=1, source_target_pairs={{0,96},{4,28},{8,104},{12,4},{16,112},{20,12},{24,120},{28,20},{32... | collective-permute-start | bytes 3145736 | tf_op jit(solution)/shard_map/ppermute | solution.py:40
  103.7 16.0 %collective-permute-start.26 = (bf16[128,4096]{1,0:T(8,128)(2,1)S(1)}, bf16[128,4096]{1,0:T(8,128)(2,1)S(1)}, u32[]{:S(2)}, u32[]{:S(2)}) collective-permute-start(bf16[128,4096]{1,0:T(8,128)(2,1)S(1)} %collective-permute-done.22.refs_0_), channel_id=1, source_target_pairs={{0,32},{4,12},{8,40},{12,20},{16,48},{20,28},{24,56},{28,4},{32,64... | collective-permute-start | bytes 3145736 | tf_op jit(solution)/shard_map/ppermute | solution.py:40
  104.0 28.4 %copy-start.6 = (bf16[448,4096]{1,0:T(8,128)(2,1)}, bf16[448,4096]{1,0:T(8,128)(2,1)S(1)}, u32[]{:S(2)}) copy-start(bf16[448,4096]{1,0:T(8,128)(2,1)S(1)} %collective-permute-done.19.refs_5_.refs_7_) | copy-start | bytes 11010052
  104.0 30.5 %collective-permute-start.23 = (bf16[128,4096]{1,0:T(8,128)(2,1)S(1)}, bf16[128,4096]{1,0:T(8,128)(2,1)S(1)}, u32[]{:S(2)}, u32[]{:S(2)}) collective-permute-start(bf16[128,4096]{1,0:T(8,128)(2,1)S(1)} %constant_dynamic-update-slice_fusion.7.refs_1_), channel_id=1, source_target_pairs={{0,32},{4,12},{8,40},{12,20},{16,48},{20,28},{24,56},{28,4},{32,64... | collective-permute-start | bytes 3145736 | tf_op jit(solution)/shard_map/ppermute | solution.py:40
  104.0 31.4 %collective-permute-start.24 = (bf16[128,4096]{1,0:T(8,128)(2,1)S(1)}, bf16[128,4096]{1,0:T(8,128)(2,1)S(1)}, u32[]{:S(2)}, u32[]{:S(2)}) collective-permute-start(bf16[128,4096]{1,0:T(8,128)(2,1)S(1)} %constant_dynamic-update-slice_fusion.2.refs_0_), channel_id=1, source_target_pairs={{0,96},{4,28},{8,104},{12,4},{16,112},{20,12},{24,120},{28,20},{32... | collective-permute-start | bytes 3145736 | tf_op jit(solution)/shard_map/ppermute | solution.py:40
  132.3 27.1 %collective-permute-start.28 = (bf16[128,4096]{1,0:T(8,128)(2,1)}, bf16[128,4096]{1,0:T(8,128)(2,1)S(1)}, u32[]{:S(2)}, u32[]{:S(2)}) collective-permute-start(bf16[128,4096]{1,0:T(8,128)(2,1)} %get-tuple-element.35), channel_id=1, source_target_pairs={{0,96},{4,28},{8,104},{12,4},{16,112},{20,12},{24,120},{28,20},{32... | collective-permute-start | bytes 3145736 | tf_op jit(solution)/shard_map/ppermute | solution.py:40
  132.4 27.4 %collective-permute-start.33 = (bf16[128,4096]{1,0:T(8,128)(2,1)}, bf16[128,4096]{1,0:T(8,128)(2,1)S(1)}, u32[]{:S(2)}, u32[]{:S(2)}) collective-permute-start(bf16[128,4096]{1,0:T(8,128)(2,1)} %get-tuple-element.40), channel_id=1, source_target_pairs={{0,32},{4,12},{8,40},{12,20},{16,48},{20,28},{24,56},{28,4},{32,64... | collective-permute-start | bytes 3145736 | tf_op jit(solution)/shard_map/ppermute | solution.py:40
  138.8 23.5 %copy-start.7 = (bf16[448,4096]{1,0:T(8,128)(2,1)S(1)}, bf16[448,4096]{1,0:T(8,128)(2,1)}, u32[]{:S(2)}) copy-start(bf16[448,4096]{1,0:T(8,128)(2,1)} %copy-done.6) | copy-start | bytes 11010052
  156.1 18.1 %collective-permute-start.30 = (bf16[128,4096]{1,0:T(8,128)(2,1)}, bf16[128,4096]{1,0:T(8,128)(2,1)S(1)}, u32[]{:S(2)}, u32[]{:S(2)}) collective-permute-start(bf16[128,4096]{1,0:T(8,128)(2,1)} %get-tuple-element.36), channel_id=1, source_target_pairs={{0,32},{4,12},{8,40},{12,20},{16,48},{20,28},{24,56},{28,4},{32,64... | collective-permute-start | bytes 3145736 | tf_op jit(solution)/shard_map/ppermute | solution.py:40
  156.2 28.9 %collective-permute-start.32 = (bf16[128,4096]{1,0:T(8,128)(2,1)S(1)}, bf16[128,4096]{1,0:T(8,128)(2,1)S(1)}, u32[]{:S(2)}, u32[]{:S(2)}) collective-permute-start(bf16[128,4096]{1,0:T(8,128)(2,1)S(1)} %get-tuple-element.38), channel_id=1, source_target_pairs={{0,96},{4,28},{8,104},{12,4},{16,112},{20,12},{24,120},{28,20},{32... | collective-permute-start | bytes 3145736 | tf_op jit(solution)/shard_map/ppermute | solution.py:40
  159.6 23.3 %collective-permute-start.29 = (bf16[128,4096]{1,0:T(8,128)(2,1)S(1)}, bf16[128,4096]{1,0:T(8,128)(2,1)S(1)}, u32[]{:S(2)}, u32[]{:S(2)}) collective-permute-start(bf16[128,4096]{1,0:T(8,128)(2,1)S(1)} %add_convert_fusion.3), channel_id=1, source_target_pairs={{0,96},{4,28},{8,104},{12,4},{16,112},{20,12},{24,120},{28,20},{32... | collective-permute-start | bytes 3145736 | tf_op jit(solution)/shard_map/ppermute | solution.py:40
  160.0 25.0 %collective-permute-start.34 = (bf16[128,4096]{1,0:T(8,128)(2,1)S(1)}, bf16[128,4096]{1,0:T(8,128)(2,1)S(1)}, u32[]{:S(2)}, u32[]{:S(2)}) collective-permute-start(bf16[128,4096]{1,0:T(8,128)(2,1)S(1)} %add_convert_fusion.1), channel_id=1, source_target_pairs={{0,32},{4,12},{8,40},{12,20},{16,48},{20,28},{24,56},{28,4},{32,64... | collective-permute-start | bytes 3145736 | tf_op jit(solution)/shard_map/ppermute | solution.py:40
  183.4 9.2 %collective-permute-start.31 = (bf16[64,4096]{1,0:T(8,128)(2,1)S(1)}, bf16[64,4096]{1,0:T(8,128)(2,1)S(1)}, u32[]{:S(2)}, u32[]{:S(2)}) collective-permute-start(bf16[64,4096]{1,0:T(8,128)(2,1)S(1)} %slice.53), channel_id=1, source_target_pairs={{0,24},{4,100},{8,0},{12,108},{16,8},{20,116},{24,16},{28,124},{32... | collective-permute-start | bytes 1572872 | tf_op jit(solution)/shard_map/ppermute | solution.py:40
  186.6 16.2 %collective-permute-start.35 = (bf16[64,4096]{1,0:T(8,128)(2,1)}, bf16[64,4096]{1,0:T(8,128)(2,1)S(1)}, u32[]{:S(2)}, u32[]{:S(2)}) collective-permute-start(bf16[64,4096]{1,0:T(8,128)(2,1)} %get-tuple-element.45), channel_id=1, source_target_pairs={{0,8},{4,36},{8,16},{12,44},{16,24},{20,52},{24,0},{28,60},{32,40}... | collective-permute-start | bytes 1572872 | tf_op jit(solution)/shard_map/ppermute | solution.py:40
  187.1 15.8 %collective-permute-start.36 = (bf16[64,4096]{1,0:T(8,128)(2,1)}, bf16[64,4096]{1,0:T(8,128)(2,1)S(1)}, u32[]{:S(2)}, u32[]{:S(2)}) collective-permute-start(bf16[64,4096]{1,0:T(8,128)(2,1)} %get-tuple-element.46), channel_id=1, source_target_pairs={{0,16},{4,68},{8,24},{12,76},{16,0},{20,84},{24,8},{28,92},{32,48}... | collective-permute-start | bytes 1572872 | tf_op jit(solution)/shard_map/ppermute | solution.py:40
  203.2 10.1 %collective-permute-start.37 = (bf16[16,4096]{1,0:T(8,128)(2,1)S(1)}, bf16[16,4096]{1,0:T(8,128)(2,1)S(1)}, u32[]{:S(2)}, u32[]{:S(2)}) collective-permute-start(bf16[16,4096]{1,0:T(8,128)(2,1)S(1)} %get-tuple-element.50), channel_id=1, source_target_pairs={{0,3},{1,0},{2,1},{3,2},{4,7},{5,4},{6,5},{7,6},{8,11},{9,8},{10,9... | collective-permute-start | bytes 393224 | tf_op jit(solution)/shard_map/ppermute | solution.py:48
  205.4 9.4 %collective-permute-start.38 = (bf16[16,4096]{1,0:T(8,128)(2,1)S(1)}, bf16[16,4096]{1,0:T(8,128)(2,1)S(1)}, u32[]{:S(2)}, u32[]{:S(2)}) collective-permute-start(bf16[16,4096]{1,0:T(8,128)(2,1)S(1)} %get-tuple-element.49), channel_id=1, source_target_pairs={{0,2},{1,3},{2,0},{3,1},{4,6},{5,7},{6,4},{7,5},{8,10},{9,11},{10,... | collective-permute-start | bytes 393224 | tf_op jit(solution)/shard_map/ppermute | solution.py:48
  211.9 6.2 %collective-permute-start.39 = (bf16[16,4096]{1,0:T(8,128)(2,1)S(1)}, bf16[16,4096]{1,0:T(8,128)(2,1)S(1)}, u32[]{:S(2)}, u32[]{:S(2)}) collective-permute-start(bf16[16,4096]{1,0:T(8,128)(2,1)S(1)} %get-tuple-element.48), channel_id=1, source_target_pairs={{0,1},{1,2},{2,3},{3,0},{4,5},{5,6},{6,7},{7,4},{8,9},{9,10},{10,1... | collective-permute-start | bytes 393224 | tf_op jit(solution)/shard_map/ppermute | solution.py:48
  (11 other events, 28.3 us)
where the time goes:
time: 219 us
  waiting for transfers between devices  91.9 us (42%)
  starting transfers between devices  57.5 us (26%)
  Pallas kernels  46.8 us (21%)
  local copies, waits for them, and re-layouts  14.4 us (7%)
  other arithmetic  6.33 us (3%)
    ppermute x24, waiting for transfers between devices, shift(): return lax.ppermute(a, 'ctx', RINGS[phase, step])  72.7 us
    pallas_call x3, Pallas kernels, expert_rows(): pl.pallas_call(kernel, out_shape=tuple((jax.ShapeDtypeStruct((size, width...  37.6 us
    ppermute x24, starting transfers between devices, shift(): return lax.ppermute(a, 'ctx', RINGS[phase, step])  35.7 us
    ppermute x9, starting transfers between devices, shift_exp(): return lax.ppermute(a, 'exp', [(i, (i + step) % 4) for i in range(4)])  21.2 us
    ppermute x9, waiting for transfers between devices, shift_exp(): return lax.ppermute(a, 'exp', [(i, (i + step) % 4) for i in range(4)])  19.2 us
    unnamed x43, local copies, waits for them, and re-layouts  10.4 us
    pallas_call x2, Pallas kernels, attend_part(): pl.pallas_call(kernel, out_shape=(shape, shape, shape), in_specs=[vmem_sp...  5.4 us
  transfers between devices with their start and end apart: 40, of which 21 were waited for; matrix products, arithmetic and copies ran while one was open for 4% of the time, Pallas kernels for 20%

commit v1 on v0

--- a/solution.py
+++ b/solution.py
@@ -257,7 +257,7 @@
             for copy in out_copies(n):
                 copy.wait()
 
-    anywhere = pl.BlockSpec(memory_space=pl.ANY)
+    anywhere = pl.BlockSpec(memory_space=pltpu.HBM)
     return pl.pallas_call(
         kernel,
         out_shape=tuple(jax.ShapeDtypeStruct((size, width), bf16) for size in sizes),
@@ -368,7 +368,8 @@
     f0, f1 = shift(l0, 2, 1), shift(r1, 2, -1)
 
     n0, n1 = expert_rows((n0, n1), own, other)
-    l0, l1, r0, r1 = expert_rows((l0, l1, r0, r1), own, other)
+    l0, r1 = expert_rows((l0, r1), own, other)
+    l1, r0 = expert_rows((l1, r0), own, other)
     f0, f1 = expert_rows((f0, f1), own, other)
 
     u1, v0 = shift(l1, 2, -1), shift(r0, 2, 1)

time: 219 us -> 216 us (0.986)
  waiting for transfers between devices: 91.9 us -> 98.4 us
  local copies, waits for them, and re-layouts: 14.4 us -> 7.96 us
  starting transfers between devices: 57.5 us -> 51.9 us
    ppermute x9, starting transfers between devices: 21.2 us -> 14.4 us  [shift_exp(): return lax.ppermute(a, 'exp', [(i, (i + step) % 4) for i in range(4)])]
    unnamed x43 -> x27, local copies, waits for them, and re-layouts: 10.4 us -> 3.98 us
    ppermute x24, waiting for transfers between devices: 72.7 us -> 76.3 us  [shift(): return lax.ppermute(a, 'ctx', RINGS[phase, step])]
    ppermute x9, waiting for transfers between devices: 19.2 us -> 22.1 us  [shift_exp(): return lax.ppermute(a, 'exp', [(i, (i + step) % 4) for i in range(4)])]
    pallas_call x3 -> x4, Pallas kernels: 37.6 us -> 39.2 us  [expert_rows(): pl.pallas_call(kernel, out_shape=tuple((jax.ShapeDtypeStruct((size, width...]
  transfers between devices with their start and end apart: 40 -> 40, of which waited for: 21 -> 22; matrix products, arithmetic and copies ran while one was open for 4% -> 4% of each run, Pallas kernels for 20% -> 21%
where the time goes in v1:
time: 216 us; the launch traced here: 215 us
  waiting for transfers between devices  98.4 us (46%)
  starting transfers between devices  51.9 us (24%)
  Pallas kernels  48.4 us (22%)
  local copies, waits for them, and re-layouts  7.96 us (4%)
  other arithmetic  6.33 us (3%)
    ppermute x24, waiting for transfers between devices, shift(): return lax.ppermute(a, 'ctx', RINGS[phase, step])  76.3 us
    pallas_call x4, Pallas kernels, expert_rows(): pl.pallas_call(kernel, out_shape=tuple((jax.ShapeDtypeStruct((size, width...  39.2 us
    ppermute x24, starting transfers between devices, shift(): return lax.ppermute(a, 'ctx', RINGS[phase, step])  37 us
    ppermute x9, waiting for transfers between devices, shift_exp(): return lax.ppermute(a, 'exp', [(i, (i + step) % 4) for i in range(4)])  22.1 us
    ppermute x9, starting transfers between devices, shift_exp(): return lax.ppermute(a, 'exp', [(i, (i + step) % 4) for i in range(4)])  14.4 us
    pallas_call x2, Pallas kernels, attend_part(): pl.pallas_call(kernel, out_shape=(shape, shape, shape), in_specs=[vmem_sp...  5.3 us
  transfers between devices with their start and end apart: 40, of which 22 were waited for; matrix products, arithmetic and copies ran while one was open for 4% of the time, Pallas kernels for 21%

profile of v1, /device:TPU:0, one launch (start us, length us, event | category | flops | bytes accessed | tf_op | source)
XLA Modules:
  0.0 215.2 jit_solution(1109645679920808894)
XLA Ops:
  1.7 1.6 collective-permute-start
  3.3 1.6 collective-permute-start.1
  5.0 1.9 collective-permute-start.2
  11.5 2.1 collective-permute-start.5
  13.6 2.2 %collective-permute-start.7 = (bf16[512,512]{1,0:T(8,128)(2,1)S(1)}, bf16[512,512]{1,0:T(8,128)(2,1)S(1)}, u32[]{:S(2)}, u32[]{:S(2)}) collective-permute-start(bf16[512,512]{1,0:T(8,128)(2,1)S(1)} %pad_maximum_fusion.refs_3_), channel_id=1, source_target_pairs={{0,96},{4,28},{8,104},{12,4},{16,112},{20,12},{24,120},{28,20},{32... | collective-permute-start | bytes 1572872 | tf_op jit(solution)/shard_map/ppermute | solution.py:40
  16.7 1.9 collective-permute-start.3
  18.8 4.0 %collective-permute-done.5.refs_3_ = bf16[512,512]{1,0:T(8,128)(2,1)S(1)} collective-permute-done((bf16[512,512]{1,0:T(8,128)(2,1)S(1)}, bf16[512,512]{1,0:T(8,128)(2,1)S(1)}, u32[]{:S(2)}, u32[]{:S(2)}) %collective-permute-start.5) | collective-permute-done | bytes 524320 | tf_op jit(solution)/shard_map/ppermute | solution.py:40
  22.9 5.3 %collective-permute-done.7.refs_5_ = bf16[512,512]{1,0:T(8,128)(2,1)S(1)} collective-permute-done((bf16[512,512]{1,0:T(8,128)(2,1)S(1)}, bf16[512,512]{1,0:T(8,128)(2,1)S(1)}, u32[]{:S(2)}, u32[]{:S(2)}) %collective-permute-start.7) | collective-permute-done | bytes 524320 | tf_op jit(solution)/shard_map/ppermute | solution.py:40
  28.1 1.8 collective-permute-done.3.refs_3_
  31.0 1.7 attend_part.2
  32.7 3.6 %attend_part.3 = (f32[1024,128]{1,0:T(8,128)S(1)}, f32[1024,128]{1,0:T(8,128)S(1)}, f32[1024,128]{1,0:T(8,128)S(1)}) custom-call(bf16[128,1024]{1,0:T(8,128)(2,1)S(1)} %copy-done.5, s32[128,128]{1,0:T(8,128)S(1)} %broadcast_in_dim.96.refs_1_, s32[4,512]{1,0:T(4,128)S(1)} %broadcast_add_fusion.refs_2_, bf16[512,512]{1,0:T(8,128)(2,1)S(1)} %collective-permute-done.5.refs_3_, ...), custom_call_target="tpu_custom_call" | custom-call | flops 2147483648 | bytes 4194304 | tf_op jit(solution)/shard_map/attend_part/pallas_call | solution.py:131
  36.4 3.8 %attend_last.1 = (f32[32,4096]{1,0:T(8,128)S(1)}, bf16[32,4096]{1,0:T(8,128)(2,1)S(1)}, bf16[32,4096]{1,0:T(8,128)(2,1)S(1)}, bf16[32,4096]{1,0:T(8,128)(2,1)S(1)}) custom-call(s32[1]{0:T(128)} %bitcast.mine_ref, bf16[128,1024]{1,0:T(8,128)(2,1)S(1)} %copy-done.5, s32[128,128]{1,0:T(8,128)S(1)} %broadcast_in_dim.96.refs_1_, ...), custom_call_target="tpu_custom_call" | custom-call | flops 1073741824 | bytes 4194304 | tf_op jit(solution)/shard_map/attend_last/pallas_call | solution.py:173
  40.2 3.3 %collective-permute-start.10 = (bf16[32,4096]{1,0:T(8,128)(2,1)S(1)}, bf16[32,4096]{1,0:T(8,128)(2,1)S(1)}, u32[]{:S(2)}, u32[]{:S(2)}) collective-permute-start(bf16[32,4096]{1,0:T(8,128)(2,1)S(1)} %get-tuple-element.30), channel_id=1, source_target_pairs={{0,2},{1,3},{2,0},{3,1},{4,6},{5,7},{6,4},{7,5},{8,10},{9,11},{10,... | collective-permute-start | bytes 786440 | tf_op jit(solution)/shard_map/ppermute | solution.py:48
  44.2 2.6 %collective-permute-start.12 = (bf16[32,4096]{1,0:T(8,128)(2,1)S(1)}, bf16[32,4096]{1,0:T(8,128)(2,1)S(1)}, u32[]{:S(2)}, u32[]{:S(2)}) collective-permute-start(bf16[32,4096]{1,0:T(8,128)(2,1)S(1)} %get-tuple-element.32), channel_id=1, source_target_pairs={{0,3},{1,0},{2,1},{3,2},{4,7},{5,4},{6,5},{7,6},{8,11},{9,8},{10,9... | collective-permute-start | bytes 786440 | tf_op jit(solution)/shard_map/ppermute | solution.py:48
  47.2 3.8 %collective-permute-done.10 = bf16[32,4096]{1,0:T(8,128)(2,1)S(1)} collective-permute-done((bf16[32,4096]{1,0:T(8,128)(2,1)S(1)}, bf16[32,4096]{1,0:T(8,128)(2,1)S(1)}, u32[]{:S(2)}, u32[]{:S(2)}) %collective-permute-start.10) | collective-permute-done | bytes 262176 | tf_op jit(solution)/shard_map/ppermute | solution.py:48
  51.0 5.1 %collective-permute-done.11 = bf16[32,4096]{1,0:T(8,128)(2,1)S(1)} collective-permute-done((bf16[32,4096]{1,0:T(8,128)(2,1)S(1)}, bf16[32,4096]{1,0:T(8,128)(2,1)S(1)}, u32[]{:S(2)}, u32[]{:S(2)}) %collective-permute-start.11) | collective-permute-done | bytes 262176 | tf_op jit(solution)/shard_map/ppermute | solution.py:48
  57.2 1.4 collective-permute-start.13
  58.7 2.7 %collective-permute-start.14 = (bf16[16,4096]{1,0:T(8,128)(2,1)S(1)}, bf16[16,4096]{1,0:T(8,128)(2,1)S(1)}, u32[]{:S(2)}, u32[]{:S(2)}) collective-permute-start(bf16[16,4096]{1,0:T(8,128)(2,1)S(1)} %get-tuple-element.54), channel_id=1, source_target_pairs={{0,2},{1,3},{2,0},{3,1},{4,6},{5,7},{6,4},{7,5},{8,10},{9,11},{10,... | collective-permute-start | bytes 393224 | tf_op jit(solution)/shard_map/ppermute | solution.py:48
  63.6 4.0 %collective-permute-done.14 = bf16[16,4096]{1,0:T(8,128)(2,1)S(1)} collective-permute-done((bf16[16,4096]{1,0:T(8,128)(2,1)S(1)}, bf16[16,4096]{1,0:T(8,128)(2,1)S(1)}, u32[]{:S(2)}, u32[]{:S(2)}) %collective-permute-start.14) | collective-permute-done | bytes 131104 | tf_op jit(solution)/shard_map/ppermute | solution.py:48
  67.7 1.8 collective-permute-start.17
  70.4 6.8 %collective-permute-done.17 = bf16[64,4096]{1,0:T(8,128)(2,1)S(1)} collective-permute-done((bf16[64,4096]{1,0:T(8,128)(2,1)S(1)}, bf16[64,4096]{1,0:T(8,128)(2,1)S(1)}, u32[]{:S(2)}, u32[]{:S(2)}) %collective-permute-start.17) | collective-permute-done | bytes 524320 | tf_op jit(solution)/shard_map/ppermute | solution.py:40
  77.5 2.7 %collective-permute-done.18 = bf16[64,4096]{1,0:T(8,128)(2,1)S(1)} collective-permute-done((bf16[64,4096]{1,0:T(8,128)(2,1)S(1)}, bf16[64,4096]{1,0:T(8,128)(2,1)S(1)}, u32[]{:S(2)}, u32[]{:S(2)}) %collective-permute-start.18) | collective-permute-done | bytes 524320 | tf_op jit(solution)/shard_map/ppermute | solution.py:40
  80.2 2.2 %collective-permute-start.23 = (bf16[128,4096]{1,0:T(8,128)(2,1)S(1)}, bf16[128,4096]{1,0:T(8,128)(2,1)S(1)}, u32[]{:S(2)}, u32[]{:S(2)}) collective-permute-start(bf16[128,4096]{1,0:T(8,128)(2,1)S(1)} %constant_dynamic-update-slice_fusion.7.refs_1_), channel_id=1, source_target_pairs={{0,96},{4,28},{8,104},{12,4},{16,112},{20,12},{24,120},{28,20},{32... | collective-permute-start | bytes 3145736 | tf_op jit(solution)/shard_map/ppermute | solution.py:40
  82.4 5.1 %collective-permute-done.16 = bf16[64,4096]{1,0:T(8,128)(2,1)S(1)} collective-permute-done((bf16[64,4096]{1,0:T(8,128)(2,1)S(1)}, bf16[64,4096]{1,0:T(8,128)(2,1)S(1)}, u32[]{:S(2)}, u32[]{:S(2)}) %collective-permute-start.16) | collective-permute-done | bytes 524320 | tf_op jit(solution)/shard_map/ppermute | solution.py:40
  87.6 1.5 collective-permute-start.22
  89.1 6.0 %collective-permute-done.23.refs_1_ = bf16[128,4096]{1,0:T(8,128)(2,1)S(1)} collective-permute-done((bf16[128,4096]{1,0:T(8,128)(2,1)S(1)}, bf16[128,4096]{1,0:T(8,128)(2,1)S(1)}, u32[]{:S(2)}, u32[]{:S(2)}) %collective-permute-start.23) | collective-permute-done | bytes 1048608 | tf_op jit(solution)/shard_map/ppermute | solution.py:40
  95.1 3.3 %collective-permute-start.25 = (bf16[128,4096]{1,0:T(8,128)(2,1)S(1)}, bf16[128,4096]{1,0:T(8,128)(2,1)S(1)}, u32[]{:S(2)}, u32[]{:S(2)}) collective-permute-start(bf16[128,4096]{1,0:T(8,128)(2,1)S(1)} %collective-permute-done.23.refs_1_), channel_id=1, source_target_pairs={{0,96},{4,28},{8,104},{12,4},{16,112},{20,12},{24,120},{28,20},{32... | collective-permute-start | bytes 3145736 | tf_op jit(solution)/shard_map/ppermute | solution.py:40
  98.4 5.2 %collective-permute-done.22.refs_0_ = bf16[128,4096]{1,0:T(8,128)(2,1)S(1)} collective-permute-done((bf16[128,4096]{1,0:T(8,128)(2,1)S(1)}, bf16[128,4096]{1,0:T(8,128)(2,1)S(1)}, u32[]{:S(2)}, u32[]{:S(2)}) %collective-permute-start.22) | collective-permute-done | bytes 1048608 | tf_op jit(solution)/shard_map/ppermute | solution.py:40
  103.9 3.2 %collective-permute-start.29 = (bf16[128,4096]{1,0:T(8,128)(2,1)S(1)}, bf16[128,4096]{1,0:T(8,128)(2,1)S(1)}, u32[]{:S(2)}, u32[]{:S(2)}) collective-permute-start(bf16[128,4096]{1,0:T(8,128)(2,1)S(1)} %constant_dynamic-update-slice_fusion.2.refs_0_), channel_id=1, source_target_pairs={{0,96},{4,28},{8,104},{12,4},{16,112},{20,12},{24,120},{28,20},{32... | collective-permute-start | bytes 3145736 | tf_op jit(solution)/shard_map/ppermute | solution.py:40
  107.1 3.6 %collective-permute-done.25.refs_1_ = bf16[128,4096]{1,0:T(8,128)(2,1)S(1)} collective-permute-done((bf16[128,4096]{1,0:T(8,128)(2,1)S(1)}, bf16[128,4096]{1,0:T(8,128)(2,1)S(1)}, u32[]{:S(2)}, u32[]{:S(2)}) %collective-permute-start.25) | collective-permute-done | bytes 1048608 | tf_op jit(solution)/shard_map/ppermute | solution.py:40
  110.8 8.9 %collective-permute-done.24.refs_0_ = bf16[128,4096]{1,0:T(8,128)(2,1)S(1)} collective-permute-done((bf16[128,4096]{1,0:T(8,128)(2,1)S(1)}, bf16[128,4096]{1,0:T(8,128)(2,1)S(1)}, u32[]{:S(2)}, u32[]{:S(2)}) %collective-permute-start.24) | collective-permute-done | bytes 1048608 | tf_op jit(solution)/shard_map/ppermute | solution.py:40
  119.6 2.0 copy-done.3
  121.7 9.8 %expert_rows.6 = (bf16[128,4096]{1,0:T(8,128)(2,1)S(1)}, bf16[128,4096]{1,0:T(8,128)(2,1)S(1)}) custom-call(bf16[128,4096]{1,0:T(8,128)(2,1)S(1)} %collective-permute-done.24.refs_0_, bf16[128,4096]{1,0:T(8,128)(2,1)S(1)} %collective-permute-done.25.refs_1_, bf16[448,4096]{1,0:T(8,128)(2,1)S(1)} %bitcast.29, bf16[448,4096]{1,0:T(8,128)(2,1)S(1)} %bitcast.34, ...), custom_call_target="tpu_custom_call" | custom-call | flops 5637144576 | bytes 22020096 | tf_op jit(solution)/shard_map/expert_rows/pallas_call | solution.py:261
  131.6 9.8 %expert_rows.7 = (bf16[128,4096]{1,0:T(8,128)(2,1)S(1)}, bf16[128,4096]{1,0:T(8,128)(2,1)S(1)}) custom-call(bf16[128,4096]{1,0:T(8,128)(2,1)S(1)} %collective-permute-done.28.refs_0_, bf16[128,4096]{1,0:T(8,128)(2,1)S(1)} %collective-permute-done.29.refs_1_, bf16[448,4096]{1,0:T(8,128)(2,1)S(1)} %bitcast.30, bf16[448,4096]{1,0:T(8,128)(2,1)S(1)} %bitcast.35, ...), custom_call_target="tpu_custom_call" | custom-call | flops 5637144576 | bytes 22020096 | tf_op jit(solution)/shard_map/expert_rows/pallas_call | solution.py:261
  141.4 2.1 collective-permute-start.30
  143.5 1.2 collective-permute-start.32
  145.5 9.8 %expert_rows.5 = (bf16[128,4096]{1,0:T(8,128)(2,1)S(1)}, bf16[128,4096]{1,0:T(8,128)(2,1)S(1)}) custom-call(bf16[128,4096]{1,0:T(8,128)(2,1)S(1)} %collective-permute-done.22.refs_0_, bf16[128,4096]{1,0:T(8,128)(2,1)S(1)} %collective-permute-done.23.refs_1_, bf16[448,4096]{1,0:T(8,128)(2,1)S(1)} %bitcast.31, bf16[448,4096]{1,0:T(8,128)(2,1)S(1)} %bitcast.36, ...), custom_call_target="tpu_custom_call" | custom-call | flops 5637144576 | bytes 22020096 | tf_op jit(solution)/shard_map/expert_rows/pallas_call | solution.py:261
  155.6 2.5 %collective-permute-start.27 = (bf16[128,4096]{1,0:T(8,128)(2,1)S(1)}, bf16[128,4096]{1,0:T(8,128)(2,1)S(1)}, u32[]{:S(2)}, u32[]{:S(2)}) collective-permute-start(bf16[128,4096]{1,0:T(8,128)(2,1)S(1)} %add_convert_fusion.3), channel_id=1, source_target_pairs={{0,96},{4,28},{8,104},{12,4},{16,112},{20,12},{24,120},{28,20},{32... | collective-permute-start | bytes 3145736 | tf_op jit(solution)/shard_map/ppermute | solution.py:40
  158.1 10.6 %collective-permute-done.33 = bf16[128,4096]{1,0:T(8,128)(2,1)S(1)} collective-permute-done((bf16[128,4096]{1,0:T(8,128)(2,1)S(1)}, bf16[128,4096]{1,0:T(8,128)(2,1)S(1)}, u32[]{:S(2)}, u32[]{:S(2)}) %collective-permute-start.33) | collective-permute-done | bytes 1048608 | tf_op jit(solution)/shard_map/ppermute | solution.py:40
  169.8 9.8 %expert_rows.4 = (bf16[128,4096]{1,0:T(8,128)(2,1)S(1)}, bf16[128,4096]{1,0:T(8,128)(2,1)S(1)}) custom-call(bf16[128,4096]{1,0:T(8,128)(2,1)S(1)} %constant_dynamic-update-slice_fusion.2.refs_0_, bf16[128,4096]{1,0:T(8,128)(2,1)S(1)} %constant_dynamic-update-slice_fusion.7.refs_1_, bf16[448,4096]{1,0:T(8,128)(2,1)S(1)} %bitcast.32, ...), custom_call_target="tpu_custom_call" | custom-call | flops 5637144576 | bytes 22020096 | tf_op jit(solution)/shard_map/expert_rows/pallas_call | solution.py:261
  180.2 1.6 collective-permute-start.31
  181.8 3.2 %collective-permute-done.34 = bf16[128,4096]{1,0:T(8,128)(2,1)S(1)} collective-permute-done((bf16[128,4096]{1,0:T(8,128)(2,1)S(1)}, bf16[128,4096]{1,0:T(8,128)(2,1)S(1)}, u32[]{:S(2)}, u32[]{:S(2)}) %collective-permute-start.34) | collective-permute-done | bytes 1048608 | tf_op jit(solution)/shard_map/ppermute | solution.py:40
  186.6 3.0 %collective-permute-start.36 = (bf16[64,4096]{1,0:T(8,128)(2,1)}, bf16[64,4096]{1,0:T(8,128)(2,1)S(1)}, u32[]{:S(2)}, u32[]{:S(2)}) collective-permute-start(bf16[64,4096]{1,0:T(8,128)(2,1)} %get-tuple-element.46), channel_id=1, source_target_pairs={{0,16},{4,68},{8,24},{12,76},{16,0},{20,84},{24,8},{28,92},{32,48}... | collective-permute-start | bytes 1572872 | tf_op jit(solution)/shard_map/ppermute | solution.py:40
  190.1 12.7 %collective-permute-done.35 = bf16[64,4096]{1,0:T(8,128)(2,1)S(1)} collective-permute-done((bf16[64,4096]{1,0:T(8,128)(2,1)}, bf16[64,4096]{1,0:T(8,128)(2,1)S(1)}, u32[]{:S(2)}, u32[]{:S(2)}) %collective-permute-start.35) | collective-permute-done | bytes 524320 | tf_op jit(solution)/shard_map/ppermute | solution.py:40
  203.1 2.2 %collective-permute-start.37 = (bf16[16,4096]{1,0:T(8,128)(2,1)S(1)}, bf16[16,4096]{1,0:T(8,128)(2,1)S(1)}, u32[]{:S(2)}, u32[]{:S(2)}) collective-permute-start(bf16[16,4096]{1,0:T(8,128)(2,1)S(1)} %get-tuple-element.50), channel_id=1, source_target_pairs={{0,3},{1,0},{2,1},{3,2},{4,7},{5,4},{6,5},{7,6},{8,11},{9,8},{10,9... | collective-permute-start | bytes 393224 | tf_op jit(solution)/shard_map/ppermute | solution.py:48
  206.4 4.2 %collective-permute-done.37 = bf16[16,4096]{1,0:T(8,128)(2,1)S(1)} collective-permute-done((bf16[16,4096]{1,0:T(8,128)(2,1)S(1)}, bf16[16,4096]{1,0:T(8,128)(2,1)S(1)}, u32[]{:S(2)}, u32[]{:S(2)}) %collective-permute-start.37) | collective-permute-done | bytes 131104 | tf_op jit(solution)/shard_map/ppermute | solution.py:48
  210.6 2.3 %collective-permute-done.38 = bf16[16,4096]{1,0:T(8,128)(2,1)S(1)} collective-permute-done((bf16[16,4096]{1,0:T(8,128)(2,1)S(1)}, bf16[16,4096]{1,0:T(8,128)(2,1)S(1)}, u32[]{:S(2)}, u32[]{:S(2)}) %collective-permute-start.38) | collective-permute-done | bytes 131104 | tf_op jit(solution)/shard_map/ppermute | solution.py:48
  212.9 1.3 collective-permute-done.39
  (141 shorter events, 21.6 us)
Async XLA Ops:
  0.0 189.6 %copy-start = (f32[4096,4]{0,1:T(4,128)S(1)}, f32[4096,4]{0,1:T(4,128)}, u32[]{:S(2)}) copy-start(f32[4096,4]{0,1:T(4,128)} %param.27) | copy-start | bytes 196612
  1.7 9.4 %collective-permute-start = (bf16[128,512]{1,0:T(8,128)(2,1)S(1)}, bf16[128,512]{1,0:T(8,128)(2,1)S(1)}, u32[]{:S(2)}, u32[]{:S(2)}) collective-permute-start(bf16[128,512]{1,0:T(8,128)(2,1)S(1)} %constant_dynamic-update-slice_fusion), channel_id=1, source_target_pairs={{0,8},{4,36},{8,16},{12,44},{16,24},{20,52},{24,0},{28,60},{32,40}... | collective-permute-start | bytes 393224 | tf_op jit(solution)/shard_map/ppermute | solution.py:40
  3.3 7.8 %collective-permute-start.1 = (bf16[128,512]{1,0:T(8,128)(2,1)S(1)}, bf16[128,512]{1,0:T(8,128)(2,1)S(1)}, u32[]{:S(2)}, u32[]{:S(2)}) collective-permute-start(bf16[128,512]{1,0:T(8,128)(2,1)S(1)} %constant_dynamic-update-slice_fusion), channel_id=1, source_target_pairs={{0,24},{4,100},{8,0},{12,108},{16,8},{20,116},{24,16},{28,124},{32... | collective-permute-start | bytes 393224 | tf_op jit(solution)/shard_map/ppermute | solution.py:40
  5.0 6.5 %collective-permute-start.2 = (bf16[128,512]{1,0:T(8,128)(2,1)S(1)}, bf16[128,512]{1,0:T(8,128)(2,1)S(1)}, u32[]{:S(2)}, u32[]{:S(2)}) collective-permute-start(bf16[128,512]{1,0:T(8,128)(2,1)S(1)} %constant_dynamic-update-slice_fusion), channel_id=1, source_target_pairs={{0,16},{4,68},{8,24},{12,76},{16,0},{20,84},{24,8},{28,92},{32,48}... | collective-permute-start | bytes 393224 | tf_op jit(solution)/shard_map/ppermute | solution.py:40
  11.5 11.4 %collective-permute-start.5 = (bf16[512,512]{1,0:T(8,128)(2,1)S(1)}, bf16[512,512]{1,0:T(8,128)(2,1)S(1)}, u32[]{:S(2)}, u32[]{:S(2)}) collective-permute-start(bf16[512,512]{1,0:T(8,128)(2,1)S(1)} %pad_maximum_fusion.refs_3_), channel_id=1, source_target_pairs={{0,32},{4,12},{8,40},{12,20},{16,48},{20,28},{24,56},{28,4},{32,64... | collective-permute-start | bytes 1572872 | tf_op jit(solution)/shard_map/ppermute | solution.py:40
  13.6 14.6 %collective-permute-start.7 = (bf16[512,512]{1,0:T(8,128)(2,1)S(1)}, bf16[512,512]{1,0:T(8,128)(2,1)S(1)}, u32[]{:S(2)}, u32[]{:S(2)}) collective-permute-start(bf16[512,512]{1,0:T(8,128)(2,1)S(1)} %pad_maximum_fusion.refs_3_), channel_id=1, source_target_pairs={{0,96},{4,28},{8,104},{12,4},{16,112},{20,12},{24,120},{28,20},{32... | collective-permute-start | bytes 1572872 | tf_op jit(solution)/shard_map/ppermute | solution.py:40
  16.7 13.2 %collective-permute-start.3 = (bf16[512,512]{1,0:T(8,128)(2,1)S(1)}, bf16[512,512]{1,0:T(8,128)(2,1)S(1)}, u32[]{:S(2)}, u32[]{:S(2)}) collective-permute-start(bf16[512,512]{1,0:T(8,128)(2,1)S(1)} %pad_maximum_fusion.refs_3_), channel_id=1, source_target_pairs={{0,64},{4,20},{8,72},{12,28},{16,80},{20,4},{24,88},{28,12},{32,96... | collective-permute-start | bytes 1572872 | tf_op jit(solution)/shard_map/ppermute | solution.py:40
  18.8 11.2 %collective-permute-start.9 = (bf16[512,512]{1,0:T(8,128)(2,1)S(1)}, bf16[512,512]{1,0:T(8,128)(2,1)S(1)}, u32[]{:S(2)}, u32[]{:S(2)}) collective-permute-start(bf16[512,512]{1,0:T(8,128)(2,1)S(1)} %pad_maximum_fusion.refs_3_), channel_id=1, source_target_pairs={{0,4},{4,0},{8,12},{12,8},{16,20},{20,16},{24,28},{28,24},{32,36},... | collective-permute-start | bytes 1572872 | tf_op jit(solution)/shard_map/ppermute | solution.py:44
  22.9 9.8 %collective-permute-start.6 = (bf16[512,512]{1,0:T(8,128)(2,1)S(1)}, bf16[512,512]{1,0:T(8,128)(2,1)S(1)}, u32[]{:S(2)}, u32[]{:S(2)}) collective-permute-start(bf16[512,512]{1,0:T(8,128)(2,1)S(1)} %collective-permute-done.5.refs_3_), channel_id=1, source_target_pairs={{0,4},{4,0},{8,12},{12,8},{16,20},{20,16},{24,28},{28,24},{32,36},... | collective-permute-start | bytes 1572872 | tf_op jit(solution)/shard_map/ppermute | solution.py:44
  28.1 4.6 %collective-permute-start.8 = (bf16[512,512]{1,0:T(8,128)(2,1)S(1)}, bf16[512,512]{1,0:T(8,128)(2,1)S(1)}, u32[]{:S(2)}, u32[]{:S(2)}) collective-permute-start(bf16[512,512]{1,0:T(8,128)(2,1)S(1)} %collective-permute-done.7.refs_5_), channel_id=1, source_target_pairs={{0,4},{4,0},{8,12},{12,8},{16,20},{20,16},{24,28},{28,24},{32,36},... | collective-permute-start | bytes 1572872 | tf_op jit(solution)/shard_map/ppermute | solution.py:44
  29.9 6.4 %collective-permute-start.4 = (bf16[512,512]{1,0:T(8,128)(2,1)S(1)}, bf16[512,512]{1,0:T(8,128)(2,1)S(1)}, u32[]{:S(2)}, u32[]{:S(2)}) collective-permute-start(bf16[512,512]{1,0:T(8,128)(2,1)S(1)} %collective-permute-done.3.refs_3_), channel_id=1, source_target_pairs={{0,4},{4,0},{8,12},{12,8},{16,20},{20,16},{24,28},{28,24},{32,36},... | collective-permute-start | bytes 1572872 | tf_op jit(solution)/shard_map/ppermute | solution.py:44
  31.0 5.3 %copy-start.4 = (bf16[1024,4096]{1,0:T(8,128)(2,1)S(1)}, bf16[1024,4096]{1,0:T(8,128)(2,1)}, u32[]{:S(2)}) copy-start(bf16[1024,4096]{1,0:T(8,128)(2,1)} %refs_8_.1) | copy-start | bytes 25165828
  36.3 10.4 %copy-start.10 = (s32[32,2]{0,1:T(2,128)S(1)}, s32[32,2]{0,1:T(2,128)}, u32[]{:S(2)}) copy-start(s32[32,2]{0,1:T(2,128)} %param.28) | copy-start | bytes 772
  36.4 20.2 %copy-start.8 = (bf16[32,4096]{1,0:T(8,128)(2,1)S(1)}, bf16[32,4096]{1,0:T(8,128)(2,1)}, u32[]{:S(2)}) copy-start(bf16[32,4096]{1,0:T(8,128)(2,1)} %param.23) | copy-start | bytes 786436
  36.4 20.4 %copy-start.9 = (f32[4096]{0:T(1024)S(1)}, f32[4096]{0:T(1024)}, u32[]{:S(2)}) copy-start(f32[4096]{0:T(1024)} %param.26) | copy-start | bytes 49156
  40.2 10.8 %collective-permute-start.10 = (bf16[32,4096]{1,0:T(8,128)(2,1)S(1)}, bf16[32,4096]{1,0:T(8,128)(2,1)S(1)}, u32[]{:S(2)}, u32[]{:S(2)}) collective-permute-start(bf16[32,4096]{1,0:T(8,128)(2,1)S(1)} %get-tuple-element.30), channel_id=1, source_target_pairs={{0,2},{1,3},{2,0},{3,1},{4,6},{5,7},{6,4},{7,5},{8,10},{9,11},{10,... | collective-permute-start | bytes 786440 | tf_op jit(solution)/shard_map/ppermute | solution.py:48
  43.5 12.6 %collective-permute-start.11 = (bf16[32,4096]{1,0:T(8,128)(2,1)S(1)}, bf16[32,4096]{1,0:T(8,128)(2,1)S(1)}, u32[]{:S(2)}, u32[]{:S(2)}) collective-permute-start(bf16[32,4096]{1,0:T(8,128)(2,1)S(1)} %get-tuple-element.31), channel_id=1, source_target_pairs={{0,1},{1,2},{2,3},{3,0},{4,5},{5,6},{6,7},{7,4},{8,9},{9,10},{10,1... | collective-permute-start | bytes 786440 | tf_op jit(solution)/shard_map/ppermute | solution.py:48
  44.2 12.3 %collective-permute-start.12 = (bf16[32,4096]{1,0:T(8,128)(2,1)S(1)}, bf16[32,4096]{1,0:T(8,128)(2,1)S(1)}, u32[]{:S(2)}, u32[]{:S(2)}) collective-permute-start(bf16[32,4096]{1,0:T(8,128)(2,1)S(1)} %get-tuple-element.32), channel_id=1, source_target_pairs={{0,3},{1,0},{2,1},{3,2},{4,7},{5,4},{6,5},{7,6},{8,11},{9,8},{10,9... | collective-permute-start | bytes 786440 | tf_op jit(solution)/shard_map/ppermute | solution.py:48
  47.1 14.8 %copy-start.1 = (bf16[1,4096,448]{1,2,0:T(8,128)(2,1)S(1)}, bf16[1,4096,448]{1,2,0:T(8,128)(2,1)}, u32[]{:S(2)}) copy-start(bf16[1,4096,448]{1,2,0:T(8,128)(2,1)} %param.29) | copy-start | bytes 11010052
  57.2 6.4 %collective-permute-start.13 = (bf16[16,4096]{1,0:T(8,128)(2,1)S(1)}, bf16[16,4096]{1,0:T(8,128)(2,1)S(1)}, u32[]{:S(2)}, u32[]{:S(2)}) collective-permute-start(bf16[16,4096]{1,0:T(8,128)(2,1)S(1)} %get-tuple-element.55), channel_id=1, source_target_pairs={{0,1},{1,2},{2,3},{3,0},{4,5},{5,6},{6,7},{7,4},{8,9},{9,10},{10,1... | collective-permute-start | bytes 393224 | tf_op jit(solution)/shard_map/ppermute | solution.py:48
  58.7 8.9 %collective-permute-start.14 = (bf16[16,4096]{1,0:T(8,128)(2,1)S(1)}, bf16[16,4096]{1,0:T(8,128)(2,1)S(1)}, u32[]{:S(2)}, u32[]{:S(2)}) collective-permute-start(bf16[16,4096]{1,0:T(8,128)(2,1)S(1)} %get-tuple-element.54), channel_id=1, source_target_pairs={{0,2},{1,3},{2,0},{3,1},{4,6},{5,7},{6,4},{7,5},{8,10},{9,11},{10,... | collective-permute-start | bytes 393224 | tf_op jit(solution)/shard_map/ppermute | solution.py:48
  61.4 6.2 %collective-permute-start.15 = (bf16[16,4096]{1,0:T(8,128)(2,1)S(1)}, bf16[16,4096]{1,0:T(8,128)(2,1)S(1)}, u32[]{:S(2)}, u32[]{:S(2)}) collective-permute-start(bf16[16,4096]{1,0:T(8,128)(2,1)S(1)} %get-tuple-element.53), channel_id=1, source_target_pairs={{0,3},{1,0},{2,1},{3,2},{4,7},{5,4},{6,5},{7,6},{8,11},{9,8},{10,9... | collective-permute-start | bytes 393224 | tf_op jit(solution)/shard_map/ppermute | solution.py:48
  62.0 41.9 %collective-permute-start.19 = (bf16[448,4096]{1,0:T(8,128)(2,1)S(1)}, bf16[448,4096]{1,0:T(8,128)(2,1)S(1)}, u32[]{:S(2)}, u32[]{:S(2)}) collective-permute-start(bf16[448,4096]{1,0:T(8,128)(2,1)S(1)} %bitcast.28), channel_id=1, source_target_pairs={{0,4},{4,0},{8,12},{12,8},{16,20},{20,16},{24,28},{28,24},{32,36},... | collective-permute-start | bytes 11010056 | tf_op jit(solution)/shard_map/ppermute | solution.py:44
  62.0 41.9 %collective-permute-start.20 = (bf16[448,4096]{1,0:T(8,128)(2,1)}, bf16[448,4096]{1,0:T(8,128)(2,1)S(1)}, u32[]{:S(2)}, u32[]{:S(2)}) collective-permute-start(bf16[448,4096]{1,0:T(8,128)(2,1)} %bitcast.33), channel_id=1, source_target_pairs={{0,4},{4,0},{8,12},{12,8},{16,20},{20,16},{24,28},{28,24},{32,36},... | collective-permute-start | bytes 11010056 | tf_op jit(solution)/shard_map/ppermute | solution.py:44
  63.6 43.5 %collective-permute-start.21 = (bf16[448,4096]{1,0:T(8,128)(2,1)}, bf16[448,4096]{1,0:T(8,128)(2,1)S(1)}, u32[]{:S(2)}, u32[]{:S(2)}) collective-permute-start(bf16[448,4096]{1,0:T(8,128)(2,1)} %bitcast.38), channel_id=1, source_target_pairs={{0,4},{4,0},{8,12},{12,8},{16,20},{20,16},{24,28},{28,24},{32,36},... | collective-permute-start | bytes 11010056 | tf_op jit(solution)/shard_map/ppermute | solution.py:44
  67.6 52.0 %copy-start.2 = (bf16[1,4096,448]{1,2,0:T(8,128)(2,1)S(1)}, bf16[1,4096,448]{1,2,0:T(8,128)(2,1)}, u32[]{:S(2)}) copy-start(bf16[1,4096,448]{1,2,0:T(8,128)(2,1)} %param.30) | copy-start | bytes 11010052
  67.7 9.5 %collective-permute-start.17 = (bf16[64,4096]{1,0:T(8,128)(2,1)S(1)}, bf16[64,4096]{1,0:T(8,128)(2,1)S(1)}, u32[]{:S(2)}, u32[]{:S(2)}) collective-permute-start(bf16[64,4096]{1,0:T(8,128)(2,1)S(1)} %pad_maximum_fusion.1), channel_id=1, source_target_pairs={{0,24},{4,100},{8,0},{12,108},{16,8},{20,116},{24,16},{28,124},{32... | collective-permute-start | bytes 1572872 | tf_op jit(solution)/shard_map/ppermute | solution.py:40
  69.5 10.7 %collective-permute-start.18 = (bf16[64,4096]{1,0:T(8,128)(2,1)S(1)}, bf16[64,4096]{1,0:T(8,128)(2,1)S(1)}, u32[]{:S(2)}, u32[]{:S(2)}) collective-permute-start(bf16[64,4096]{1,0:T(8,128)(2,1)S(1)} %pad_maximum_fusion.1), channel_id=1, source_target_pairs={{0,16},{4,68},{8,24},{12,76},{16,0},{20,84},{24,8},{28,92},{32,48}... | collective-permute-start | bytes 1572872 | tf_op jit(solution)/shard_map/ppermute | solution.py:40
  77.1 10.4 %collective-permute-start.16 = (bf16[64,4096]{1,0:T(8,128)(2,1)S(1)}, bf16[64,4096]{1,0:T(8,128)(2,1)S(1)}, u32[]{:S(2)}, u32[]{:S(2)}) collective-permute-start(bf16[64,4096]{1,0:T(8,128)(2,1)S(1)} %pad_maximum_fusion.1), channel_id=1, source_target_pairs={{0,8},{4,36},{8,16},{12,44},{16,24},{20,52},{24,0},{28,60},{32,40}... | collective-permute-start | bytes 1572872 | tf_op jit(solution)/shard_map/ppermute | solution.py:40
  80.2 14.9 %collective-permute-start.23 = (bf16[128,4096]{1,0:T(8,128)(2,1)S(1)}, bf16[128,4096]{1,0:T(8,128)(2,1)S(1)}, u32[]{:S(2)}, u32[]{:S(2)}) collective-permute-start(bf16[128,4096]{1,0:T(8,128)(2,1)S(1)} %constant_dynamic-update-slice_fusion.7.refs_1_), channel_id=1, source_target_pairs={{0,96},{4,28},{8,104},{12,4},{16,112},{20,12},{24,120},{28,20},{32... | collective-permute-start | bytes 3145736 | tf_op jit(solution)/shard_map/ppermute | solution.py:40
  87.6 16.1 %collective-permute-start.22 = (bf16[128,4096]{1,0:T(8,128)(2,1)S(1)}, bf16[128,4096]{1,0:T(8,128)(2,1)S(1)}, u32[]{:S(2)}, u32[]{:S(2)}) collective-permute-start(bf16[128,4096]{1,0:T(8,128)(2,1)S(1)} %constant_dynamic-update-slice_fusion.2.refs_0_), channel_id=1, source_target_pairs={{0,32},{4,12},{8,40},{12,20},{16,48},{20,28},{24,56},{28,4},{32,64... | collective-permute-start | bytes 3145736 | tf_op jit(solution)/shard_map/ppermute | solution.py:40
  95.1 15.7 %collective-permute-start.25 = (bf16[128,4096]{1,0:T(8,128)(2,1)S(1)}, bf16[128,4096]{1,0:T(8,128)(2,1)S(1)}, u32[]{:S(2)}, u32[]{:S(2)}) collective-permute-start(bf16[128,4096]{1,0:T(8,128)(2,1)S(1)} %collective-permute-done.23.refs_1_), channel_id=1, source_target_pairs={{0,96},{4,28},{8,104},{12,4},{16,112},{20,12},{24,120},{28,20},{32... | collective-permute-start | bytes 3145736 | tf_op jit(solution)/shard_map/ppermute | solution.py:40
  103.6 16.0 %collective-permute-start.24 = (bf16[128,4096]{1,0:T(8,128)(2,1)S(1)}, bf16[128,4096]{1,0:T(8,128)(2,1)S(1)}, u32[]{:S(2)}, u32[]{:S(2)}) collective-permute-start(bf16[128,4096]{1,0:T(8,128)(2,1)S(1)} %collective-permute-done.22.refs_0_), channel_id=1, source_target_pairs={{0,32},{4,12},{8,40},{12,20},{16,48},{20,28},{24,56},{28,4},{32,64... | collective-permute-start | bytes 3145736 | tf_op jit(solution)/shard_map/ppermute | solution.py:40
  103.9 27.7 %collective-permute-start.28 = (bf16[128,4096]{1,0:T(8,128)(2,1)S(1)}, bf16[128,4096]{1,0:T(8,128)(2,1)S(1)}, u32[]{:S(2)}, u32[]{:S(2)}) collective-permute-start(bf16[128,4096]{1,0:T(8,128)(2,1)S(1)} %constant_dynamic-update-slice_fusion.7.refs_1_), channel_id=1, source_target_pairs={{0,32},{4,12},{8,40},{12,20},{16,48},{20,28},{24,56},{28,4},{32,64... | collective-permute-start | bytes 3145736 | tf_op jit(solution)/shard_map/ppermute | solution.py:40
  103.9 6.9 %copy-start.6 = (bf16[448,4096]{1,0:T(8,128)(2,1)}, bf16[448,4096]{1,0:T(8,128)(2,1)S(1)}, u32[]{:S(2)}) copy-start(bf16[448,4096]{1,0:T(8,128)(2,1)S(1)} %collective-permute-done.20.refs_6_) | copy-start | bytes 11010052
  103.9 27.7 %collective-permute-start.29 = (bf16[128,4096]{1,0:T(8,128)(2,1)S(1)}, bf16[128,4096]{1,0:T(8,128)(2,1)S(1)}, u32[]{:S(2)}, u32[]{:S(2)}) collective-permute-start(bf16[128,4096]{1,0:T(8,128)(2,1)S(1)} %constant_dynamic-update-slice_fusion.2.refs_0_), channel_id=1, source_target_pairs={{0,96},{4,28},{8,104},{12,4},{16,112},{20,12},{24,120},{28,20},{32... | collective-permute-start | bytes 3145736 | tf_op jit(solution)/shard_map/ppermute | solution.py:40
  131.5 23.8 %collective-permute-start.26 = (bf16[128,4096]{1,0:T(8,128)(2,1)S(1)}, bf16[128,4096]{1,0:T(8,128)(2,1)S(1)}, u32[]{:S(2)}, u32[]{:S(2)}) collective-permute-start(bf16[128,4096]{1,0:T(8,128)(2,1)S(1)} %get-tuple-element.35), channel_id=1, source_target_pairs={{0,96},{4,28},{8,104},{12,4},{16,112},{20,12},{24,120},{28,20},{32... | collective-permute-start | bytes 3145736 | tf_op jit(solution)/shard_map/ppermute | solution.py:40
  141.4 38.2 %collective-permute-start.30 = (bf16[128,4096]{1,0:T(8,128)(2,1)S(1)}, bf16[128,4096]{1,0:T(8,128)(2,1)S(1)}, u32[]{:S(2)}, u32[]{:S(2)}) collective-permute-start(bf16[128,4096]{1,0:T(8,128)(2,1)S(1)} %get-tuple-element.36), channel_id=1, source_target_pairs={{0,32},{4,12},{8,40},{12,20},{16,48},{20,28},{24,56},{28,4},{32,64... | collective-permute-start | bytes 3145736 | tf_op jit(solution)/shard_map/ppermute | solution.py:40
  143.5 38.4 %collective-permute-start.32 = (bf16[128,4096]{1,0:T(8,128)(2,1)S(1)}, bf16[128,4096]{1,0:T(8,128)(2,1)S(1)}, u32[]{:S(2)}, u32[]{:S(2)}) collective-permute-start(bf16[128,4096]{1,0:T(8,128)(2,1)S(1)} %get-tuple-element.38), channel_id=1, source_target_pairs={{0,96},{4,28},{8,104},{12,4},{16,112},{20,12},{24,120},{28,20},{32... | collective-permute-start | bytes 3145736 | tf_op jit(solution)/shard_map/ppermute | solution.py:40
  144.7 24.0 %collective-permute-start.33 = (bf16[128,4096]{1,0:T(8,128)(2,1)S(1)}, bf16[128,4096]{1,0:T(8,128)(2,1)S(1)}, u32[]{:S(2)}, u32[]{:S(2)}) collective-permute-start(bf16[128,4096]{1,0:T(8,128)(2,1)S(1)} %get-tuple-element.40), channel_id=1, source_target_pairs={{0,32},{4,12},{8,40},{12,20},{16,48},{20,28},{24,56},{28,4},{32,64... | collective-permute-start | bytes 3145736 | tf_op jit(solution)/shard_map/ppermute | solution.py:40
  155.6 24.1 %collective-permute-start.27 = (bf16[128,4096]{1,0:T(8,128)(2,1)S(1)}, bf16[128,4096]{1,0:T(8,128)(2,1)S(1)}, u32[]{:S(2)}, u32[]{:S(2)}) collective-permute-start(bf16[128,4096]{1,0:T(8,128)(2,1)S(1)} %add_convert_fusion.3), channel_id=1, source_target_pairs={{0,96},{4,28},{8,104},{12,4},{16,112},{20,12},{24,120},{28,20},{32... | collective-permute-start | bytes 3145736 | tf_op jit(solution)/shard_map/ppermute | solution.py:40
  169.0 16.1 %collective-permute-start.34 = (bf16[128,4096]{1,0:T(8,128)(2,1)S(1)}, bf16[128,4096]{1,0:T(8,128)(2,1)S(1)}, u32[]{:S(2)}, u32[]{:S(2)}) collective-permute-start(bf16[128,4096]{1,0:T(8,128)(2,1)S(1)} %add_convert_fusion.1), channel_id=1, source_target_pairs={{0,32},{4,12},{8,40},{12,20},{16,48},{20,28},{24,56},{28,4},{32,64... | collective-permute-start | bytes 3145736 | tf_op jit(solution)/shard_map/ppermute | solution.py:40
  180.2 9.9 %collective-permute-start.31 = (bf16[64,4096]{1,0:T(8,128)(2,1)S(1)}, bf16[64,4096]{1,0:T(8,128)(2,1)S(1)}, u32[]{:S(2)}, u32[]{:S(2)}) collective-permute-start(bf16[64,4096]{1,0:T(8,128)(2,1)S(1)} %slice.53), channel_id=1, source_target_pairs={{0,24},{4,100},{8,0},{12,108},{16,8},{20,116},{24,16},{28,124},{32... | collective-permute-start | bytes 1572872 | tf_op jit(solution)/shard_map/ppermute | solution.py:40
  186.6 16.2 %collective-permute-start.35 = (bf16[64,4096]{1,0:T(8,128)(2,1)}, bf16[64,4096]{1,0:T(8,128)(2,1)S(1)}, u32[]{:S(2)}, u32[]{:S(2)}) collective-permute-start(bf16[64,4096]{1,0:T(8,128)(2,1)} %get-tuple-element.45), channel_id=1, source_target_pairs={{0,8},{4,36},{8,16},{12,44},{16,24},{20,52},{24,0},{28,60},{32,40}... | collective-permute-start | bytes 1572872 | tf_op jit(solution)/shard_map/ppermute | solution.py:40
  186.6 16.2 %collective-permute-start.36 = (bf16[64,4096]{1,0:T(8,128)(2,1)}, bf16[64,4096]{1,0:T(8,128)(2,1)S(1)}, u32[]{:S(2)}, u32[]{:S(2)}) collective-permute-start(bf16[64,4096]{1,0:T(8,128)(2,1)} %get-tuple-element.46), channel_id=1, source_target_pairs={{0,16},{4,68},{8,24},{12,76},{16,0},{20,84},{24,8},{28,92},{32,48}... | collective-permute-start | bytes 1572872 | tf_op jit(solution)/shard_map/ppermute | solution.py:40
  203.1 7.4 %collective-permute-start.37 = (bf16[16,4096]{1,0:T(8,128)(2,1)S(1)}, bf16[16,4096]{1,0:T(8,128)(2,1)S(1)}, u32[]{:S(2)}, u32[]{:S(2)}) collective-permute-start(bf16[16,4096]{1,0:T(8,128)(2,1)S(1)} %get-tuple-element.50), channel_id=1, source_target_pairs={{0,3},{1,0},{2,1},{3,2},{4,7},{5,4},{6,5},{7,6},{8,11},{9,8},{10,9... | collective-permute-start | bytes 393224 | tf_op jit(solution)/shard_map/ppermute | solution.py:48
  205.4 7.5 %collective-permute-start.38 = (bf16[16,4096]{1,0:T(8,128)(2,1)S(1)}, bf16[16,4096]{1,0:T(8,128)(2,1)S(1)}, u32[]{:S(2)}, u32[]{:S(2)}) collective-permute-start(bf16[16,4096]{1,0:T(8,128)(2,1)S(1)} %get-tuple-element.49), channel_id=1, source_target_pairs={{0,2},{1,3},{2,0},{3,1},{4,6},{5,7},{6,4},{7,5},{8,10},{9,11},{10,... | collective-permute-start | bytes 393224 | tf_op jit(solution)/shard_map/ppermute | solution.py:48
  206.0 8.1 %collective-permute-start.39 = (bf16[16,4096]{1,0:T(8,128)(2,1)S(1)}, bf16[16,4096]{1,0:T(8,128)(2,1)S(1)}, u32[]{:S(2)}, u32[]{:S(2)}) collective-permute-start(bf16[16,4096]{1,0:T(8,128)(2,1)S(1)} %get-tuple-element.48), channel_id=1, source_target_pairs={{0,1},{1,2},{2,3},{3,0},{4,5},{5,6},{6,7},{7,4},{8,9},{9,10},{10,1... | collective-permute-start | bytes 393224 | tf_op jit(solution)/shard_map/ppermute | solution.py:48
  (3 other events, 6.6 us)

commit v2 on v1

v2 whole, which is shorter than its diff:
```python
import math

import jax
import jax.numpy as jnp
from jax import lax
from jax.experimental import pallas as pl
from jax.experimental.pallas import tpu as pltpu
from jax.sharding import PartitionSpec as P

HEAD_SIZE = 128
SPAN = 64
RING = 4
NEVER = -1e30

f32 = jnp.float32
bf16 = jnp.bfloat16
i32 = jnp.int32


def ctx_index_of(z, x, core):
    return (z % RING) * 8 + (x % RING) * 2 + core


def ring_pairs(phase, step):
    pairs = []
    for z in range(RING):
        for x in range(RING):
            for core in range(2):
                along_x = (core == 0) == (phase == 1)
                target = ctx_index_of(z, x + step, core) if along_x else ctx_index_of(z + step, x, core)
                pairs.append((ctx_index_of(z, x, core), target))
    return pairs


RINGS = {(phase, step): ring_pairs(phase, step) for phase in (1, 2) for step in (1, -1, 2)}
SWAP = [(i, i ^ 1) for i in range(32)]


def shift(a, phase, step):
    return lax.ppermute(a, "ctx", RINGS[phase, step])


def swap(a):
    return lax.ppermute(a, "ctx", SWAP)


def shift_exp(a, step):
    return lax.ppermute(a, "exp", [(i, (i + step) % 4) for i in range(4)])


def join(*parts):
    return jnp.concatenate(parts, axis=0)


def total(*terms):
    return sum(t.astype(f32) for t in terms).astype(bf16)


def positions_of(span_ids, span_order):
    matches = span_ids[:, None] == jnp.arange(span_order.shape[0], dtype=i32)[None, :]
    starts = jnp.sum(jnp.where(matches, span_order[None, :], 0), axis=1) * SPAN
    return (starts[:, None] + jnp.arange(SPAN, dtype=i32)[None, :]).reshape(-1)


def vmem_spec():
    return pl.BlockSpec(memory_space=pltpu.VMEM)


def attend(mine, q, qpos, kpos, kvs, out_weight):
    tok = q.shape[0]
    heads = q.shape[1] // HEAD_SIZE
    kv_heads = kvs[0].shape[1] // (2 * HEAD_SIZE)
    cluster = heads // kv_heads
    rows = cluster * tok
    sub = tok // 4
    width = out_weight.shape[1]
    count = len(kvs)
    slope = math.log2(math.e) / math.sqrt(HEAD_SIZE)

    def kernel(mine_ref, q_ref, qpos_ref, kpos_ref, *refs):
        kv_refs, weight_hbm = refs[:count], refs[count]
        outs = refs[count + 1 : count + 5]
        attended, ordered, weight, sem = refs[count + 5 :]
        fetch = pltpu.make_async_copy(weight_hbm, weight, sem)
        fetch.start()

        @pl.loop(0, kv_heads)
        def _(h):
            def column(i):
                return pl.ds(pl.multiple_of(i * HEAD_SIZE, HEAD_SIZE), HEAD_SIZE)

            q_rows = jnp.concatenate([q_ref[:, column(h * cluster + g)] for g in range(cluster)], axis=0)
            for n, kv in enumerate(kv_refs):
                k = kv[:, column(h)]
                v = kv[:, column(kv_heads + h)]
                s = lax.dot_general(q_rows, k, (((1,), (1,)), ((), ())), preferred_element_type=f32)
                mask = jnp.where(kpos_ref[n : n + 1, :] <= qpos_ref[:, 0:1], 0.0, NEVER)
                s = (s.reshape(cluster, tok, -1) * slope + mask[None]).reshape(rows, -1)
                top = jnp.max(s, axis=1, keepdims=True)
                if n == 0:
                    m = top
                    p = jnp.exp2(s - m)
                    l = jnp.sum(p, axis=1, keepdims=True)
                    acc = jnp.dot(p.astype(bf16), v, preferred_element_type=f32)
                else:
                    new = jnp.maximum(m, top)
                    fade = jnp.exp2(m - new)
                    p = jnp.exp2(s - new)
                    l = l * fade + jnp.sum(p, axis=1, keepdims=True)
                    acc = acc * fade + jnp.dot(p.astype(bf16), v, preferred_element_type=f32)
                    m = new
            result = (acc / l).astype(bf16)
            for g in range(cluster):
                attended[:, column(h * cluster + g)] = result[g * tok : (g + 1) * tok]

        for r in range(4):
            start = pl.multiple_of(lax.rem(mine_ref[0] + r, 4) * sub, sub)
            ordered[r * sub : (r + 1) * sub, :] = attended[pl.ds(start, sub), :]
        fetch.wait()

        @pl.loop(0, 4)
        def _(n):
            at = pl.ds(pl.multiple_of(n * (width // 4), width // 4), width // 4)
            product = jnp.dot(ordered[...], weight[:, at], preferred_element_type=f32)
            for r in range(4):
                outs[r][:, at] = product[r * sub : (r + 1) * sub].astype(outs[r].dtype)

    work = q.shape[0] * q.shape[1] * sum(kv.shape[0] for kv in kvs)
    return pl.pallas_call(
        kernel,
        out_shape=tuple(jax.ShapeDtypeStruct((sub, width), t) for t in (f32, bf16, bf16, bf16)),
        in_specs=[pl.BlockSpec(memory_space=pltpu.SMEM)] + [vmem_spec()] * (count + 3)
        + [pl.BlockSpec(memory_space=pltpu.HBM)],
        out_specs=(vmem_spec(),) * 4,
        scratch_shapes=[
            pltpu.VMEM((tok, q.shape[1]), bf16),
            pltpu.VMEM((tok, q.shape[1]), bf16),
            pltpu.VMEM(out_weight.shape, bf16),
            pltpu.SemaphoreType.DMA,
        ],
        cost_estimate=pl.CostEstimate(
            flops=8 * work, transcendentals=work // HEAD_SIZE, bytes_accessed=4 << 20
        ),
        compiler_params=pltpu.CompilerParams(vmem_limit_bytes=52 << 20),
        name="attend",
    )(mine, q, qpos, kpos, *kvs, out_weight)


def expert_rows(pieces, own, other):
    hid, depth = own[0].shape
    width = own[2].shape[1]
    chunks = 4
    deep, wide = depth // chunks, width // chunks
    sizes = [p.shape[0] for p in pieces]
    rows = sum(sizes)
    count = len(pieces)
    starts = [sum(sizes[:i]) for i in range(count)]

    def kernel(*refs):
        ins, refs = refs[:count], refs[count:]
        (ga, ua, da, gb, ub, db), refs = refs[:6], refs[6:]
        outs, refs = refs[:count], refs[count:]
        x, sums, hidden, out, in_sems, out_sems = refs
        fetches = [
            pltpu.make_async_copy(ref, x.at[pl.ds(start, size), :], in_sems.at[i])
            for i, (ref, start, size) in enumerate(zip(ins, starts, sizes))
        ]
        for copy in fetches:
            copy.start()
        for copy in fetches:
            copy.wait()
        sums[...] = jnp.zeros_like(sums)

        @pl.loop(0, chunks)
        def _(k):
            at = pl.ds(pl.multiple_of(k * deep, deep), deep)
            for i, w in enumerate((ga, ua, gb, ub)):
                sums[i] += lax.dot_general(
                    x[:, at], w[:, at], (((1,), (1,)), ((), ())), preferred_element_type=f32
                )

        for i in range(2):
            hidden[i] = (jax.nn.silu(sums[2 * i]) * sums[2 * i + 1]).astype(bf16)

        def out_copies(n):
            at = pl.ds(pl.multiple_of(n * wide, wide), wide)
            for i, ref in enumerate(outs):
                yield pltpu.make_async_copy(
                    out.at[n, pl.ds(starts[i], sizes[i]), :], ref.at[:, at], out_sems.at[n, i]
                )

        @pl.loop(0, chunks)
        def _(n):
            at = pl.ds(pl.multiple_of(n * wide, wide), wide)
            product = jnp.dot(hidden[0], da[:, at], preferred_element_type=f32)
            out[n] = (product + jnp.dot(hidden[1], db[:, at], preferred_element_type=f32)).astype(bf16)
            for copy in out_copies(n):
                copy.start()

        for n in range(chunks):
            for copy in out_copies(n):
                copy.wait()

    far_away = pl.BlockSpec(memory_space=pltpu.HBM)
    return pl.pallas_call(
        kernel,
        out_shape=tuple(jax.ShapeDtypeStruct((size, width), bf16) for size in sizes),
        in_specs=[far_away] * count + [vmem_spec()] * 6,
        out_specs=(far_away,) * count,
        scratch_shapes=[
            pltpu.VMEM((rows, depth), bf16),
            pltpu.VMEM((4, rows, hid), f32),
            pltpu.VMEM((2, rows, hid), bf16),
            pltpu.VMEM((chunks, rows, wide), bf16),
            pltpu.SemaphoreType.DMA((count,)),
            pltpu.SemaphoreType.DMA((chunks, count)),
        ],
        cost_estimate=pl.CostEstimate(
            flops=12 * rows * depth * hid, transcendentals=2 * rows * hid, bytes_accessed=4 * rows * depth
        ),
        compiler_params=pltpu.CompilerParams(vmem_limit_bytes=18 << 20),
        name="expert_rows",
    )(*pieces, *own, *other)


def layer(
    queries,
    keys,
    values,
    resid_in,
    span_order,
    out_weight,
    norm_gain,
    router,
    expert_ids,
    w_gate,
    w_up,
    w_down,
):
    me = lax.axis_index("ctx")
    mine = lax.axis_index("exp").astype(i32)
    my_z, my_x, my_core = me // 8, (me // 2) % RING, me % 2

    kv = jnp.concatenate((keys, values), axis=1)
    near = join(kv, shift(kv, 1, 1), shift(kv, 1, -1), shift(kv, 1, 2))
    left, right = shift(near, 2, 1), shift(near, 2, -1)
    far = shift(near, 2, 2)

    def block_positions(seconds):
        spans = []
        for second in seconds:
            for core in (my_core, 1 - my_core):
                a = jnp.array([0, -1, 1, 2], i32)
                z = jnp.where(core == 0, my_z + second, my_z + a) % RING
                x = jnp.where(core == 0, my_x + a, my_x + second) % RING
                block = z * 8 + x * 2 + core
                spans.append((block[:, None] * 2 + jnp.arange(2, dtype=i32)[None, :]).reshape(-1))
        return positions_of(jnp.concatenate(spans), span_order).reshape(2 * len(seconds), -1)

    query_pos = positions_of(me * 2 + jnp.arange(2, dtype=i32), span_order)
    query_pos = jnp.broadcast_to(query_pos[:, None], (query_pos.shape[0], HEAD_SIZE))
    near_other, far_other = swap(near), swap(far)
    left_other, right_other = swap(left), swap(right)
    sum0, sum1, sum2, sum3 = attend(
        mine.reshape(1),
        queries,
        query_pos,
        block_positions((0, -1, 1, 2)),
        (near, near_other, left, left_other, right, right_other, far, far_other),
        out_weight,
    )

    sub = resid_in.shape[0]
    back2, back1, back3 = shift_exp(sum2, 2), shift_exp(sum1, 1), shift_exp(sum3, 3)
    own_sum = (sum0 + back2.astype(f32)) + (back1.astype(f32) + back3.astype(f32))
    stream = (resid_in.astype(f32) + own_sum).astype(bf16)
    stream_wide = stream.astype(f32)
    mean_square = jnp.mean(stream_wide * stream_wide, axis=-1, keepdims=True)
    normed = (stream_wide * lax.rsqrt(mean_square + 1e-05) * norm_gain).astype(bf16)
    logits = jnp.dot(normed.astype(f32), router, precision=lax.Precision.HIGHEST)
    experts = router.shape[1]
    expert_axis = (mine + jnp.arange(experts, dtype=i32)) % experts
    picked = expert_ids[:, :, None] == jnp.arange(experts, dtype=i32)[None, None, :]
    chosen = jnp.sum(jnp.where(picked, logits[:, None, :], 0.0), axis=-1)
    mixing = jax.nn.softmax(chosen, axis=-1)
    picked = expert_ids[:, :, None] == expert_axis[None, None, :]
    token_weight = jnp.sum(jnp.where(picked, mixing[:, :, None], 0.0), axis=1)
    routed = jnp.any(picked, axis=1)
    rank_of = jnp.cumsum(routed.astype(i32), axis=0) - 1
    slot_count = sub * expert_ids.shape[1] // experts
    slot_axis = jnp.arange(slot_count, dtype=i32)
    placing = jnp.logical_and(routed.T[:, None, :], rank_of.T[:, None, :] == slot_axis[None, :, None])
    outgoing = jnp.dot(
        placing.reshape(experts * slot_count, sub).astype(bf16), normed, preferred_element_type=f32
    ).astype(bf16)
    o0, o1, o2, o3 = (outgoing[i * slot_count : (i + 1) * slot_count] for i in range(4))
    rows = join(o0, shift_exp(o1, 1), shift_exp(o2, 2), shift_exp(o3, 3))

    own = (w_gate[0].T, w_up[0].T, w_down[0])
    other = tuple(swap(w) for w in own)
    n0 = join(rows, shift(rows, 1, 1))
    n1 = join(shift(rows, 1, -1), shift(rows, 1, 2))
    l0, r0 = shift(n0, 2, 1), shift(n0, 2, -1)
    r1, l1 = shift(n1, 2, -1), shift(n1, 2, 1)
    f0, f1 = shift(l0, 2, 1), shift(r1, 2, -1)

    n0, n1 = expert_rows((n0, n1), own, other)
    l0, r1 = expert_rows((l0, r1), own, other)
    l1, r0 = expert_rows((l1, r0), own, other)
    f0, f1 = expert_rows((f0, f1), own, other)

    u0, v1 = shift(l0, 2, -1), shift(r1, 2, 1)
    u1, v0 = shift(l1, 2, -1), shift(r0, 2, 1)
    f0, f1 = shift(f0, 2, 2), shift(f1, 2, 2)
    n0, n1 = total(n0, u0, v0, f0), total(n1, u1, v1, f1)
    part = rows.shape[0]
    back = (shift(n0[part:], 1, -1), shift(n1[:part], 1, 1), shift(n1[part:], 1, 2))
    own_rows = total(n0[:part], *back)

    r0, r1, r2, r3 = (own_rows[i * slot_count : (i + 1) * slot_count] for i in range(4))
    returned = join(r0, shift_exp(r1, 3), shift_exp(r2, 2), shift_exp(r3, 1))
    coefficient = placing.astype(f32) * token_weight.T[:, None, :]
    combined = jnp.einsum("est,esd->td", coefficient, returned.reshape(experts, slot_count, -1).astype(f32))
    return (stream_wide + combined).astype(bf16)


def solution(mesh):
    placed = (
        P("ctx", "exp"),
        P("ctx", "exp"),
        P("ctx", "exp"),
        P(("ctx", "exp"), None),
        P(),
        P("exp", None),
        P(),
        P(),
        P(("ctx", "exp"), None),
        P("exp", None, "ctx"),
        P("exp", None, "ctx"),
        P("exp", "ctx", None),
    )
    return jax.shard_map(layer, mesh=mesh, in_specs=placed, out_specs=P(("ctx", "exp"), None), check_vma=False)
```

time: 216 us -> 226 us (1.046)
  the two profiles are of different devices: /device:TPU:0 before, /device:TPU:96 now
where the time goes in v2:
time: 226 us
  waiting for transfers between devices  125 us (55%)
  Pallas kernels  45.7 us (20%)
  starting transfers between devices  40.2 us (18%)
  local copies, waits for them, and re-layouts  7.54 us (3%)
  other arithmetic  5.15 us (2%)
    ppermute x24, waiting for transfers between devices, shift(): return lax.ppermute(a, 'ctx', RINGS[phase, step])  102 us
    pallas_call x4, Pallas kernels, expert_rows(): pl.pallas_call(kernel, out_shape=tuple((jax.ShapeDtypeStruct((size, width...  34.5 us
    ppermute x24, starting transfers between devices, shift(): return lax.ppermute(a, 'ctx', RINGS[phase, step])  24.6 us
    ppermute x9, waiting for transfers between devices, shift_exp(): return lax.ppermute(a, 'exp', [(i, (i + step) % 4) for i in range(4)])  21 us
    ppermute x9, starting transfers between devices, shift_exp(): return lax.ppermute(a, 'exp', [(i, (i + step) % 4) for i in range(4)])  14.5 us
    pallas_call x1, Pallas kernels, attend(): pl.pallas_call(kernel, out_shape=tuple((jax.ShapeDtypeStruct((sub, width)...  11.2 us
  transfers between devices with their start and end apart: 40, of which 25 were waited for; matrix products, arithmetic and copies ran while one was open for 3% of the time, Pallas kernels for 15%

profile of v2, /device:TPU:96, one launch (start us, length us, event | category | flops | bytes accessed | tf_op | source)
XLA Modules:
  0.0 225.6 jit_solution(10707952275119713567)
XLA Ops:
  0.0 0.9 constant_dynamic-update-slice_fusion.1
  1.7 3.0 %collective-permute-start.2 = (bf16[128,512]{1,0:T(8,128)(2,1)S(1)}, bf16[128,512]{1,0:T(8,128)(2,1)S(1)}, u32[]{:S(2)}, u32[]{:S(2)}) collective-permute-start(bf16[128,512]{1,0:T(8,128)(2,1)S(1)} %constant_dynamic-update-slice_fusion), channel_id=1, source_target_pairs={{0,16},{4,68},{8,24},{12,76},{16,0},{20,84},{24,8},{28,92},{32,48}... | collective-permute-start | bytes 393224 | tf_op jit(solution)/shard_map/ppermute | solution.py:40
  4.7 1.1 collective-permute-start.1
  5.9 0.9 collective-permute-start
  9.7 2.4 %collective-permute-done = bf16[128,512]{1,0:T(8,128)(2,1)S(1)} collective-permute-done((bf16[128,512]{1,0:T(8,128)(2,1)S(1)}, bf16[128,512]{1,0:T(8,128)(2,1)S(1)}, u32[]{:S(2)}, u32[]{:S(2)}) %collective-permute-start) | collective-permute-done | bytes 131104 | tf_op jit(solution)/shard_map/ppermute | solution.py:40
  12.8 3.2 %collective-permute-start.4 = (bf16[512,512]{1,0:T(8,128)(2,1)S(1)}, bf16[512,512]{1,0:T(8,128)(2,1)S(1)}, u32[]{:S(2)}, u32[]{:S(2)}) collective-permute-start(bf16[512,512]{1,0:T(8,128)(2,1)S(1)} %pad_maximum_fusion.refs_0_), channel_id=1, source_target_pairs={{0,32},{4,12},{8,40},{12,20},{16,48},{20,28},{24,56},{28,4},{32,64... | collective-permute-start | bytes 1572872 | tf_op jit(solution)/shard_map/ppermute | solution.py:40
  17.5 5.5 %collective-permute-done.8.refs_6_ = bf16[512,512]{1,0:T(8,128)(2,1)S(1)} collective-permute-done((bf16[512,512]{1,0:T(8,128)(2,1)S(1)}, bf16[512,512]{1,0:T(8,128)(2,1)S(1)}, u32[]{:S(2)}, u32[]{:S(2)}) %collective-permute-start.8) | collective-permute-done | bytes 524320 | tf_op jit(solution)/shard_map/ppermute | solution.py:40
  23.0 5.5 %collective-permute-done.6.refs_4_ = bf16[512,512]{1,0:T(8,128)(2,1)S(1)} collective-permute-done((bf16[512,512]{1,0:T(8,128)(2,1)S(1)}, bf16[512,512]{1,0:T(8,128)(2,1)S(1)}, u32[]{:S(2)}, u32[]{:S(2)}) %collective-permute-start.6) | collective-permute-done | bytes 524320 | tf_op jit(solution)/shard_map/ppermute | solution.py:40
  29.3 1.2 collective-permute-done.7.refs_5_
  31.4 0.9 copy-done.5
  32.4 11.2 %attend.1 = (f32[32,4096]{1,0:T(8,128)S(1)}, bf16[32,4096]{1,0:T(8,128)(2,1)S(1)}, bf16[32,4096]{1,0:T(8,128)(2,1)S(1)}, bf16[32,4096]{1,0:T(8,128)(2,1)S(1)}) custom-call(s32[1]{0:T(128)} %bitcast.mine_ref, bf16[128,1024]{1,0:T(8,128)(2,1)S(1)} %copy-done.5, s32[128,128]{1,0:T(8,128)S(1)} %broadcast_in_dim.125.qpos_ref, ...), custom_call_target="tpu_custom_call" | custom-call | flops 4294967296 | bytes 4194304 | tf_op jit(solution)/shard_map/attend/pallas_call | solution.py:129
  43.5 3.3 %collective-permute-start.10 = (bf16[32,4096]{1,0:T(8,128)(2,1)S(1)}, bf16[32,4096]{1,0:T(8,128)(2,1)S(1)}, u32[]{:S(2)}, u32[]{:S(2)}) collective-permute-start(bf16[32,4096]{1,0:T(8,128)(2,1)S(1)} %get-tuple-element.18), channel_id=1, source_target_pairs={{0,2},{1,3},{2,0},{3,1},{4,6},{5,7},{6,4},{7,5},{8,10},{9,11},{10,... | collective-permute-start | bytes 786440 | tf_op jit(solution)/shard_map/ppermute | solution.py:48
  47.5 2.6 %collective-permute-start.12 = (bf16[32,4096]{1,0:T(8,128)(2,1)S(1)}, bf16[32,4096]{1,0:T(8,128)(2,1)S(1)}, u32[]{:S(2)}, u32[]{:S(2)}) collective-permute-start(bf16[32,4096]{1,0:T(8,128)(2,1)S(1)} %get-tuple-element.20), channel_id=1, source_target_pairs={{0,3},{1,0},{2,1},{3,2},{4,7},{5,4},{6,5},{7,6},{8,11},{9,8},{10,9... | collective-permute-start | bytes 786440 | tf_op jit(solution)/shard_map/ppermute | solution.py:48
  50.5 3.8 %collective-permute-done.10 = bf16[32,4096]{1,0:T(8,128)(2,1)S(1)} collective-permute-done((bf16[32,4096]{1,0:T(8,128)(2,1)S(1)}, bf16[32,4096]{1,0:T(8,128)(2,1)S(1)}, u32[]{:S(2)}, u32[]{:S(2)}) %collective-permute-start.10) | collective-permute-done | bytes 262176 | tf_op jit(solution)/shard_map/ppermute | solution.py:48
  54.3 4.7 %collective-permute-done.11 = bf16[32,4096]{1,0:T(8,128)(2,1)S(1)} collective-permute-done((bf16[32,4096]{1,0:T(8,128)(2,1)S(1)}, bf16[32,4096]{1,0:T(8,128)(2,1)S(1)}, u32[]{:S(2)}, u32[]{:S(2)}) %collective-permute-start.11) | collective-permute-done | bytes 262176 | tf_op jit(solution)/shard_map/ppermute | solution.py:48
  60.2 2.7 %collective-permute-start.15 = (bf16[16,4096]{1,0:T(8,128)(2,1)S(1)}, bf16[16,4096]{1,0:T(8,128)(2,1)S(1)}, u32[]{:S(2)}, u32[]{:S(2)}) collective-permute-start(bf16[16,4096]{1,0:T(8,128)(2,1)S(1)} %get-tuple-element.39), channel_id=1, source_target_pairs={{0,3},{1,0},{2,1},{3,2},{4,7},{5,4},{6,5},{7,6},{8,11},{9,8},{10,9... | collective-permute-start | bytes 393224 | tf_op jit(solution)/shard_map/ppermute | solution.py:48
  64.4 4.3 %collective-permute-done.15 = bf16[16,4096]{1,0:T(8,128)(2,1)S(1)} collective-permute-done((bf16[16,4096]{1,0:T(8,128)(2,1)S(1)}, bf16[16,4096]{1,0:T(8,128)(2,1)S(1)}, u32[]{:S(2)}, u32[]{:S(2)}) %collective-permute-start.15) | collective-permute-done | bytes 131104 | tf_op jit(solution)/shard_map/ppermute | solution.py:48
  68.6 2.1 collective-permute-done.14
  70.8 1.6 collective-permute-done.13
  72.8 1.7 collective-permute-start.16
  74.5 8.6 %collective-permute-done.16 = bf16[64,4096]{1,0:T(8,128)(2,1)S(1)} collective-permute-done((bf16[64,4096]{1,0:T(8,128)(2,1)S(1)}, bf16[64,4096]{1,0:T(8,128)(2,1)S(1)}, u32[]{:S(2)}, u32[]{:S(2)}) %collective-permute-start.16) | collective-permute-done | bytes 524320 | tf_op jit(solution)/shard_map/ppermute | solution.py:40
  84.5 15.0 %collective-permute-done.18 = bf16[64,4096]{1,0:T(8,128)(2,1)S(1)} collective-permute-done((bf16[64,4096]{1,0:T(8,128)(2,1)S(1)}, bf16[64,4096]{1,0:T(8,128)(2,1)S(1)}, u32[]{:S(2)}, u32[]{:S(2)}) %collective-permute-start.18) | collective-permute-done | bytes 524320 | tf_op jit(solution)/shard_map/ppermute | solution.py:40
  99.6 3.4 %collective-permute-done.22.refs_0_ = bf16[128,4096]{1,0:T(8,128)(2,1)S(1)} collective-permute-done((bf16[128,4096]{1,0:T(8,128)(2,1)S(1)}, bf16[128,4096]{1,0:T(8,128)(2,1)S(1)}, u32[]{:S(2)}, u32[]{:S(2)}) %collective-permute-start.22) | collective-permute-done | bytes 1048608 | tf_op jit(solution)/shard_map/ppermute | solution.py:40
  103.2 12.3 %collective-permute-done.23.refs_1_ = bf16[128,4096]{1,0:T(8,128)(2,1)S(1)} collective-permute-done((bf16[128,4096]{1,0:T(8,128)(2,1)S(1)}, bf16[128,4096]{1,0:T(8,128)(2,1)S(1)}, u32[]{:S(2)}, u32[]{:S(2)}) %collective-permute-start.23) | collective-permute-done | bytes 1048608 | tf_op jit(solution)/shard_map/ppermute | solution.py:40
  115.6 2.1 collective-permute-start.29
  117.7 2.0 copy-done.3
  119.7 8.6 %expert_rows.5 = (bf16[128,4096]{1,0:T(8,128)(2,1)S(1)}, bf16[128,4096]{1,0:T(8,128)(2,1)S(1)}) custom-call(bf16[128,4096]{1,0:T(8,128)(2,1)S(1)} %collective-permute-done.22.refs_0_, bf16[128,4096]{1,0:T(8,128)(2,1)S(1)} %collective-permute-done.23.refs_1_, bf16[448,4096]{1,0:T(8,128)(2,1)S(1)} %bitcast.29, bf16[448,4096]{1,0:T(8,128)(2,1)S(1)} %bitcast.34, ...), custom_call_target="tpu_custom_call" | custom-call | flops 5637144576 | bytes 4194304 | tf_op jit(solution)/shard_map/expert_rows/pallas_call | solution.py:205
  128.4 2.0 collective-permute-start.24
  130.4 8.6 %expert_rows.6 = (bf16[128,4096]{1,0:T(8,128)(2,1)S(1)}, bf16[128,4096]{1,0:T(8,128)(2,1)S(1)}) custom-call(bf16[128,4096]{1,0:T(8,128)(2,1)S(1)} %collective-permute-done.25.refs_0_, bf16[128,4096]{1,0:T(8,128)(2,1)S(1)} %collective-permute-done.26.refs_1_, bf16[448,4096]{1,0:T(8,128)(2,1)S(1)} %bitcast.30, bf16[448,4096]{1,0:T(8,128)(2,1)S(1)} %bitcast.35, ...), custom_call_target="tpu_custom_call" | custom-call | flops 5637144576 | bytes 4194304 | tf_op jit(solution)/shard_map/expert_rows/pallas_call | solution.py:205
  139.1 1.3 collective-permute-start.27
  140.4 1.2 collective-permute-done.28.refs_0_
  141.6 8.6 %expert_rows.7 = (bf16[128,4096]{1,0:T(8,128)(2,1)S(1)}, bf16[128,4096]{1,0:T(8,128)(2,1)S(1)}) custom-call(bf16[128,4096]{1,0:T(8,128)(2,1)S(1)} %collective-permute-done.28.refs_0_, bf16[128,4096]{1,0:T(8,128)(2,1)S(1)} %collective-permute-done.29.refs_1_, bf16[448,4096]{1,0:T(8,128)(2,1)S(1)} %bitcast.31, bf16[448,4096]{1,0:T(8,128)(2,1)S(1)} %bitcast.36, ...), custom_call_target="tpu_custom_call" | custom-call | flops 5637144576 | bytes 4194304 | tf_op jit(solution)/shard_map/expert_rows/pallas_call | solution.py:205
  150.4 2.2 collective-permute-start.33
  152.6 3.3 %collective-permute-start.34 = (bf16[128,4096]{1,0:T(8,128)(2,1)S(1)}, bf16[128,4096]{1,0:T(8,128)(2,1)S(1)}, u32[]{:S(2)}, u32[]{:S(2)}) collective-permute-start(bf16[128,4096]{1,0:T(8,128)(2,1)S(1)} %get-tuple-element.28), channel_id=1, source_target_pairs={{0,64},{4,20},{8,72},{12,28},{16,80},{20,4},{24,88},{28,12},{32,96... | collective-permute-start | bytes 3145736 | tf_op jit(solution)/shard_map/ppermute | solution.py:40
  155.9 8.6 %expert_rows.4 = (bf16[128,4096]{1,0:T(8,128)(2,1)S(1)}, bf16[128,4096]{1,0:T(8,128)(2,1)S(1)}) custom-call(bf16[128,4096]{1,0:T(8,128)(2,1)S(1)} %constant_dynamic-update-slice_fusion.2.refs_0_, bf16[128,4096]{1,0:T(8,128)(2,1)S(1)} %constant_dynamic-update-slice_fusion.7.refs_1_, bf16[448,4096]{1,0:T(8,128)(2,1)S(1)} %bitcast.32, ...), custom_call_target="tpu_custom_call" | custom-call | flops 5637144576 | bytes 4194304 | tf_op jit(solution)/shard_map/expert_rows/pallas_call | solution.py:205
  164.6 2.5 %collective-permute-done.30 = bf16[128,4096]{1,0:T(8,128)(2,1)S(1)} collective-permute-done((bf16[128,4096]{1,0:T(8,128)(2,1)S(1)}, bf16[128,4096]{1,0:T(8,128)(2,1)S(1)}, u32[]{:S(2)}, u32[]{:S(2)}) %collective-permute-start.30) | collective-permute-done | bytes 1048608 | tf_op jit(solution)/shard_map/ppermute | solution.py:40
  167.9 8.6 %collective-permute-done.33 = bf16[128,4096]{1,0:T(8,128)(2,1)S(1)} collective-permute-done((bf16[128,4096]{1,0:T(8,128)(2,1)S(1)}, bf16[128,4096]{1,0:T(8,128)(2,1)S(1)}, u32[]{:S(2)}, u32[]{:S(2)}) %collective-permute-start.33) | collective-permute-done | bytes 1048608 | tf_op jit(solution)/shard_map/ppermute | solution.py:40
  176.5 7.0 %collective-permute-done.32 = bf16[128,4096]{1,0:T(8,128)(2,1)S(1)} collective-permute-done((bf16[128,4096]{1,0:T(8,128)(2,1)S(1)}, bf16[128,4096]{1,0:T(8,128)(2,1)S(1)}, u32[]{:S(2)}, u32[]{:S(2)}) %collective-permute-start.32) | collective-permute-done | bytes 1048608 | tf_op jit(solution)/shard_map/ppermute | solution.py:40
  183.5 14.3 %collective-permute-done.34 = bf16[128,4096]{1,0:T(8,128)(2,1)S(1)} collective-permute-done((bf16[128,4096]{1,0:T(8,128)(2,1)S(1)}, bf16[128,4096]{1,0:T(8,128)(2,1)S(1)}, u32[]{:S(2)}, u32[]{:S(2)}) %collective-permute-start.34) | collective-permute-done | bytes 1048608 | tf_op jit(solution)/shard_map/ppermute | solution.py:40
  198.5 1.1 fusion.78
  200.9 14.9 %collective-permute-done.35 = bf16[64,4096]{1,0:T(8,128)(2,1)S(1)} collective-permute-done((bf16[64,4096]{1,0:T(8,128)(2,1)}, bf16[64,4096]{1,0:T(8,128)(2,1)S(1)}, u32[]{:S(2)}, u32[]{:S(2)}) %collective-permute-start.35) | collective-permute-done | bytes 524320 | tf_op jit(solution)/shard_map/ppermute | solution.py:40
  216.1 1.2 collective-permute-start.39
  217.3 1.1 collective-permute-start.38
  218.3 2.1 collective-permute-start.37
  220.5 1.8 collective-permute-done.39
  222.4 1.4 collective-permute-done.38
  223.8 0.9 collective-permute-done.37
  224.7 1.0 fusion.1
  (129 shorter events, 16.7 us)
Async XLA Ops:
  0.0 200.4 %copy-start = (f32[4096,4]{0,1:T(4,128)S(1)}, f32[4096,4]{0,1:T(4,128)}, u32[]{:S(2)}) copy-start(f32[4096,4]{0,1:T(4,128)} %param.27) | copy-start | bytes 196612
  1.7 7.3 %collective-permute-start.2 = (bf16[128,512]{1,0:T(8,128)(2,1)S(1)}, bf16[128,512]{1,0:T(8,128)(2,1)S(1)}, u32[]{:S(2)}, u32[]{:S(2)}) collective-permute-start(bf16[128,512]{1,0:T(8,128)(2,1)S(1)} %constant_dynamic-update-slice_fusion), channel_id=1, source_target_pairs={{0,16},{4,68},{8,24},{12,76},{16,0},{20,84},{24,8},{28,92},{32,48}... | collective-permute-start | bytes 393224 | tf_op jit(solution)/shard_map/ppermute | solution.py:40
  4.7 5.0 %collective-permute-start.1 = (bf16[128,512]{1,0:T(8,128)(2,1)S(1)}, bf16[128,512]{1,0:T(8,128)(2,1)S(1)}, u32[]{:S(2)}, u32[]{:S(2)}) collective-permute-start(bf16[128,512]{1,0:T(8,128)(2,1)S(1)} %constant_dynamic-update-slice_fusion), channel_id=1, source_target_pairs={{0,24},{4,100},{8,0},{12,108},{16,8},{20,116},{24,16},{28,124},{32... | collective-permute-start | bytes 393224 | tf_op jit(solution)/shard_map/ppermute | solution.py:40
  5.9 6.2 %collective-permute-start = (bf16[128,512]{1,0:T(8,128)(2,1)S(1)}, bf16[128,512]{1,0:T(8,128)(2,1)S(1)}, u32[]{:S(2)}, u32[]{:S(2)}) collective-permute-start(bf16[128,512]{1,0:T(8,128)(2,1)S(1)} %constant_dynamic-update-slice_fusion), channel_id=1, source_target_pairs={{0,8},{4,36},{8,16},{12,44},{16,24},{20,52},{24,0},{28,60},{32,40}... | collective-permute-start | bytes 393224 | tf_op jit(solution)/shard_map/ppermute | solution.py:40
  12.1 19.3 %copy-start.6 = (bf16[512,512]{1,0:T(8,128)(2,1)}, bf16[512,512]{1,0:T(8,128)(2,1)S(1)}, u32[]{:S(2)}) copy-start(bf16[512,512]{1,0:T(8,128)(2,1)S(1)} %pad_maximum_fusion.refs_0_) | copy-start | bytes 1572868
  12.1 10.9 %collective-permute-start.8 = (bf16[512,512]{1,0:T(8,128)(2,1)S(1)}, bf16[512,512]{1,0:T(8,128)(2,1)S(1)}, u32[]{:S(2)}, u32[]{:S(2)}) collective-permute-start(bf16[512,512]{1,0:T(8,128)(2,1)S(1)} %pad_maximum_fusion.refs_0_), channel_id=1, source_target_pairs={{0,64},{4,20},{8,72},{12,28},{16,80},{20,4},{24,88},{28,12},{32,96... | collective-permute-start | bytes 1572872 | tf_op jit(solution)/shard_map/ppermute | solution.py:40
  12.7 15.8 %collective-permute-start.6 = (bf16[512,512]{1,0:T(8,128)(2,1)S(1)}, bf16[512,512]{1,0:T(8,128)(2,1)S(1)}, u32[]{:S(2)}, u32[]{:S(2)}) collective-permute-start(bf16[512,512]{1,0:T(8,128)(2,1)S(1)} %pad_maximum_fusion.refs_0_), channel_id=1, source_target_pairs={{0,96},{4,28},{8,104},{12,4},{16,112},{20,12},{24,120},{28,20},{32... | collective-permute-start | bytes 1572872 | tf_op jit(solution)/shard_map/ppermute | solution.py:40
  12.8 15.8 %collective-permute-start.4 = (bf16[512,512]{1,0:T(8,128)(2,1)S(1)}, bf16[512,512]{1,0:T(8,128)(2,1)S(1)}, u32[]{:S(2)}, u32[]{:S(2)}) collective-permute-start(bf16[512,512]{1,0:T(8,128)(2,1)S(1)} %pad_maximum_fusion.refs_0_), channel_id=1, source_target_pairs={{0,32},{4,12},{8,40},{12,20},{16,48},{20,28},{24,56},{28,4},{32,64... | collective-permute-start | bytes 1572872 | tf_op jit(solution)/shard_map/ppermute | solution.py:40
  17.4 11.9 %collective-permute-start.3 = (bf16[512,512]{1,0:T(8,128)(2,1)S(1)}, bf16[512,512]{1,0:T(8,128)(2,1)}, u32[]{:S(2)}, u32[]{:S(2)}) collective-permute-start(bf16[512,512]{1,0:T(8,128)(2,1)S(1)} %pad_maximum_fusion.refs_0_), channel_id=1, source_target_pairs={{0,4},{4,0},{8,12},{12,8},{16,20},{20,16},{24,28},{28,24},{32,36},... | collective-permute-start | bytes 1572872 | tf_op jit(solution)/shard_map/ppermute | solution.py:44
  23.0 6.3 %collective-permute-start.9 = (bf16[512,512]{1,0:T(8,128)(2,1)S(1)}, bf16[512,512]{1,0:T(8,128)(2,1)}, u32[]{:S(2)}, u32[]{:S(2)}) collective-permute-start(bf16[512,512]{1,0:T(8,128)(2,1)S(1)} %collective-permute-done.8.refs_6_), channel_id=1, source_target_pairs={{0,4},{4,0},{8,12},{12,8},{16,20},{20,16},{24,28},{28,24},{32,36},... | collective-permute-start | bytes 1572872 | tf_op jit(solution)/shard_map/ppermute | solution.py:44
  28.5 2.0 collective-permute-start.7
  28.5 2.8 %collective-permute-start.5 = (bf16[512,512]{1,0:T(8,128)(2,1)S(1)}, bf16[512,512]{1,0:T(8,128)(2,1)}, u32[]{:S(2)}, u32[]{:S(2)}) collective-permute-start(bf16[512,512]{1,0:T(8,128)(2,1)S(1)} %collective-permute-done.4.refs_2_), channel_id=1, source_target_pairs={{0,4},{4,0},{8,12},{12,8},{16,20},{20,16},{24,28},{28,24},{32,36},... | collective-permute-start | bytes 1572872 | tf_op jit(solution)/shard_map/ppermute | solution.py:44
  32.4 17.7 %copy-start.9 = (s32[32,2]{0,1:T(2,128)S(1)}, s32[32,2]{0,1:T(2,128)}, u32[]{:S(2)}) copy-start(s32[32,2]{0,1:T(2,128)} %param.28) | copy-start | bytes 772
  32.4 27.1 %copy-start.7 = (bf16[32,4096]{1,0:T(8,128)(2,1)S(1)}, bf16[32,4096]{1,0:T(8,128)(2,1)}, u32[]{:S(2)}) copy-start(bf16[32,4096]{1,0:T(8,128)(2,1)} %param.23) | copy-start | bytes 786436
  32.4 27.4 %copy-start.8 = (f32[4096]{0:T(1024)S(1)}, f32[4096]{0:T(1024)}, u32[]{:S(2)}) copy-start(f32[4096]{0:T(1024)} %param.26) | copy-start | bytes 49156
  43.5 10.8 %collective-permute-start.10 = (bf16[32,4096]{1,0:T(8,128)(2,1)S(1)}, bf16[32,4096]{1,0:T(8,128)(2,1)S(1)}, u32[]{:S(2)}, u32[]{:S(2)}) collective-permute-start(bf16[32,4096]{1,0:T(8,128)(2,1)S(1)} %get-tuple-element.18), channel_id=1, source_target_pairs={{0,2},{1,3},{2,0},{3,1},{4,6},{5,7},{6,4},{7,5},{8,10},{9,11},{10,... | collective-permute-start | bytes 786440 | tf_op jit(solution)/shard_map/ppermute | solution.py:48
  46.8 12.3 %collective-permute-start.11 = (bf16[32,4096]{1,0:T(8,128)(2,1)S(1)}, bf16[32,4096]{1,0:T(8,128)(2,1)S(1)}, u32[]{:S(2)}, u32[]{:S(2)}) collective-permute-start(bf16[32,4096]{1,0:T(8,128)(2,1)S(1)} %get-tuple-element.19), channel_id=1, source_target_pairs={{0,1},{1,2},{2,3},{3,0},{4,5},{5,6},{6,7},{7,4},{8,9},{9,10},{10,1... | collective-permute-start | bytes 786440 | tf_op jit(solution)/shard_map/ppermute | solution.py:48
  47.5 12.0 %collective-permute-start.12 = (bf16[32,4096]{1,0:T(8,128)(2,1)S(1)}, bf16[32,4096]{1,0:T(8,128)(2,1)S(1)}, u32[]{:S(2)}, u32[]{:S(2)}) collective-permute-start(bf16[32,4096]{1,0:T(8,128)(2,1)S(1)} %get-tuple-element.20), channel_id=1, source_target_pairs={{0,3},{1,0},{2,1},{3,2},{4,7},{5,4},{6,5},{7,6},{8,11},{9,8},{10,9... | collective-permute-start | bytes 786440 | tf_op jit(solution)/shard_map/ppermute | solution.py:48
  50.4 13.4 %copy-start.1 = (bf16[1,4096,448]{1,2,0:T(8,128)(2,1)S(1)}, bf16[1,4096,448]{1,2,0:T(8,128)(2,1)}, u32[]{:S(2)}) copy-start(bf16[1,4096,448]{1,2,0:T(8,128)(2,1)} %param.29) | copy-start | bytes 11010052
  60.2 8.4 %collective-permute-start.15 = (bf16[16,4096]{1,0:T(8,128)(2,1)S(1)}, bf16[16,4096]{1,0:T(8,128)(2,1)S(1)}, u32[]{:S(2)}, u32[]{:S(2)}) collective-permute-start(bf16[16,4096]{1,0:T(8,128)(2,1)S(1)} %get-tuple-element.39), channel_id=1, source_target_pairs={{0,3},{1,0},{2,1},{3,2},{4,7},{5,4},{6,5},{7,6},{8,11},{9,8},{10,9... | collective-permute-start | bytes 393224 | tf_op jit(solution)/shard_map/ppermute | solution.py:48
  62.9 7.9 %collective-permute-start.14 = (bf16[16,4096]{1,0:T(8,128)(2,1)S(1)}, bf16[16,4096]{1,0:T(8,128)(2,1)S(1)}, u32[]{:S(2)}, u32[]{:S(2)}) collective-permute-start(bf16[16,4096]{1,0:T(8,128)(2,1)S(1)} %get-tuple-element.40), channel_id=1, source_target_pairs={{0,2},{1,3},{2,0},{3,1},{4,6},{5,7},{6,4},{7,5},{8,10},{9,11},{10,... | collective-permute-start | bytes 393224 | tf_op jit(solution)/shard_map/ppermute | solution.py:48
  63.7 8.7 %collective-permute-start.13 = (bf16[16,4096]{1,0:T(8,128)(2,1)S(1)}, bf16[16,4096]{1,0:T(8,128)(2,1)S(1)}, u32[]{:S(2)}, u32[]{:S(2)}) collective-permute-start(bf16[16,4096]{1,0:T(8,128)(2,1)S(1)} %get-tuple-element.41), channel_id=1, source_target_pairs={{0,1},{1,2},{2,3},{3,0},{4,5},{5,6},{6,7},{7,4},{8,9},{9,10},{10,1... | collective-permute-start | bytes 393224 | tf_op jit(solution)/shard_map/ppermute | solution.py:48
  63.8 51.7 %collective-permute-start.19 = (bf16[448,4096]{1,0:T(8,128)(2,1)S(1)}, bf16[448,4096]{1,0:T(8,128)(2,1)S(1)}, u32[]{:S(2)}, u32[]{:S(2)}) collective-permute-start(bf16[448,4096]{1,0:T(8,128)(2,1)S(1)} %bitcast.28), channel_id=1, source_target_pairs={{0,4},{4,0},{8,12},{12,8},{16,20},{20,16},{24,28},{28,24},{32,36},... | collective-permute-start | bytes 11010056 | tf_op jit(solution)/shard_map/ppermute | solution.py:44
  63.8 51.7 %collective-permute-start.20 = (bf16[448,4096]{1,0:T(8,128)(2,1)}, bf16[448,4096]{1,0:T(8,128)(2,1)S(1)}, u32[]{:S(2)}, u32[]{:S(2)}) collective-permute-start(bf16[448,4096]{1,0:T(8,128)(2,1)} %bitcast.33), channel_id=1, source_target_pairs={{0,4},{4,0},{8,12},{12,8},{16,20},{20,16},{24,28},{28,24},{32,36},... | collective-permute-start | bytes 11010056 | tf_op jit(solution)/shard_map/ppermute | solution.py:44
  68.6 49.1 %collective-permute-start.21 = (bf16[448,4096]{1,0:T(8,128)(2,1)}, bf16[448,4096]{1,0:T(8,128)(2,1)S(1)}, u32[]{:S(2)}, u32[]{:S(2)}) collective-permute-start(bf16[448,4096]{1,0:T(8,128)(2,1)} %bitcast.38), channel_id=1, source_target_pairs={{0,4},{4,0},{8,12},{12,8},{16,20},{20,16},{24,28},{28,24},{32,36},... | collective-permute-start | bytes 11010056 | tf_op jit(solution)/shard_map/ppermute | solution.py:44
  72.4 45.3 %copy-start.2 = (bf16[1,4096,448]{1,2,0:T(8,128)(2,1)S(1)}, bf16[1,4096,448]{1,2,0:T(8,128)(2,1)}, u32[]{:S(2)}) copy-start(bf16[1,4096,448]{1,2,0:T(8,128)(2,1)} %param.30) | copy-start | bytes 11010052
  72.4 11.4 %collective-permute-start.17 = (bf16[64,4096]{1,0:T(8,128)(2,1)S(1)}, bf16[64,4096]{1,0:T(8,128)(2,1)S(1)}, u32[]{:S(2)}, u32[]{:S(2)}) collective-permute-start(bf16[64,4096]{1,0:T(8,128)(2,1)S(1)} %pad_maximum_fusion.1), channel_id=1, source_target_pairs={{0,24},{4,100},{8,0},{12,108},{16,8},{20,116},{24,16},{28,124},{32... | collective-permute-start | bytes 1572872 | tf_op jit(solution)/shard_map/ppermute | solution.py:40
  72.8 10.4 %collective-permute-start.16 = (bf16[64,4096]{1,0:T(8,128)(2,1)S(1)}, bf16[64,4096]{1,0:T(8,128)(2,1)S(1)}, u32[]{:S(2)}, u32[]{:S(2)}) collective-permute-start(bf16[64,4096]{1,0:T(8,128)(2,1)S(1)} %pad_maximum_fusion.1), channel_id=1, source_target_pairs={{0,8},{4,36},{8,16},{12,44},{16,24},{20,52},{24,0},{28,60},{32,40}... | collective-permute-start | bytes 1572872 | tf_op jit(solution)/shard_map/ppermute | solution.py:40
  83.2 16.3 %collective-permute-start.18 = (bf16[64,4096]{1,0:T(8,128)(2,1)S(1)}, bf16[64,4096]{1,0:T(8,128)(2,1)S(1)}, u32[]{:S(2)}, u32[]{:S(2)}) collective-permute-start(bf16[64,4096]{1,0:T(8,128)(2,1)S(1)} %pad_maximum_fusion.1), channel_id=1, source_target_pairs={{0,16},{4,68},{8,24},{12,76},{16,0},{20,84},{24,8},{28,92},{32,48}... | collective-permute-start | bytes 1572872 | tf_op jit(solution)/shard_map/ppermute | solution.py:40
  83.8 19.2 %collective-permute-start.22 = (bf16[128,4096]{1,0:T(8,128)(2,1)S(1)}, bf16[128,4096]{1,0:T(8,128)(2,1)S(1)}, u32[]{:S(2)}, u32[]{:S(2)}) collective-permute-start(bf16[128,4096]{1,0:T(8,128)(2,1)S(1)} %constant_dynamic-update-slice_fusion.2.refs_0_), channel_id=1, source_target_pairs={{0,32},{4,12},{8,40},{12,20},{16,48},{20,28},{24,56},{28,4},{32,64... | collective-permute-start | bytes 3145736 | tf_op jit(solution)/shard_map/ppermute | solution.py:40
  99.5 16.1 %collective-permute-start.23 = (bf16[128,4096]{1,0:T(8,128)(2,1)S(1)}, bf16[128,4096]{1,0:T(8,128)(2,1)S(1)}, u32[]{:S(2)}, u32[]{:S(2)}) collective-permute-start(bf16[128,4096]{1,0:T(8,128)(2,1)S(1)} %constant_dynamic-update-slice_fusion.7.refs_1_), channel_id=1, source_target_pairs={{0,96},{4,28},{8,104},{12,4},{16,112},{20,12},{24,120},{28,20},{32... | collective-permute-start | bytes 3145736 | tf_op jit(solution)/shard_map/ppermute | solution.py:40
  103.0 27.5 %collective-permute-start.26 = (bf16[128,4096]{1,0:T(8,128)(2,1)S(1)}, bf16[128,4096]{1,0:T(8,128)(2,1)S(1)}, u32[]{:S(2)}, u32[]{:S(2)}) collective-permute-start(bf16[128,4096]{1,0:T(8,128)(2,1)S(1)} %constant_dynamic-update-slice_fusion.2.refs_0_), channel_id=1, source_target_pairs={{0,96},{4,28},{8,104},{12,4},{16,112},{20,12},{24,120},{28,20},{32... | collective-permute-start | bytes 3145736 | tf_op jit(solution)/shard_map/ppermute | solution.py:40
  115.6 14.8 %collective-permute-start.25 = (bf16[128,4096]{1,0:T(8,128)(2,1)S(1)}, bf16[128,4096]{1,0:T(8,128)(2,1)S(1)}, u32[]{:S(2)}, u32[]{:S(2)}) collective-permute-start(bf16[128,4096]{1,0:T(8,128)(2,1)S(1)} %constant_dynamic-update-slice_fusion.7.refs_1_), channel_id=1, source_target_pairs={{0,32},{4,12},{8,40},{12,20},{16,48},{20,28},{24,56},{28,4},{32,64... | collective-permute-start | bytes 3145736 | tf_op jit(solution)/shard_map/ppermute | solution.py:40
  115.6 26.0 %collective-permute-start.28 = (bf16[128,4096]{1,0:T(8,128)(2,1)S(1)}, bf16[128,4096]{1,0:T(8,128)(2,1)S(1)}, u32[]{:S(2)}, u32[]{:S(2)}) collective-permute-start(bf16[128,4096]{1,0:T(8,128)(2,1)S(1)} %collective-permute-done.22.refs_0_), channel_id=1, source_target_pairs={{0,32},{4,12},{8,40},{12,20},{16,48},{20,28},{24,56},{28,4},{32,64... | collective-permute-start | bytes 3145736 | tf_op jit(solution)/shard_map/ppermute | solution.py:40
  115.6 26.0 %collective-permute-start.29 = (bf16[128,4096]{1,0:T(8,128)(2,1)S(1)}, bf16[128,4096]{1,0:T(8,128)(2,1)S(1)}, u32[]{:S(2)}, u32[]{:S(2)}) collective-permute-start(bf16[128,4096]{1,0:T(8,128)(2,1)S(1)} %collective-permute-done.23.refs_1_), channel_id=1, source_target_pairs={{0,96},{4,28},{8,104},{12,4},{16,112},{20,12},{24,120},{28,20},{32... | collective-permute-start | bytes 3145736 | tf_op jit(solution)/shard_map/ppermute | solution.py:40
  128.4 24.2 %collective-permute-start.24 = (bf16[128,4096]{1,0:T(8,128)(2,1)S(1)}, bf16[128,4096]{1,0:T(8,128)(2,1)S(1)}, u32[]{:S(2)}, u32[]{:S(2)}) collective-permute-start(bf16[128,4096]{1,0:T(8,128)(2,1)S(1)} %get-tuple-element.22), channel_id=1, source_target_pairs={{0,96},{4,28},{8,104},{12,4},{16,112},{20,12},{24,120},{28,20},{32... | collective-permute-start | bytes 3145736 | tf_op jit(solution)/shard_map/ppermute | solution.py:40
  130.4 11.2 %copy-start.4 = (bf16[1,448,4096]{2,1,0:T(8,128)(2,1)S(1)}, bf16[1,448,4096]{2,1,0:T(8,128)(2,1)}, u32[]{:S(2)}) copy-start(bf16[1,448,4096]{2,1,0:T(8,128)(2,1)} %param.31) | copy-start | bytes 11010052
  139.1 25.5 %collective-permute-start.27 = (bf16[128,4096]{1,0:T(8,128)(2,1)S(1)}, bf16[128,4096]{1,0:T(8,128)(2,1)S(1)}, u32[]{:S(2)}, u32[]{:S(2)}) collective-permute-start(bf16[128,4096]{1,0:T(8,128)(2,1)S(1)} %get-tuple-element.23), channel_id=1, source_target_pairs={{0,32},{4,12},{8,40},{12,20},{16,48},{20,28},{24,56},{28,4},{32,64... | collective-permute-start | bytes 3145736 | tf_op jit(solution)/shard_map/ppermute | solution.py:40
  150.3 16.8 %collective-permute-start.30 = (bf16[128,4096]{1,0:T(8,128)(2,1)S(1)}, bf16[128,4096]{1,0:T(8,128)(2,1)S(1)}, u32[]{:S(2)}, u32[]{:S(2)}) collective-permute-start(bf16[128,4096]{1,0:T(8,128)(2,1)S(1)} %get-tuple-element.24), channel_id=1, source_target_pairs={{0,64},{4,20},{8,72},{12,28},{16,80},{20,4},{24,88},{28,12},{32,96... | collective-permute-start | bytes 3145736 | tf_op jit(solution)/shard_map/ppermute | solution.py:40
  150.4 26.1 %collective-permute-start.33 = (bf16[128,4096]{1,0:T(8,128)(2,1)S(1)}, bf16[128,4096]{1,0:T(8,128)(2,1)S(1)}, u32[]{:S(2)}, u32[]{:S(2)}) collective-permute-start(bf16[128,4096]{1,0:T(8,128)(2,1)S(1)} %get-tuple-element.27), channel_id=1, source_target_pairs={{0,32},{4,12},{8,40},{12,20},{16,48},{20,28},{24,56},{28,4},{32,64... | collective-permute-start | bytes 3145736 | tf_op jit(solution)/shard_map/ppermute | solution.py:40
  152.6 30.9 %collective-permute-start.32 = (bf16[128,4096]{1,0:T(8,128)(2,1)S(1)}, bf16[128,4096]{1,0:T(8,128)(2,1)S(1)}, u32[]{:S(2)}, u32[]{:S(2)}) collective-permute-start(bf16[128,4096]{1,0:T(8,128)(2,1)S(1)} %get-tuple-element.26), channel_id=1, source_target_pairs={{0,96},{4,28},{8,104},{12,4},{16,112},{20,12},{24,120},{28,20},{32... | collective-permute-start | bytes 3145736 | tf_op jit(solution)/shard_map/ppermute | solution.py:40
  152.6 45.3 %collective-permute-start.34 = (bf16[128,4096]{1,0:T(8,128)(2,1)S(1)}, bf16[128,4096]{1,0:T(8,128)(2,1)S(1)}, u32[]{:S(2)}, u32[]{:S(2)}) collective-permute-start(bf16[128,4096]{1,0:T(8,128)(2,1)S(1)} %get-tuple-element.28), channel_id=1, source_target_pairs={{0,64},{4,20},{8,72},{12,28},{16,80},{20,4},{24,88},{28,12},{32,96... | collective-permute-start | bytes 3145736 | tf_op jit(solution)/shard_map/ppermute | solution.py:40
  167.8 33.1 %collective-permute-start.31 = (bf16[64,4096]{1,0:T(8,128)(2,1)S(1)}, bf16[64,4096]{1,0:T(8,128)(2,1)S(1)}, u32[]{:S(2)}, u32[]{:S(2)}) collective-permute-start(bf16[64,4096]{1,0:T(8,128)(2,1)S(1)} %slice.53), channel_id=1, source_target_pairs={{0,24},{4,100},{8,0},{12,108},{16,8},{20,116},{24,16},{28,124},{32... | collective-permute-start | bytes 1572872 | tf_op jit(solution)/shard_map/ppermute | solution.py:40
  199.6 16.2 %collective-permute-start.35 = (bf16[64,4096]{1,0:T(8,128)(2,1)}, bf16[64,4096]{1,0:T(8,128)(2,1)S(1)}, u32[]{:S(2)}, u32[]{:S(2)}) collective-permute-start(bf16[64,4096]{1,0:T(8,128)(2,1)} %get-tuple-element.31), channel_id=1, source_target_pairs={{0,8},{4,36},{8,16},{12,44},{16,24},{20,52},{24,0},{28,60},{32,40}... | collective-permute-start | bytes 1572872 | tf_op jit(solution)/shard_map/ppermute | solution.py:40
  199.6 16.2 %collective-permute-start.36 = (bf16[64,4096]{1,0:T(8,128)(2,1)}, bf16[64,4096]{1,0:T(8,128)(2,1)S(1)}, u32[]{:S(2)}, u32[]{:S(2)}) collective-permute-start(bf16[64,4096]{1,0:T(8,128)(2,1)} %get-tuple-element.32), channel_id=1, source_target_pairs={{0,16},{4,68},{8,24},{12,76},{16,0},{20,84},{24,8},{28,92},{32,48}... | collective-permute-start | bytes 1572872 | tf_op jit(solution)/shard_map/ppermute | solution.py:40
  216.1 6.3 %collective-permute-start.39 = (bf16[16,4096]{1,0:T(8,128)(2,1)S(1)}, bf16[16,4096]{1,0:T(8,128)(2,1)S(1)}, u32[]{:S(2)}, u32[]{:S(2)}) collective-permute-start(bf16[16,4096]{1,0:T(8,128)(2,1)S(1)} %get-tuple-element.34), channel_id=1, source_target_pairs={{0,1},{1,2},{2,3},{3,0},{4,5},{5,6},{6,7},{7,4},{8,9},{9,10},{10,1... | collective-permute-start | bytes 393224 | tf_op jit(solution)/shard_map/ppermute | solution.py:48
  217.3 6.5 %collective-permute-start.38 = (bf16[16,4096]{1,0:T(8,128)(2,1)S(1)}, bf16[16,4096]{1,0:T(8,128)(2,1)S(1)}, u32[]{:S(2)}, u32[]{:S(2)}) collective-permute-start(bf16[16,4096]{1,0:T(8,128)(2,1)S(1)} %get-tuple-element.35), channel_id=1, source_target_pairs={{0,2},{1,3},{2,0},{3,1},{4,6},{5,7},{6,4},{7,5},{8,10},{9,11},{10,... | collective-permute-start | bytes 393224 | tf_op jit(solution)/shard_map/ppermute | solution.py:48
  218.3 6.3 %collective-permute-start.37 = (bf16[16,4096]{1,0:T(8,128)(2,1)S(1)}, bf16[16,4096]{1,0:T(8,128)(2,1)S(1)}, u32[]{:S(2)}, u32[]{:S(2)}) collective-permute-start(bf16[16,4096]{1,0:T(8,128)(2,1)S(1)} %get-tuple-element.36), channel_id=1, source_target_pairs={{0,3},{1,0},{2,1},{3,2},{4,7},{5,4},{6,5},{7,6},{8,11},{9,8},{10,9... | collective-permute-start | bytes 393224 | tf_op jit(solution)/shard_map/ppermute | solution.py:48
  (5 other events, 17.1 us)

commit v3 on v2

--- a/solution.py
+++ b/solution.py
@@ -160,27 +160,21 @@
         ins, refs = refs[:count], refs[count:]
         (ga, ua, da, gb, ub, db), refs = refs[:6], refs[6:]
         outs, refs = refs[:count], refs[count:]
-        x, sums, hidden, out, in_sems, out_sems = refs
-        fetches = [
-            pltpu.make_async_copy(ref, x.at[pl.ds(start, size), :], in_sems.at[i])
-            for i, (ref, start, size) in enumerate(zip(ins, starts, sizes))
-        ]
-        for copy in fetches:
-            copy.start()
-        for copy in fetches:
-            copy.wait()
-        sums[...] = jnp.zeros_like(sums)
-
-        @pl.loop(0, chunks)
-        def _(k):
+        x, w, dw, sums, hidden, out, x_sems, w_sems, d_sems, out_sems = refs
+
+        def first_copies(k):
             at = pl.ds(pl.multiple_of(k * deep, deep), deep)
-            for i, w in enumerate((ga, ua, gb, ub)):
-                sums[i] += lax.dot_general(
-                    x[:, at], w[:, at], (((1,), (1,)), ((), ())), preferred_element_type=f32
+            for i, ref in enumerate((ga, gb, ua, ub)):
+                yield pltpu.make_async_copy(ref.at[:, at], w.at[k, pl.ds(i * hid, hid), :], w_sems.at[k, i])
+            for i, ref in enumerate(ins):
+                yield pltpu.make_async_copy(
+                    ref.at[:, at], x.at[k, pl.ds(starts[i], sizes[i]), :], x_sems.at[k, i]
                 )
 
-        for i in range(2):
-            hidden[i] = (jax.nn.silu(sums[2 * i]) * sums[2 * i + 1]).astype(bf16)
+        def last_copies(n):
+            at = pl.ds(pl.multiple_of(n * wide, wide), wide)
+            for i, ref in enumerate((da, db)):
+                yield pltpu.make_async_copy(ref.at[:, at], dw.at[n, pl.ds(i * hid, hid), :], d_sems.at[n, i])
 
         def out_copies(n):
             at = pl.ds(pl.multiple_of(n * wide, wide), wide)
@@ -189,11 +183,27 @@
                     out.at[n, pl.ds(starts[i], sizes[i]), :], ref.at[:, at], out_sems.at[n, i]
                 )
 
+        for k in range(chunks):
+            for copy in first_copies(k):
+                copy.start()
+        for n in range(chunks):
+            for copy in last_copies(n):
+                copy.start()
+        sums[...] = jnp.zeros_like(sums)
+
+        @pl.loop(0, chunks)
+        def _(k):
+            for copy in first_copies(k):
+                copy.wait()
+            sums[...] += lax.dot_general(x[k], w[k], (((1,), (1,)), ((), ())), preferred_element_type=f32)
+
+        hidden[...] = (jax.nn.silu(sums[:, : 2 * hid]) * sums[:, 2 * hid :]).astype(bf16)
+
         @pl.loop(0, chunks)
         def _(n):
-            at = pl.ds(pl.multiple_of(n * wide, wide), wide)
-            product = jnp.dot(hidden[0], da[:, at], preferred_element_type=f32)
-            out[n] = (product + jnp.dot(hidden[1], db[:, at], preferred_element_type=f32)).astype(bf16)
+            for copy in last_copies(n):
+                copy.wait()
+            out[n] = jnp.dot(hidden[...], dw[n], preferred_element_type=f32).astype(bf16)
             for copy in out_copies(n):
                 copy.start()
 
@@ -201,24 +211,28 @@
             for copy in out_copies(n):
                 copy.wait()
 
-    far_away = pl.BlockSpec(memory_space=pltpu.HBM)
+    anywhere = pl.BlockSpec(memory_space=pltpu.HBM)
     return pl.pallas_call(
         kernel,
         out_shape=tuple(jax.ShapeDtypeStruct((size, width), bf16) for size in sizes),
-        in_specs=[far_away] * count + [vmem_spec()] * 6,
-        out_specs=(far_away,) * count,
+        in_specs=[anywhere] * (count + 6),
+        out_specs=(anywhere,) * count,
         scratch_shapes=[
-            pltpu.VMEM((rows, depth), bf16),
-            pltpu.VMEM((4, rows, hid), f32),
-            pltpu.VMEM((2, rows, hid), bf16),
+            pltpu.VMEM((chunks, rows, deep), bf16),
+            pltpu.VMEM((chunks, 4 * hid, deep), bf16),
+            pltpu.VMEM((chunks, 2 * hid, wide), bf16),
+            pltpu.VMEM((rows, 4 * hid), f32),
+            pltpu.VMEM((rows, 2 * hid), bf16),
             pltpu.VMEM((chunks, rows, wide), bf16),
-            pltpu.SemaphoreType.DMA((count,)),
+            pltpu.SemaphoreType.DMA((chunks, count)),
+            pltpu.SemaphoreType.DMA((chunks, 4)),
+            pltpu.SemaphoreType.DMA((chunks, 2)),
             pltpu.SemaphoreType.DMA((chunks, count)),
         ],
         cost_estimate=pl.CostEstimate(
-            flops=12 * rows * depth * hid, transcendentals=2 * rows * hid, bytes_accessed=4 * rows * depth
+            flops=12 * rows * depth * hid, transcendentals=2 * rows * hid, bytes_accessed=12 * depth * hid
         ),
-        compiler_params=pltpu.CompilerParams(vmem_limit_bytes=18 << 20),
+        compiler_params=pltpu.CompilerParams(vmem_limit_bytes=(26 << 20) + rows * (32 << 10)),
         name="expert_rows",
     )(*pieces, *own, *other)
 

time: 226 us -> 235 us (1.040)
  the two profiles are of different devices: /device:TPU:96 before, /device:TPU:32 now
where the time goes in v3:
time: 235 us; the launch traced here: 234 us
  waiting for transfers between devices  118 us (50%)
  Pallas kernels  51.7 us (22%)
  starting transfers between devices  45.8 us (19%)
  local copies, waits for them, and re-layouts  10.3 us (4%)
  other arithmetic  6.34 us (3%)
    ppermute x24, waiting for transfers between devices, shift(): return lax.ppermute(a, 'ctx', RINGS[phase, step])  94.5 us
    pallas_call x4, Pallas kernels, expert_rows(): pl.pallas_call(kernel, out_shape=tuple((jax.ShapeDtypeStruct((size, width...  40.5 us
    ppermute x24, starting transfers between devices, shift(): return lax.ppermute(a, 'ctx', RINGS[phase, step])  31.4 us
    ppermute x9, waiting for transfers between devices, shift_exp(): return lax.ppermute(a, 'exp', [(i, (i + step) % 4) for i in range(4)])  21.7 us
    ppermute x9, starting transfers between devices, shift_exp(): return lax.ppermute(a, 'exp', [(i, (i + step) % 4) for i in range(4)])  13.8 us
    pallas_call x1, Pallas kernels, attend(): pl.pallas_call(kernel, out_shape=tuple((jax.ShapeDtypeStruct((sub, width)...  11.2 us
    unnamed x37, local copies, waits for them, and re-layouts  6.72 us
  transfers between devices with their start and end apart: 40, of which 24 were waited for; matrix products, arithmetic and copies ran while one was open for 4% of the time, Pallas kernels for 17%

profile of v3, /device:TPU:32, one launch (start us, length us, event | category | flops | bytes accessed | tf_op | source)
XLA Modules:
  0.0 234.4 jit_solution(7951894952443027594)
XLA Ops:
  1.7 3.0 %collective-permute-start.2 = (bf16[128,512]{1,0:T(8,128)(2,1)S(1)}, bf16[128,512]{1,0:T(8,128)(2,1)S(1)}, u32[]{:S(2)}, u32[]{:S(2)}) collective-permute-start(bf16[128,512]{1,0:T(8,128)(2,1)S(1)} %constant_dynamic-update-slice_fusion), channel_id=1, source_target_pairs={{0,16},{4,68},{8,24},{12,76},{16,0},{20,84},{24,8},{28,92},{32,48}... | collective-permute-start | bytes 393224 | tf_op jit(solution)/shard_map/ppermute | solution.py:40
  4.7 1.1 collective-permute-start.1
  9.7 2.4 %collective-permute-done = bf16[128,512]{1,0:T(8,128)(2,1)S(1)} collective-permute-done((bf16[128,512]{1,0:T(8,128)(2,1)S(1)}, bf16[128,512]{1,0:T(8,128)(2,1)S(1)}, u32[]{:S(2)}, u32[]{:S(2)}) %collective-permute-start) | collective-permute-done | bytes 131104 | tf_op jit(solution)/shard_map/ppermute | solution.py:40
  12.1 3.1 %collective-permute-start.8 = (bf16[512,512]{1,0:T(8,128)(2,1)S(1)}, bf16[512,512]{1,0:T(8,128)(2,1)S(1)}, u32[]{:S(2)}, u32[]{:S(2)}) collective-permute-start(bf16[512,512]{1,0:T(8,128)(2,1)S(1)} %pad_maximum_fusion.refs_0_), channel_id=1, source_target_pairs={{0,64},{4,20},{8,72},{12,28},{16,80},{20,4},{24,88},{28,12},{32,96... | collective-permute-start | bytes 1572872 | tf_op jit(solution)/shard_map/ppermute | solution.py:40
  15.2 1.0 collective-permute-start.6
  16.2 1.0 collective-permute-start.4
  18.7 4.3 %collective-permute-done.8.refs_6_ = bf16[512,512]{1,0:T(8,128)(2,1)S(1)} collective-permute-done((bf16[512,512]{1,0:T(8,128)(2,1)S(1)}, bf16[512,512]{1,0:T(8,128)(2,1)S(1)}, u32[]{:S(2)}, u32[]{:S(2)}) %collective-permute-start.8) | collective-permute-done | bytes 524320 | tf_op jit(solution)/shard_map/ppermute | solution.py:40
  23.0 5.5 %collective-permute-done.6.refs_4_ = bf16[512,512]{1,0:T(8,128)(2,1)S(1)} collective-permute-done((bf16[512,512]{1,0:T(8,128)(2,1)S(1)}, bf16[512,512]{1,0:T(8,128)(2,1)S(1)}, u32[]{:S(2)}, u32[]{:S(2)}) %collective-permute-start.6) | collective-permute-done | bytes 524320 | tf_op jit(solution)/shard_map/ppermute | solution.py:40
  29.3 1.2 collective-permute-done.7.refs_5_
  32.4 11.2 %attend.1 = (f32[32,4096]{1,0:T(8,128)S(1)}, bf16[32,4096]{1,0:T(8,128)(2,1)S(1)}, bf16[32,4096]{1,0:T(8,128)(2,1)S(1)}, bf16[32,4096]{1,0:T(8,128)(2,1)S(1)}) custom-call(s32[1]{0:T(128)} %bitcast.mine_ref, bf16[128,1024]{1,0:T(8,128)(2,1)S(1)} %copy-done.7, s32[128,128]{1,0:T(8,128)S(1)} %broadcast_in_dim.125.qpos_ref, ...), custom_call_target="tpu_custom_call" | custom-call | flops 4294967296 | bytes 4194304 | tf_op jit(solution)/shard_map/attend/pallas_call | solution.py:129
  43.5 3.3 %collective-permute-start.10 = (bf16[32,4096]{1,0:T(8,128)(2,1)S(1)}, bf16[32,4096]{1,0:T(8,128)(2,1)S(1)}, u32[]{:S(2)}, u32[]{:S(2)}) collective-permute-start(bf16[32,4096]{1,0:T(8,128)(2,1)S(1)} %get-tuple-element.18), channel_id=1, source_target_pairs={{0,2},{1,3},{2,0},{3,1},{4,6},{5,7},{6,4},{7,5},{8,10},{9,11},{10,... | collective-permute-start | bytes 786440 | tf_op jit(solution)/shard_map/ppermute | solution.py:48
  47.5 2.6 %collective-permute-start.12 = (bf16[32,4096]{1,0:T(8,128)(2,1)S(1)}, bf16[32,4096]{1,0:T(8,128)(2,1)S(1)}, u32[]{:S(2)}, u32[]{:S(2)}) collective-permute-start(bf16[32,4096]{1,0:T(8,128)(2,1)S(1)} %get-tuple-element.20), channel_id=1, source_target_pairs={{0,3},{1,0},{2,1},{3,2},{4,7},{5,4},{6,5},{7,6},{8,11},{9,8},{10,9... | collective-permute-start | bytes 786440 | tf_op jit(solution)/shard_map/ppermute | solution.py:48
  50.5 3.8 %collective-permute-done.10 = bf16[32,4096]{1,0:T(8,128)(2,1)S(1)} collective-permute-done((bf16[32,4096]{1,0:T(8,128)(2,1)S(1)}, bf16[32,4096]{1,0:T(8,128)(2,1)S(1)}, u32[]{:S(2)}, u32[]{:S(2)}) %collective-permute-start.10) | collective-permute-done | bytes 262176 | tf_op jit(solution)/shard_map/ppermute | solution.py:48
  54.3 4.7 %collective-permute-done.11 = bf16[32,4096]{1,0:T(8,128)(2,1)S(1)} collective-permute-done((bf16[32,4096]{1,0:T(8,128)(2,1)S(1)}, bf16[32,4096]{1,0:T(8,128)(2,1)S(1)}, u32[]{:S(2)}, u32[]{:S(2)}) %collective-permute-start.11) | collective-permute-done | bytes 262176 | tf_op jit(solution)/shard_map/ppermute | solution.py:48
  60.2 2.7 %collective-permute-start.15 = (bf16[16,4096]{1,0:T(8,128)(2,1)S(1)}, bf16[16,4096]{1,0:T(8,128)(2,1)S(1)}, u32[]{:S(2)}, u32[]{:S(2)}) collective-permute-start(bf16[16,4096]{1,0:T(8,128)(2,1)S(1)} %get-tuple-element.39), channel_id=1, source_target_pairs={{0,3},{1,0},{2,1},{3,2},{4,7},{5,4},{6,5},{7,6},{8,11},{9,8},{10,9... | collective-permute-start | bytes 393224 | tf_op jit(solution)/shard_map/ppermute | solution.py:48
  64.4 4.3 %collective-permute-done.15 = bf16[16,4096]{1,0:T(8,128)(2,1)S(1)} collective-permute-done((bf16[16,4096]{1,0:T(8,128)(2,1)S(1)}, bf16[16,4096]{1,0:T(8,128)(2,1)S(1)}, u32[]{:S(2)}, u32[]{:S(2)}) %collective-permute-start.15) | collective-permute-done | bytes 131104 | tf_op jit(solution)/shard_map/ppermute | solution.py:48
  68.6 2.1 collective-permute-done.14
  70.8 1.6 collective-permute-done.13
  72.8 1.7 collective-permute-start.16
  74.5 8.6 %collective-permute-done.16 = bf16[64,4096]{1,0:T(8,128)(2,1)S(1)} collective-permute-done((bf16[64,4096]{1,0:T(8,128)(2,1)S(1)}, bf16[64,4096]{1,0:T(8,128)(2,1)S(1)}, u32[]{:S(2)}, u32[]{:S(2)}) %collective-permute-start.16) | collective-permute-done | bytes 524320 | tf_op jit(solution)/shard_map/ppermute | solution.py:40
  83.8 1.2 collective-permute-start.22
  85.0 14.4 %collective-permute-done.18 = bf16[64,4096]{1,0:T(8,128)(2,1)S(1)} collective-permute-done((bf16[64,4096]{1,0:T(8,128)(2,1)S(1)}, bf16[64,4096]{1,0:T(8,128)(2,1)S(1)}, u32[]{:S(2)}, u32[]{:S(2)}) %collective-permute-start.18) | collective-permute-done | bytes 524320 | tf_op jit(solution)/shard_map/ppermute | solution.py:40
  99.5 1.6 collective-permute-start.23
  101.1 2.2 collective-permute-done.22.refs_0_
  103.3 3.2 %collective-permute-start.26 = (bf16[128,4096]{1,0:T(8,128)(2,1)S(1)}, bf16[128,4096]{1,0:T(8,128)(2,1)S(1)}, u32[]{:S(2)}, u32[]{:S(2)}) collective-permute-start(bf16[128,4096]{1,0:T(8,128)(2,1)S(1)} %constant_dynamic-update-slice_fusion.2.refs_0_), channel_id=1, source_target_pairs={{0,96},{4,28},{8,104},{12,4},{16,112},{20,12},{24,120},{28,20},{32... | collective-permute-start | bytes 3145736 | tf_op jit(solution)/shard_map/ppermute | solution.py:40
  106.5 7.8 %collective-permute-done.23.refs_1_ = bf16[128,4096]{1,0:T(8,128)(2,1)S(1)} collective-permute-done((bf16[128,4096]{1,0:T(8,128)(2,1)S(1)}, bf16[128,4096]{1,0:T(8,128)(2,1)S(1)}, u32[]{:S(2)}, u32[]{:S(2)}) %collective-permute-start.23) | collective-permute-done | bytes 1048608 | tf_op jit(solution)/shard_map/ppermute | solution.py:40
  114.4 1.5 collective-permute-start.25
  115.9 3.2 %collective-permute-start.28 = (bf16[128,4096]{1,0:T(8,128)(2,1)S(1)}, bf16[128,4096]{1,0:T(8,128)(2,1)S(1)}, u32[]{:S(2)}, u32[]{:S(2)}) collective-permute-start(bf16[128,4096]{1,0:T(8,128)(2,1)S(1)} %collective-permute-done.22.refs_0_), channel_id=1, source_target_pairs={{0,32},{4,12},{8,40},{12,20},{16,48},{20,28},{24,56},{28,4},{32,64... | collective-permute-start | bytes 3145736 | tf_op jit(solution)/shard_map/ppermute | solution.py:40
  119.1 1.8 copy-done.8
  120.9 2.0 copy-done.3
  123.0 10.4 %expert_rows.5 = (bf16[128,4096]{1,0:T(8,128)(2,1)}, bf16[128,4096]{1,0:T(8,128)(2,1)S(1)}) custom-call(bf16[128,4096]{1,0:T(8,128)(2,1)S(1)} %collective-permute-done.22.refs_0_, bf16[128,4096]{1,0:T(8,128)(2,1)S(1)} %collective-permute-done.23.refs_1_, bf16[448,4096]{1,0:T(8,128)(2,1)S(1)} %bitcast.29, bf16[448,4096]{1,0:T(8,128)(2,1)S(1)} %bitcast.34, ...), custom_call_target="tpu_custom_call" | custom-call | flops 5637144576 | bytes 22020096 | tf_op jit(solution)/shard_map/expert_rows/pallas_call | solution.py:215
  133.5 10.4 %expert_rows.6 = (bf16[128,4096]{1,0:T(8,128)(2,1)S(1)}, bf16[128,4096]{1,0:T(8,128)(2,1)}) custom-call(bf16[128,4096]{1,0:T(8,128)(2,1)S(1)} %collective-permute-done.25.refs_0_, bf16[128,4096]{1,0:T(8,128)(2,1)S(1)} %collective-permute-done.26.refs_1_, bf16[448,4096]{1,0:T(8,128)(2,1)S(1)} %bitcast.30, bf16[448,4096]{1,0:T(8,128)(2,1)S(1)} %bitcast.35, ...), custom_call_target="tpu_custom_call" | custom-call | flops 5637144576 | bytes 22020096 | tf_op jit(solution)/shard_map/expert_rows/pallas_call | solution.py:215
  144.9 2.0 collective-permute-start.27
  146.9 9.8 %expert_rows.7 = (bf16[128,4096]{1,0:T(8,128)(2,1)S(1)}, bf16[128,4096]{1,0:T(8,128)(2,1)S(1)}) custom-call(bf16[128,4096]{1,0:T(8,128)(2,1)S(1)} %collective-permute-done.28.refs_0_, bf16[128,4096]{1,0:T(8,128)(2,1)S(1)} %collective-permute-done.29.refs_1_, bf16[448,4096]{1,0:T(8,128)(2,1)S(1)} %bitcast.31, bf16[448,4096]{1,0:T(8,128)(2,1)S(1)} %bitcast.36, ...), custom_call_target="tpu_custom_call" | custom-call | flops 5637144576 | bytes 22020096 | tf_op jit(solution)/shard_map/expert_rows/pallas_call | solution.py:215
  156.8 1.1 collective-permute-start.30
  158.3 1.5 collective-permute-start.32
  159.9 2.6 %collective-permute-start.34 = (bf16[128,4096]{1,0:T(8,128)(2,1)S(1)}, bf16[128,4096]{1,0:T(8,128)(2,1)S(1)}, u32[]{:S(2)}, u32[]{:S(2)}) collective-permute-start(bf16[128,4096]{1,0:T(8,128)(2,1)S(1)} %get-tuple-element.28), channel_id=1, source_target_pairs={{0,64},{4,20},{8,72},{12,28},{16,80},{20,4},{24,88},{28,12},{32,96... | collective-permute-start | bytes 3145736 | tf_op jit(solution)/shard_map/ppermute | solution.py:40
  162.4 9.8 %expert_rows.4 = (bf16[128,4096]{1,0:T(8,128)(2,1)S(1)}, bf16[128,4096]{1,0:T(8,128)(2,1)S(1)}) custom-call(bf16[128,4096]{1,0:T(8,128)(2,1)S(1)} %constant_dynamic-update-slice_fusion.2.refs_0_, bf16[128,4096]{1,0:T(8,128)(2,1)S(1)} %constant_dynamic-update-slice_fusion.7.refs_1_, bf16[448,4096]{1,0:T(8,128)(2,1)S(1)} %bitcast.32, ...), custom_call_target="tpu_custom_call" | custom-call | flops 5637144576 | bytes 22020096 | tf_op jit(solution)/shard_map/expert_rows/pallas_call | solution.py:215
  172.2 2.9 %collective-permute-done.30 = bf16[128,4096]{1,0:T(8,128)(2,1)S(1)} collective-permute-done((bf16[128,4096]{1,0:T(8,128)(2,1)S(1)}, bf16[128,4096]{1,0:T(8,128)(2,1)S(1)}, u32[]{:S(2)}, u32[]{:S(2)}) %collective-permute-start.30) | collective-permute-done | bytes 1048608 | tf_op jit(solution)/shard_map/ppermute | solution.py:40
  175.2 1.9 add_convert_fusion.1
  177.2 6.0 %collective-permute-done.33 = bf16[128,4096]{1,0:T(8,128)(2,1)S(1)} collective-permute-done((bf16[128,4096]{1,0:T(8,128)(2,1)S(1)}, bf16[128,4096]{1,0:T(8,128)(2,1)S(1)}, u32[]{:S(2)}, u32[]{:S(2)}) %collective-permute-start.33) | collective-permute-done | bytes 1048608 | tf_op jit(solution)/shard_map/ppermute | solution.py:40
  183.2 6.8 %collective-permute-done.32 = bf16[128,4096]{1,0:T(8,128)(2,1)S(1)} collective-permute-done((bf16[128,4096]{1,0:T(8,128)(2,1)S(1)}, bf16[128,4096]{1,0:T(8,128)(2,1)S(1)}, u32[]{:S(2)}, u32[]{:S(2)}) %collective-permute-start.32) | collective-permute-done | bytes 1048608 | tf_op jit(solution)/shard_map/ppermute | solution.py:40
  190.0 16.6 %collective-permute-done.34 = bf16[128,4096]{1,0:T(8,128)(2,1)S(1)} collective-permute-done((bf16[128,4096]{1,0:T(8,128)(2,1)S(1)}, bf16[128,4096]{1,0:T(8,128)(2,1)S(1)}, u32[]{:S(2)}, u32[]{:S(2)}) %collective-permute-start.34) | collective-permute-done | bytes 1048608 | tf_op jit(solution)/shard_map/ppermute | solution.py:40
  207.3 1.1 fusion.78
  208.8 15.7 %collective-permute-done.35 = bf16[64,4096]{1,0:T(8,128)(2,1)S(1)} collective-permute-done((bf16[64,4096]{1,0:T(8,128)(2,1)}, bf16[64,4096]{1,0:T(8,128)(2,1)S(1)}, u32[]{:S(2)}, u32[]{:S(2)}) %collective-permute-start.35) | collective-permute-done | bytes 524320 | tf_op jit(solution)/shard_map/ppermute | solution.py:40
  225.0 2.2 collective-permute-start.38
  227.2 1.3 collective-permute-start.37
  228.6 4.0 %collective-permute-done.39 = bf16[16,4096]{1,0:T(8,128)(2,1)S(1)} collective-permute-done((bf16[16,4096]{1,0:T(8,128)(2,1)S(1)}, bf16[16,4096]{1,0:T(8,128)(2,1)S(1)}, u32[]{:S(2)}, u32[]{:S(2)}) %collective-permute-start.39) | collective-permute-done | bytes 131104 | tf_op jit(solution)/shard_map/ppermute | solution.py:48
  (135 shorter events, 19.6 us)
Async XLA Ops:
  0.0 208.4 %copy-start = (f32[4096,4]{0,1:T(4,128)S(1)}, f32[4096,4]{0,1:T(4,128)}, u32[]{:S(2)}) copy-start(f32[4096,4]{0,1:T(4,128)} %param.27) | copy-start | bytes 196612
  1.7 7.3 %collective-permute-start.2 = (bf16[128,512]{1,0:T(8,128)(2,1)S(1)}, bf16[128,512]{1,0:T(8,128)(2,1)S(1)}, u32[]{:S(2)}, u32[]{:S(2)}) collective-permute-start(bf16[128,512]{1,0:T(8,128)(2,1)S(1)} %constant_dynamic-update-slice_fusion), channel_id=1, source_target_pairs={{0,16},{4,68},{8,24},{12,76},{16,0},{20,84},{24,8},{28,92},{32,48}... | collective-permute-start | bytes 393224 | tf_op jit(solution)/shard_map/ppermute | solution.py:40
  4.7 5.0 %collective-permute-start.1 = (bf16[128,512]{1,0:T(8,128)(2,1)S(1)}, bf16[128,512]{1,0:T(8,128)(2,1)S(1)}, u32[]{:S(2)}, u32[]{:S(2)}) collective-permute-start(bf16[128,512]{1,0:T(8,128)(2,1)S(1)} %constant_dynamic-update-slice_fusion), channel_id=1, source_target_pairs={{0,24},{4,100},{8,0},{12,108},{16,8},{20,116},{24,16},{28,124},{32... | collective-permute-start | bytes 393224 | tf_op jit(solution)/shard_map/ppermute | solution.py:40
  5.9 6.2 %collective-permute-start = (bf16[128,512]{1,0:T(8,128)(2,1)S(1)}, bf16[128,512]{1,0:T(8,128)(2,1)S(1)}, u32[]{:S(2)}, u32[]{:S(2)}) collective-permute-start(bf16[128,512]{1,0:T(8,128)(2,1)S(1)} %constant_dynamic-update-slice_fusion), channel_id=1, source_target_pairs={{0,8},{4,36},{8,16},{12,44},{16,24},{20,52},{24,0},{28,60},{32,40}... | collective-permute-start | bytes 393224 | tf_op jit(solution)/shard_map/ppermute | solution.py:40
  12.1 19.3 %copy-start.9 = (bf16[512,512]{1,0:T(8,128)(2,1)}, bf16[512,512]{1,0:T(8,128)(2,1)S(1)}, u32[]{:S(2)}) copy-start(bf16[512,512]{1,0:T(8,128)(2,1)S(1)} %pad_maximum_fusion.refs_0_) | copy-start | bytes 1572868
  12.1 10.9 %collective-permute-start.8 = (bf16[512,512]{1,0:T(8,128)(2,1)S(1)}, bf16[512,512]{1,0:T(8,128)(2,1)S(1)}, u32[]{:S(2)}, u32[]{:S(2)}) collective-permute-start(bf16[512,512]{1,0:T(8,128)(2,1)S(1)} %pad_maximum_fusion.refs_0_), channel_id=1, source_target_pairs={{0,64},{4,20},{8,72},{12,28},{16,80},{20,4},{24,88},{28,12},{32,96... | collective-permute-start | bytes 1572872 | tf_op jit(solution)/shard_map/ppermute | solution.py:40
  15.2 13.3 %collective-permute-start.6 = (bf16[512,512]{1,0:T(8,128)(2,1)S(1)}, bf16[512,512]{1,0:T(8,128)(2,1)S(1)}, u32[]{:S(2)}, u32[]{:S(2)}) collective-permute-start(bf16[512,512]{1,0:T(8,128)(2,1)S(1)} %pad_maximum_fusion.refs_0_), channel_id=1, source_target_pairs={{0,96},{4,28},{8,104},{12,4},{16,112},{20,12},{24,120},{28,20},{32... | collective-permute-start | bytes 1572872 | tf_op jit(solution)/shard_map/ppermute | solution.py:40
  16.2 12.8 %collective-permute-start.4 = (bf16[512,512]{1,0:T(8,128)(2,1)S(1)}, bf16[512,512]{1,0:T(8,128)(2,1)S(1)}, u32[]{:S(2)}, u32[]{:S(2)}) collective-permute-start(bf16[512,512]{1,0:T(8,128)(2,1)S(1)} %pad_maximum_fusion.refs_0_), channel_id=1, source_target_pairs={{0,32},{4,12},{8,40},{12,20},{16,48},{20,28},{24,56},{28,4},{32,64... | collective-permute-start | bytes 1572872 | tf_op jit(solution)/shard_map/ppermute | solution.py:40
  18.6 10.7 %collective-permute-start.3 = (bf16[512,512]{1,0:T(8,128)(2,1)S(1)}, bf16[512,512]{1,0:T(8,128)(2,1)}, u32[]{:S(2)}, u32[]{:S(2)}) collective-permute-start(bf16[512,512]{1,0:T(8,128)(2,1)S(1)} %pad_maximum_fusion.refs_0_), channel_id=1, source_target_pairs={{0,4},{4,0},{8,12},{12,8},{16,20},{20,16},{24,28},{28,24},{32,36},... | collective-permute-start | bytes 1572872 | tf_op jit(solution)/shard_map/ppermute | solution.py:44
  23.0 6.3 %collective-permute-start.9 = (bf16[512,512]{1,0:T(8,128)(2,1)S(1)}, bf16[512,512]{1,0:T(8,128)(2,1)}, u32[]{:S(2)}, u32[]{:S(2)}) collective-permute-start(bf16[512,512]{1,0:T(8,128)(2,1)S(1)} %collective-permute-done.8.refs_6_), channel_id=1, source_target_pairs={{0,4},{4,0},{8,12},{12,8},{16,20},{20,16},{24,28},{28,24},{32,36},... | collective-permute-start | bytes 1572872 | tf_op jit(solution)/shard_map/ppermute | solution.py:44
  28.5 2.0 collective-permute-start.7
  29.0 2.3 collective-permute-start.5
  32.4 17.7 %copy-start.12 = (s32[32,2]{0,1:T(2,128)S(1)}, s32[32,2]{0,1:T(2,128)}, u32[]{:S(2)}) copy-start(s32[32,2]{0,1:T(2,128)} %param.28) | copy-start | bytes 772
  32.4 27.1 %copy-start.10 = (bf16[32,4096]{1,0:T(8,128)(2,1)S(1)}, bf16[32,4096]{1,0:T(8,128)(2,1)}, u32[]{:S(2)}) copy-start(bf16[32,4096]{1,0:T(8,128)(2,1)} %param.23) | copy-start | bytes 786436
  32.4 27.4 %copy-start.11 = (f32[4096]{0:T(1024)S(1)}, f32[4096]{0:T(1024)}, u32[]{:S(2)}) copy-start(f32[4096]{0:T(1024)} %param.26) | copy-start | bytes 49156
  43.5 10.8 %collective-permute-start.10 = (bf16[32,4096]{1,0:T(8,128)(2,1)S(1)}, bf16[32,4096]{1,0:T(8,128)(2,1)S(1)}, u32[]{:S(2)}, u32[]{:S(2)}) collective-permute-start(bf16[32,4096]{1,0:T(8,128)(2,1)S(1)} %get-tuple-element.18), channel_id=1, source_target_pairs={{0,2},{1,3},{2,0},{3,1},{4,6},{5,7},{6,4},{7,5},{8,10},{9,11},{10,... | collective-permute-start | bytes 786440 | tf_op jit(solution)/shard_map/ppermute | solution.py:48
  46.8 12.3 %collective-permute-start.11 = (bf16[32,4096]{1,0:T(8,128)(2,1)S(1)}, bf16[32,4096]{1,0:T(8,128)(2,1)S(1)}, u32[]{:S(2)}, u32[]{:S(2)}) collective-permute-start(bf16[32,4096]{1,0:T(8,128)(2,1)S(1)} %get-tuple-element.19), channel_id=1, source_target_pairs={{0,1},{1,2},{2,3},{3,0},{4,5},{5,6},{6,7},{7,4},{8,9},{9,10},{10,1... | collective-permute-start | bytes 786440 | tf_op jit(solution)/shard_map/ppermute | solution.py:48
  47.5 12.0 %collective-permute-start.12 = (bf16[32,4096]{1,0:T(8,128)(2,1)S(1)}, bf16[32,4096]{1,0:T(8,128)(2,1)S(1)}, u32[]{:S(2)}, u32[]{:S(2)}) collective-permute-start(bf16[32,4096]{1,0:T(8,128)(2,1)S(1)} %get-tuple-element.20), channel_id=1, source_target_pairs={{0,3},{1,0},{2,1},{3,2},{4,7},{5,4},{6,5},{7,6},{8,11},{9,8},{10,9... | collective-permute-start | bytes 786440 | tf_op jit(solution)/shard_map/ppermute | solution.py:48
  60.2 8.4 %collective-permute-start.15 = (bf16[16,4096]{1,0:T(8,128)(2,1)S(1)}, bf16[16,4096]{1,0:T(8,128)(2,1)S(1)}, u32[]{:S(2)}, u32[]{:S(2)}) collective-permute-start(bf16[16,4096]{1,0:T(8,128)(2,1)S(1)} %get-tuple-element.39), channel_id=1, source_target_pairs={{0,3},{1,0},{2,1},{3,2},{4,7},{5,4},{6,5},{7,6},{8,11},{9,8},{10,9... | collective-permute-start | bytes 393224 | tf_op jit(solution)/shard_map/ppermute | solution.py:48
  62.9 7.9 %collective-permute-start.14 = (bf16[16,4096]{1,0:T(8,128)(2,1)S(1)}, bf16[16,4096]{1,0:T(8,128)(2,1)S(1)}, u32[]{:S(2)}, u32[]{:S(2)}) collective-permute-start(bf16[16,4096]{1,0:T(8,128)(2,1)S(1)} %get-tuple-element.40), channel_id=1, source_target_pairs={{0,2},{1,3},{2,0},{3,1},{4,6},{5,7},{6,4},{7,5},{8,10},{9,11},{10,... | collective-permute-start | bytes 393224 | tf_op jit(solution)/shard_map/ppermute | solution.py:48
  63.7 8.7 %collective-permute-start.13 = (bf16[16,4096]{1,0:T(8,128)(2,1)S(1)}, bf16[16,4096]{1,0:T(8,128)(2,1)S(1)}, u32[]{:S(2)}, u32[]{:S(2)}) collective-permute-start(bf16[16,4096]{1,0:T(8,128)(2,1)S(1)} %get-tuple-element.41), channel_id=1, source_target_pairs={{0,1},{1,2},{2,3},{3,0},{4,5},{5,6},{6,7},{7,4},{8,9},{9,10},{10,1... | collective-permute-start | bytes 393224 | tf_op jit(solution)/shard_map/ppermute | solution.py:48
  63.8 52.0 %collective-permute-start.19 = (bf16[448,4096]{1,0:T(8,128)(2,1)S(1)}, bf16[448,4096]{1,0:T(8,128)(2,1)S(1)}, u32[]{:S(2)}, u32[]{:S(2)}) collective-permute-start(bf16[448,4096]{1,0:T(8,128)(2,1)S(1)} %bitcast.28), channel_id=1, source_target_pairs={{0,4},{4,0},{8,12},{12,8},{16,20},{20,16},{24,28},{28,24},{32,36},... | collective-permute-start | bytes 11010056 | tf_op jit(solution)/shard_map/ppermute | solution.py:44
  63.9 55.3 %collective-permute-start.20 = (bf16[448,4096]{1,0:T(8,128)(2,1)}, bf16[448,4096]{1,0:T(8,128)(2,1)S(1)}, u32[]{:S(2)}, u32[]{:S(2)}) collective-permute-start(bf16[448,4096]{1,0:T(8,128)(2,1)} %bitcast.33), channel_id=1, source_target_pairs={{0,4},{4,0},{8,12},{12,8},{16,20},{20,16},{24,28},{28,24},{32,36},... | collective-permute-start | bytes 11010056 | tf_op jit(solution)/shard_map/ppermute | solution.py:44
  68.6 50.5 %collective-permute-start.21 = (bf16[448,4096]{1,0:T(8,128)(2,1)}, bf16[448,4096]{1,0:T(8,128)(2,1)}, u32[]{:S(2)}, u32[]{:S(2)}) collective-permute-start(bf16[448,4096]{1,0:T(8,128)(2,1)} %bitcast.38), channel_id=1, source_target_pairs={{0,4},{4,0},{8,12},{12,8},{16,20},{20,16},{24,28},{28,24},{32,36},... | collective-permute-start | bytes 11010056 | tf_op jit(solution)/shard_map/ppermute | solution.py:44
  72.4 48.6 %copy-start.2 = (bf16[1,4096,448]{1,2,0:T(8,128)(2,1)S(1)}, bf16[1,4096,448]{1,2,0:T(8,128)(2,1)}, u32[]{:S(2)}) copy-start(bf16[1,4096,448]{1,2,0:T(8,128)(2,1)} %param.30) | copy-start | bytes 11010052
  72.4 11.4 %collective-permute-start.17 = (bf16[64,4096]{1,0:T(8,128)(2,1)S(1)}, bf16[64,4096]{1,0:T(8,128)(2,1)S(1)}, u32[]{:S(2)}, u32[]{:S(2)}) collective-permute-start(bf16[64,4096]{1,0:T(8,128)(2,1)S(1)} %pad_maximum_fusion.1), channel_id=1, source_target_pairs={{0,24},{4,100},{8,0},{12,108},{16,8},{20,116},{24,16},{28,124},{32... | collective-permute-start | bytes 1572872 | tf_op jit(solution)/shard_map/ppermute | solution.py:40
  72.8 10.4 %collective-permute-start.16 = (bf16[64,4096]{1,0:T(8,128)(2,1)S(1)}, bf16[64,4096]{1,0:T(8,128)(2,1)S(1)}, u32[]{:S(2)}, u32[]{:S(2)}) collective-permute-start(bf16[64,4096]{1,0:T(8,128)(2,1)S(1)} %pad_maximum_fusion.1), channel_id=1, source_target_pairs={{0,8},{4,36},{8,16},{12,44},{16,24},{20,52},{24,0},{28,60},{32,40}... | collective-permute-start | bytes 1572872 | tf_op jit(solution)/shard_map/ppermute | solution.py:40
  83.2 16.3 %collective-permute-start.18 = (bf16[64,4096]{1,0:T(8,128)(2,1)S(1)}, bf16[64,4096]{1,0:T(8,128)(2,1)S(1)}, u32[]{:S(2)}, u32[]{:S(2)}) collective-permute-start(bf16[64,4096]{1,0:T(8,128)(2,1)S(1)} %pad_maximum_fusion.1), channel_id=1, source_target_pairs={{0,16},{4,68},{8,24},{12,76},{16,0},{20,84},{24,8},{28,92},{32,48}... | collective-permute-start | bytes 1572872 | tf_op jit(solution)/shard_map/ppermute | solution.py:40
  83.8 19.5 %collective-permute-start.22 = (bf16[128,4096]{1,0:T(8,128)(2,1)S(1)}, bf16[128,4096]{1,0:T(8,128)(2,1)S(1)}, u32[]{:S(2)}, u32[]{:S(2)}) collective-permute-start(bf16[128,4096]{1,0:T(8,128)(2,1)S(1)} %constant_dynamic-update-slice_fusion.2.refs_0_), channel_id=1, source_target_pairs={{0,32},{4,12},{8,40},{12,20},{16,48},{20,28},{24,56},{28,4},{32,64... | collective-permute-start | bytes 3145736 | tf_op jit(solution)/shard_map/ppermute | solution.py:40
  99.5 14.9 %collective-permute-start.23 = (bf16[128,4096]{1,0:T(8,128)(2,1)S(1)}, bf16[128,4096]{1,0:T(8,128)(2,1)S(1)}, u32[]{:S(2)}, u32[]{:S(2)}) collective-permute-start(bf16[128,4096]{1,0:T(8,128)(2,1)S(1)} %constant_dynamic-update-slice_fusion.7.refs_1_), channel_id=1, source_target_pairs={{0,96},{4,28},{8,104},{12,4},{16,112},{20,12},{24,120},{28,20},{32... | collective-permute-start | bytes 3145736 | tf_op jit(solution)/shard_map/ppermute | solution.py:40
  103.3 30.2 %collective-permute-start.26 = (bf16[128,4096]{1,0:T(8,128)(2,1)S(1)}, bf16[128,4096]{1,0:T(8,128)(2,1)S(1)}, u32[]{:S(2)}, u32[]{:S(2)}) collective-permute-start(bf16[128,4096]{1,0:T(8,128)(2,1)S(1)} %constant_dynamic-update-slice_fusion.2.refs_0_), channel_id=1, source_target_pairs={{0,96},{4,28},{8,104},{12,4},{16,112},{20,12},{24,120},{28,20},{32... | collective-permute-start | bytes 3145736 | tf_op jit(solution)/shard_map/ppermute | solution.py:40
  114.4 19.1 %collective-permute-start.25 = (bf16[128,4096]{1,0:T(8,128)(2,1)S(1)}, bf16[128,4096]{1,0:T(8,128)(2,1)S(1)}, u32[]{:S(2)}, u32[]{:S(2)}) collective-permute-start(bf16[128,4096]{1,0:T(8,128)(2,1)S(1)} %constant_dynamic-update-slice_fusion.7.refs_1_), channel_id=1, source_target_pairs={{0,32},{4,12},{8,40},{12,20},{16,48},{20,28},{24,56},{28,4},{32,64... | collective-permute-start | bytes 3145736 | tf_op jit(solution)/shard_map/ppermute | solution.py:40
  115.9 31.0 %collective-permute-start.28 = (bf16[128,4096]{1,0:T(8,128)(2,1)S(1)}, bf16[128,4096]{1,0:T(8,128)(2,1)S(1)}, u32[]{:S(2)}, u32[]{:S(2)}) collective-permute-start(bf16[128,4096]{1,0:T(8,128)(2,1)S(1)} %collective-permute-done.22.refs_0_), channel_id=1, source_target_pairs={{0,32},{4,12},{8,40},{12,20},{16,48},{20,28},{24,56},{28,4},{32,64... | collective-permute-start | bytes 3145736 | tf_op jit(solution)/shard_map/ppermute | solution.py:40
  119.1 27.8 %collective-permute-start.29 = (bf16[128,4096]{1,0:T(8,128)(2,1)S(1)}, bf16[128,4096]{1,0:T(8,128)(2,1)S(1)}, u32[]{:S(2)}, u32[]{:S(2)}) collective-permute-start(bf16[128,4096]{1,0:T(8,128)(2,1)S(1)} %collective-permute-done.23.refs_1_), channel_id=1, source_target_pairs={{0,96},{4,28},{8,104},{12,4},{16,112},{20,12},{24,120},{28,20},{32... | collective-permute-start | bytes 3145736 | tf_op jit(solution)/shard_map/ppermute | solution.py:40
  133.4 26.4 %collective-permute-start.24 = (bf16[128,4096]{1,0:T(8,128)(2,1)}, bf16[128,4096]{1,0:T(8,128)(2,1)}, u32[]{:S(2)}, u32[]{:S(2)}) collective-permute-start(bf16[128,4096]{1,0:T(8,128)(2,1)} %get-tuple-element.22), channel_id=1, source_target_pairs={{0,96},{4,28},{8,104},{12,4},{16,112},{20,12},{24,120},{28,20},{32... | collective-permute-start | bytes 3145736 | tf_op jit(solution)/shard_map/ppermute | solution.py:40
  133.5 13.4 %copy-start.4 = (bf16[1,448,4096]{2,1,0:T(8,128)(2,1)S(1)}, bf16[1,448,4096]{2,1,0:T(8,128)(2,1)}, u32[]{:S(2)}) copy-start(bf16[1,448,4096]{2,1,0:T(8,128)(2,1)} %param.31) | copy-start | bytes 11010052
  144.9 13.4 %copy-start.6 = (bf16[128,4096]{1,0:T(8,128)(2,1)S(1)}, bf16[128,4096]{1,0:T(8,128)(2,1)}, u32[]{:S(2)}) copy-start(bf16[128,4096]{1,0:T(8,128)(2,1)} %copy-done.5) | copy-start | bytes 3145732
  144.9 27.3 %collective-permute-start.27 = (bf16[128,4096]{1,0:T(8,128)(2,1)}, bf16[128,4096]{1,0:T(8,128)(2,1)S(1)}, u32[]{:S(2)}, u32[]{:S(2)}) collective-permute-start(bf16[128,4096]{1,0:T(8,128)(2,1)} %get-tuple-element.23), channel_id=1, source_target_pairs={{0,32},{4,12},{8,40},{12,20},{16,48},{20,28},{24,56},{28,4},{32,64... | collective-permute-start | bytes 3145736 | tf_op jit(solution)/shard_map/ppermute | solution.py:40
  156.8 18.4 %collective-permute-start.30 = (bf16[128,4096]{1,0:T(8,128)(2,1)S(1)}, bf16[128,4096]{1,0:T(8,128)(2,1)S(1)}, u32[]{:S(2)}, u32[]{:S(2)}) collective-permute-start(bf16[128,4096]{1,0:T(8,128)(2,1)S(1)} %get-tuple-element.24), channel_id=1, source_target_pairs={{0,64},{4,20},{8,72},{12,28},{16,80},{20,4},{24,88},{28,12},{32,96... | collective-permute-start | bytes 3145736 | tf_op jit(solution)/shard_map/ppermute | solution.py:40
  157.8 25.4 %collective-permute-start.33 = (bf16[128,4096]{1,0:T(8,128)(2,1)S(1)}, bf16[128,4096]{1,0:T(8,128)(2,1)S(1)}, u32[]{:S(2)}, u32[]{:S(2)}) collective-permute-start(bf16[128,4096]{1,0:T(8,128)(2,1)S(1)} %get-tuple-element.27), channel_id=1, source_target_pairs={{0,32},{4,12},{8,40},{12,20},{16,48},{20,28},{24,56},{28,4},{32,64... | collective-permute-start | bytes 3145736 | tf_op jit(solution)/shard_map/ppermute | solution.py:40
  158.3 31.7 %collective-permute-start.32 = (bf16[128,4096]{1,0:T(8,128)(2,1)S(1)}, bf16[128,4096]{1,0:T(8,128)(2,1)S(1)}, u32[]{:S(2)}, u32[]{:S(2)}) collective-permute-start(bf16[128,4096]{1,0:T(8,128)(2,1)S(1)} %copy-done.6), channel_id=1, source_target_pairs={{0,96},{4,28},{8,104},{12,4},{16,112},{20,12},{24,120},{28,20},{32... | collective-permute-start | bytes 3145736 | tf_op jit(solution)/shard_map/ppermute | solution.py:40
  159.9 46.8 %collective-permute-start.34 = (bf16[128,4096]{1,0:T(8,128)(2,1)S(1)}, bf16[128,4096]{1,0:T(8,128)(2,1)S(1)}, u32[]{:S(2)}, u32[]{:S(2)}) collective-permute-start(bf16[128,4096]{1,0:T(8,128)(2,1)S(1)} %get-tuple-element.28), channel_id=1, source_target_pairs={{0,64},{4,20},{8,72},{12,28},{16,80},{20,4},{24,88},{28,12},{32,96... | collective-permute-start | bytes 3145736 | tf_op jit(solution)/shard_map/ppermute | solution.py:40
  177.1 31.7 %collective-permute-start.31 = (bf16[64,4096]{1,0:T(8,128)(2,1)S(1)}, bf16[64,4096]{1,0:T(8,128)(2,1)S(1)}, u32[]{:S(2)}, u32[]{:S(2)}) collective-permute-start(bf16[64,4096]{1,0:T(8,128)(2,1)S(1)} %slice.53), channel_id=1, source_target_pairs={{0,24},{4,100},{8,0},{12,108},{16,8},{20,116},{24,16},{28,124},{32... | collective-permute-start | bytes 1572872 | tf_op jit(solution)/shard_map/ppermute | solution.py:40
  208.4 16.2 %collective-permute-start.35 = (bf16[64,4096]{1,0:T(8,128)(2,1)}, bf16[64,4096]{1,0:T(8,128)(2,1)S(1)}, u32[]{:S(2)}, u32[]{:S(2)}) collective-permute-start(bf16[64,4096]{1,0:T(8,128)(2,1)} %get-tuple-element.31), channel_id=1, source_target_pairs={{0,8},{4,36},{8,16},{12,44},{16,24},{20,52},{24,0},{28,60},{32,40}... | collective-permute-start | bytes 1572872 | tf_op jit(solution)/shard_map/ppermute | solution.py:40
  208.4 16.2 %collective-permute-start.36 = (bf16[64,4096]{1,0:T(8,128)(2,1)}, bf16[64,4096]{1,0:T(8,128)(2,1)S(1)}, u32[]{:S(2)}, u32[]{:S(2)}) collective-permute-start(bf16[64,4096]{1,0:T(8,128)(2,1)} %get-tuple-element.32), channel_id=1, source_target_pairs={{0,16},{4,68},{8,24},{12,76},{16,0},{20,84},{24,8},{28,92},{32,48}... | collective-permute-start | bytes 1572872 | tf_op jit(solution)/shard_map/ppermute | solution.py:40
  224.9 7.7 %collective-permute-start.39 = (bf16[16,4096]{1,0:T(8,128)(2,1)S(1)}, bf16[16,4096]{1,0:T(8,128)(2,1)S(1)}, u32[]{:S(2)}, u32[]{:S(2)}) collective-permute-start(bf16[16,4096]{1,0:T(8,128)(2,1)S(1)} %get-tuple-element.34), channel_id=1, source_target_pairs={{0,1},{1,2},{2,3},{3,0},{4,5},{5,6},{6,7},{7,4},{8,9},{9,10},{10,1... | collective-permute-start | bytes 393224 | tf_op jit(solution)/shard_map/ppermute | solution.py:48
  225.0 7.6 %collective-permute-start.38 = (bf16[16,4096]{1,0:T(8,128)(2,1)S(1)}, bf16[16,4096]{1,0:T(8,128)(2,1)S(1)}, u32[]{:S(2)}, u32[]{:S(2)}) collective-permute-start(bf16[16,4096]{1,0:T(8,128)(2,1)S(1)} %get-tuple-element.35), channel_id=1, source_target_pairs={{0,2},{1,3},{2,0},{3,1},{4,6},{5,7},{6,4},{7,5},{8,10},{9,11},{10,... | collective-permute-start | bytes 393224 | tf_op jit(solution)/shard_map/ppermute | solution.py:48
  227.2 6.2 %collective-permute-start.37 = (bf16[16,4096]{1,0:T(8,128)(2,1)S(1)}, bf16[16,4096]{1,0:T(8,128)(2,1)S(1)}, u32[]{:S(2)}, u32[]{:S(2)}) collective-permute-start(bf16[16,4096]{1,0:T(8,128)(2,1)S(1)} %get-tuple-element.36), channel_id=1, source_target_pairs={{0,3},{1,0},{2,1},{3,2},{4,7},{5,4},{6,5},{7,6},{8,11},{9,8},{10,9... | collective-permute-start | bytes 393224 | tf_op jit(solution)/shard_map/ppermute | solution.py:48
  (8 other events, 32.7 us)

commit v4 on v3

--- a/solution.py
+++ b/solution.py
@@ -149,8 +149,8 @@
 def expert_rows(pieces, own, other):
     hid, depth = own[0].shape
     width = own[2].shape[1]
-    chunks = 4
-    deep, wide = depth // chunks, width // chunks
+    chunks, panels = 4, 4
+    deep, wide = depth // chunks, width // panels
     sizes = [p.shape[0] for p in pieces]
     rows = sum(sizes)
     count = len(pieces)
@@ -186,7 +186,7 @@
         for k in range(chunks):
             for copy in first_copies(k):
                 copy.start()
-        for n in range(chunks):
+        for n in range(panels):
             for copy in last_copies(n):
                 copy.start()
         sums[...] = jnp.zeros_like(sums)
@@ -199,7 +199,7 @@
 
         hidden[...] = (jax.nn.silu(sums[:, : 2 * hid]) * sums[:, 2 * hid :]).astype(bf16)
 
-        @pl.loop(0, chunks)
+        @pl.loop(0, panels)
         def _(n):
             for copy in last_copies(n):
                 copy.wait()
@@ -207,7 +207,7 @@
             for copy in out_copies(n):
                 copy.start()
 
-        for n in range(chunks):
+        for n in range(panels):
             for copy in out_copies(n):
                 copy.wait()
 
@@ -220,14 +220,14 @@
         scratch_shapes=[
             pltpu.VMEM((chunks, rows, deep), bf16),
             pltpu.VMEM((chunks, 4 * hid, deep), bf16),
-            pltpu.VMEM((chunks, 2 * hid, wide), bf16),
+            pltpu.VMEM((panels, 2 * hid, wide), bf16),
             pltpu.VMEM((rows, 4 * hid), f32),
             pltpu.VMEM((rows, 2 * hid), bf16),
-            pltpu.VMEM((chunks, rows, wide), bf16),
+            pltpu.VMEM((panels, rows, wide), bf16),
             pltpu.SemaphoreType.DMA((chunks, count)),
             pltpu.SemaphoreType.DMA((chunks, 4)),
-            pltpu.SemaphoreType.DMA((chunks, 2)),
-            pltpu.SemaphoreType.DMA((chunks, count)),
+            pltpu.SemaphoreType.DMA((panels, 2)),
+            pltpu.SemaphoreType.DMA((panels, count)),
         ],
         cost_estimate=pl.CostEstimate(
             flops=12 * rows * depth * hid, transcendentals=2 * rows * hid, bytes_accessed=12 * depth * hid
@@ -312,8 +312,10 @@
 
     own = (w_gate[0].T, w_up[0].T, w_down[0])
     other = tuple(swap(w) for w in own)
-    n0 = join(rows, shift(rows, 1, 1))
-    n1 = join(shift(rows, 1, -1), shift(rows, 1, 2))
+    half = rows.shape[0] // 2
+    beside0, beside1 = shift(rows, 1, 1), shift(rows, 1, -1)
+    n0 = join(rows, beside0)
+    n1 = join(beside1, shift(beside0[:half], 1, 1), shift(beside1[half:], 1, -1))
     l0, r0 = shift(n0, 2, 1), shift(n0, 2, -1)
     r1, l1 = shift(n1, 2, -1), shift(n1, 2, 1)
     f0, f1 = shift(l0, 2, 1), shift(r1, 2, -1)
@@ -323,13 +325,14 @@
     l1, r0 = expert_rows((l1, r0), own, other)
     f0, f1 = expert_rows((f0, f1), own, other)
 
-    u0, v1 = shift(l0, 2, -1), shift(r1, 2, 1)
     u1, v0 = shift(l1, 2, -1), shift(r0, 2, 1)
-    f0, f1 = shift(f0, 2, 2), shift(f1, 2, 2)
-    n0, n1 = total(n0, u0, v0, f0), total(n1, u1, v1, f1)
+    q0, q1 = shift(f0, 2, -1), shift(f1, 2, 1)
+    u0, v1 = shift(total(l0, q0), 2, -1), shift(total(r1, q1), 2, 1)
+    level = lax.ppermute(v1[:16, :128], "ctx", [(2 * i, 2 * i + 1) for i in range(16)])
+    n0, n1 = total(n0, u0, v0), total(n1, u1, v1)
     part = rows.shape[0]
     back = (shift(n0[part:], 1, -1), shift(n1[:part], 1, 1), shift(n1[part:], 1, 2))
-    own_rows = total(n0[:part], *back)
+    own_rows = total(n0[:part] + jnp.max(level) * 0, *back)
 
     r0, r1, r2, r3 = (own_rows[i * slot_count : (i + 1) * slot_count] for i in range(4))
     returned = join(r0, shift_exp(r1, 3), shift_exp(r2, 2), shift_exp(r3, 1))

time: 235 us -> 231 us (0.983)
  the two profiles are of different devices: /device:TPU:32 before, /device:TPU:0 now
where the time goes in v4:
time: 231 us
  waiting for transfers between devices  95.8 us (41%)
  starting transfers between devices  66.8 us (29%)
  Pallas kernels  50.4 us (22%)
  local copies, waits for them, and re-layouts  7.61 us (3%)
  other arithmetic  7.09 us (3%)
    ppermute x25, waiting for transfers between devices, shift(): return lax.ppermute(a, 'ctx', RINGS[phase, step])  74.3 us
    ppermute x25, starting transfers between devices, shift(): return lax.ppermute(a, 'ctx', RINGS[phase, step])  44.5 us
    pallas_call x4, Pallas kernels, expert_rows(): pl.pallas_call(kernel, out_shape=tuple((jax.ShapeDtypeStruct((size, width...  39.2 us
    ppermute x9, starting transfers between devices, shift_exp(): return lax.ppermute(a, 'exp', [(i, (i + step) % 4) for i in range(4)])  20.4 us
    ppermute x9, waiting for transfers between devices, shift_exp(): return lax.ppermute(a, 'exp', [(i, (i + step) % 4) for i in range(4)])  18.8 us
    pallas_call x1, Pallas kernels, attend(): pl.pallas_call(kernel, out_shape=tuple((jax.ShapeDtypeStruct((sub, width)...  11.2 us
  transfers between devices with their start and end apart: 42, of which 22 were waited for; matrix products, arithmetic and copies ran while one was open for 4% of the time, Pallas kernels for 17%

profile of v4, /device:TPU:0, one launch (start us, length us, event | category | flops | bytes accessed | tf_op | source)
XLA Modules:
  0.0 230.5 jit_solution(3412829072971550899)
XLA Ops:
  1.7 1.6 collective-permute-start
  3.3 1.6 collective-permute-start.1
  5.0 1.9 collective-permute-start.2
  9.5 1.9 collective-permute-done.2
  11.5 2.1 collective-permute-start.4
  13.6 2.2 collective-permute-start.6
  15.8 1.8 collective-permute-start.8
  18.8 4.0 %collective-permute-done.4.refs_2_ = bf16[512,512]{1,0:T(8,128)(2,1)S(1)} collective-permute-done((bf16[512,512]{1,0:T(8,128)(2,1)S(1)}, bf16[512,512]{1,0:T(8,128)(2,1)S(1)}, u32[]{:S(2)}, u32[]{:S(2)}) %collective-permute-start.4) | collective-permute-done | bytes 524320 | tf_op jit(solution)/shard_map/ppermute | solution.py:40
  22.9 5.3 %collective-permute-done.6.refs_4_ = bf16[512,512]{1,0:T(8,128)(2,1)S(1)} collective-permute-done((bf16[512,512]{1,0:T(8,128)(2,1)S(1)}, bf16[512,512]{1,0:T(8,128)(2,1)S(1)}, u32[]{:S(2)}, u32[]{:S(2)}) %collective-permute-start.6) | collective-permute-done | bytes 524320 | tf_op jit(solution)/shard_map/ppermute | solution.py:40
  28.1 1.8 collective-permute-done.8.refs_6_
  30.2 1.8 collective-permute-done.9.refs_7_
  33.1 11.2 %attend.1 = (f32[32,4096]{1,0:T(8,128)S(1)}, bf16[32,4096]{1,0:T(8,128)(2,1)S(1)}, bf16[32,4096]{1,0:T(8,128)(2,1)S(1)}, bf16[32,4096]{1,0:T(8,128)(2,1)S(1)}) custom-call(s32[1]{0:T(128)} %bitcast.mine_ref, bf16[128,1024]{1,0:T(8,128)(2,1)S(1)} %copy-done.4, s32[128,128]{1,0:T(8,128)S(1)} %broadcast_in_dim.125.qpos_ref, ...), custom_call_target="tpu_custom_call" | custom-call | flops 4294967296 | bytes 4194304 | tf_op jit(solution)/shard_map/attend/pallas_call | solution.py:129
  44.2 3.3 %collective-permute-start.10 = (bf16[32,4096]{1,0:T(8,128)(2,1)S(1)}, bf16[32,4096]{1,0:T(8,128)(2,1)S(1)}, u32[]{:S(2)}, u32[]{:S(2)}) collective-permute-start(bf16[32,4096]{1,0:T(8,128)(2,1)S(1)} %get-tuple-element.18), channel_id=1, source_target_pairs={{0,2},{1,3},{2,0},{3,1},{4,6},{5,7},{6,4},{7,5},{8,10},{9,11},{10,... | collective-permute-start | bytes 786440 | tf_op jit(solution)/shard_map/ppermute | solution.py:48
  48.2 2.6 %collective-permute-start.12 = (bf16[32,4096]{1,0:T(8,128)(2,1)S(1)}, bf16[32,4096]{1,0:T(8,128)(2,1)S(1)}, u32[]{:S(2)}, u32[]{:S(2)}) collective-permute-start(bf16[32,4096]{1,0:T(8,128)(2,1)S(1)} %get-tuple-element.20), channel_id=1, source_target_pairs={{0,3},{1,0},{2,1},{3,2},{4,7},{5,4},{6,5},{7,6},{8,11},{9,8},{10,9... | collective-permute-start | bytes 786440 | tf_op jit(solution)/shard_map/ppermute | solution.py:48
  51.2 3.8 %collective-permute-done.10 = bf16[32,4096]{1,0:T(8,128)(2,1)S(1)} collective-permute-done((bf16[32,4096]{1,0:T(8,128)(2,1)S(1)}, bf16[32,4096]{1,0:T(8,128)(2,1)S(1)}, u32[]{:S(2)}, u32[]{:S(2)}) %collective-permute-start.10) | collective-permute-done | bytes 262176 | tf_op jit(solution)/shard_map/ppermute | solution.py:48
  55.0 4.7 %collective-permute-done.11 = bf16[32,4096]{1,0:T(8,128)(2,1)S(1)} collective-permute-done((bf16[32,4096]{1,0:T(8,128)(2,1)S(1)}, bf16[32,4096]{1,0:T(8,128)(2,1)S(1)}, u32[]{:S(2)}, u32[]{:S(2)}) %collective-permute-start.11) | collective-permute-done | bytes 262176 | tf_op jit(solution)/shard_map/ppermute | solution.py:48
  60.9 1.4 collective-permute-start.13
  62.3 2.7 %collective-permute-start.14 = (bf16[16,4096]{1,0:T(8,128)(2,1)S(1)}, bf16[16,4096]{1,0:T(8,128)(2,1)S(1)}, u32[]{:S(2)}, u32[]{:S(2)}) collective-permute-start(bf16[16,4096]{1,0:T(8,128)(2,1)S(1)} %get-tuple-element.40), channel_id=1, source_target_pairs={{0,2},{1,3},{2,0},{3,1},{4,6},{5,7},{6,4},{7,5},{8,10},{9,11},{10,... | collective-permute-start | bytes 393224 | tf_op jit(solution)/shard_map/ppermute | solution.py:48
  67.3 4.0 %collective-permute-done.14 = bf16[16,4096]{1,0:T(8,128)(2,1)S(1)} collective-permute-done((bf16[16,4096]{1,0:T(8,128)(2,1)S(1)}, bf16[16,4096]{1,0:T(8,128)(2,1)S(1)}, u32[]{:S(2)}, u32[]{:S(2)}) %collective-permute-start.14) | collective-permute-done | bytes 131104 | tf_op jit(solution)/shard_map/ppermute | solution.py:48
  71.3 1.6 collective-permute-start.17
  73.5 9.8 %collective-permute-done.16 = bf16[64,4096]{1,0:T(8,128)(2,1)S(1)} collective-permute-done((bf16[64,4096]{1,0:T(8,128)(2,1)S(1)}, bf16[64,4096]{1,0:T(8,128)(2,1)S(1)}, u32[]{:S(2)}, u32[]{:S(2)}) %collective-permute-start.16) | collective-permute-done | bytes 524320 | tf_op jit(solution)/shard_map/ppermute | solution.py:40
  83.5 3.3 %collective-permute-start.19 = (bf16[32,4096]{1,0:T(8,128)(2,1)S(1)}, bf16[32,4096]{1,0:T(8,128)(2,1)S(1)}, u32[]{:S(2)}, u32[]{:S(2)}) collective-permute-start(bf16[32,4096]{1,0:T(8,128)(2,1)S(1)} %slice.65), channel_id=1, source_target_pairs={{0,24},{4,100},{8,0},{12,108},{16,8},{20,116},{24,16},{28,124},{32... | collective-permute-start | bytes 786440 | tf_op jit(solution)/shard_map/ppermute | solution.py:40
  86.8 4.2 %collective-permute-done.18 = bf16[32,4096]{1,0:T(8,128)(2,1)S(1)} collective-permute-done((bf16[32,4096]{1,0:T(8,128)(2,1)S(1)}, bf16[32,4096]{1,0:T(8,128)(2,1)S(1)}, u32[]{:S(2)}, u32[]{:S(2)}) %collective-permute-start.18) | collective-permute-done | bytes 262176 | tf_op jit(solution)/shard_map/ppermute | solution.py:40
  91.0 2.0 collective-permute-start.23
  93.1 1.7 collective-permute-start.24
  94.7 12.6 %collective-permute-done.23.refs_0_ = bf16[128,4096]{1,0:T(8,128)(2,1)S(1)} collective-permute-done((bf16[128,4096]{1,0:T(8,128)(2,1)S(1)}, bf16[128,4096]{1,0:T(8,128)(2,1)S(1)}, u32[]{:S(2)}, u32[]{:S(2)}) %collective-permute-start.23) | collective-permute-done | bytes 1048608 | tf_op jit(solution)/shard_map/ppermute | solution.py:40
  107.9 2.8 %collective-permute-start.26 = (bf16[128,4096]{1,0:T(8,128)(2,1)S(1)}, bf16[128,4096]{1,0:T(8,128)(2,1)S(1)}, u32[]{:S(2)}, u32[]{:S(2)}) collective-permute-start(bf16[128,4096]{1,0:T(8,128)(2,1)S(1)} %collective-permute-done.24.refs_1_), channel_id=1, source_target_pairs={{0,96},{4,28},{8,104},{12,4},{16,112},{20,12},{24,120},{28,20},{32... | collective-permute-start | bytes 3145736 | tf_op jit(solution)/shard_map/ppermute | solution.py:40
  112.8 10.6 %collective-permute-done.25.refs_0_ = bf16[128,4096]{1,0:T(8,128)(2,1)S(1)} collective-permute-done((bf16[128,4096]{1,0:T(8,128)(2,1)S(1)}, bf16[128,4096]{1,0:T(8,128)(2,1)S(1)}, u32[]{:S(2)}, u32[]{:S(2)}) %collective-permute-start.25) | collective-permute-done | bytes 1048608 | tf_op jit(solution)/shard_map/ppermute | solution.py:40
  123.4 2.0 copy-done.3
  125.5 9.8 %expert_rows.6 = (bf16[128,4096]{1,0:T(8,128)(2,1)S(1)}, bf16[128,4096]{1,0:T(8,128)(2,1)S(1)}) custom-call(bf16[128,4096]{1,0:T(8,128)(2,1)S(1)} %collective-permute-done.25.refs_0_, bf16[128,4096]{1,0:T(8,128)(2,1)S(1)} %collective-permute-done.26.refs_1_, bf16[448,4096]{1,0:T(8,128)(2,1)S(1)} %bitcast.29, bf16[448,4096]{1,0:T(8,128)(2,1)S(1)} %bitcast.34, ...), custom_call_target="tpu_custom_call" | custom-call | flops 5637144576 | bytes 22020096 | tf_op jit(solution)/shard_map/expert_rows/pallas_call | solution.py:215
  135.3 3.4 %collective-permute-start.27 = (bf16[128,4096]{1,0:T(8,128)(2,1)S(1)}, bf16[128,4096]{1,0:T(8,128)(2,1)S(1)}, u32[]{:S(2)}, u32[]{:S(2)}) collective-permute-start(bf16[128,4096]{1,0:T(8,128)(2,1)S(1)} %get-tuple-element.23), channel_id=1, source_target_pairs={{0,96},{4,28},{8,104},{12,4},{16,112},{20,12},{24,120},{28,20},{32... | collective-permute-start | bytes 3145736 | tf_op jit(solution)/shard_map/ppermute | solution.py:40
  138.7 9.8 %expert_rows.7 = (bf16[128,4096]{1,0:T(8,128)(2,1)S(1)}, bf16[128,4096]{1,0:T(8,128)(2,1)S(1)}) custom-call(bf16[128,4096]{1,0:T(8,128)(2,1)S(1)} %collective-permute-done.29.refs_0_, bf16[128,4096]{1,0:T(8,128)(2,1)S(1)} %collective-permute-done.30.refs_1_, bf16[448,4096]{1,0:T(8,128)(2,1)S(1)} %bitcast.30, bf16[448,4096]{1,0:T(8,128)(2,1)S(1)} %bitcast.35, ...), custom_call_target="tpu_custom_call" | custom-call | flops 5637144576 | bytes 22020096 | tf_op jit(solution)/shard_map/expert_rows/pallas_call | solution.py:215
  148.6 3.2 %collective-permute-start.36 = (bf16[128,4096]{1,0:T(8,128)(2,1)S(1)}, bf16[128,4096]{1,0:T(8,128)(2,1)S(1)}, u32[]{:S(2)}, u32[]{:S(2)}) collective-permute-start(bf16[128,4096]{1,0:T(8,128)(2,1)S(1)} %get-tuple-element.28), channel_id=1, source_target_pairs={{0,96},{4,28},{8,104},{12,4},{16,112},{20,12},{24,120},{28,20},{32... | collective-permute-start | bytes 3145736 | tf_op jit(solution)/shard_map/ppermute | solution.py:40
  151.8 9.8 %expert_rows.5 = (bf16[128,4096]{1,0:T(8,128)(2,1)S(1)}, bf16[128,4096]{1,0:T(8,128)(2,1)S(1)}) custom-call(bf16[128,4096]{1,0:T(8,128)(2,1)S(1)} %collective-permute-done.23.refs_0_, bf16[128,4096]{1,0:T(8,128)(2,1)S(1)} %collective-permute-done.24.refs_1_, bf16[448,4096]{1,0:T(8,128)(2,1)S(1)} %bitcast.31, bf16[448,4096]{1,0:T(8,128)(2,1)S(1)} %bitcast.36, ...), custom_call_target="tpu_custom_call" | custom-call | flops 5637144576 | bytes 22020096 | tf_op jit(solution)/shard_map/expert_rows/pallas_call | solution.py:215
  161.9 3.3 %collective-permute-start.28 = (bf16[128,4096]{1,0:T(8,128)(2,1)S(1)}, bf16[128,4096]{1,0:T(8,128)(2,1)S(1)}, u32[]{:S(2)}, u32[]{:S(2)}) collective-permute-start(bf16[128,4096]{1,0:T(8,128)(2,1)S(1)} %add_convert_fusion.3), channel_id=1, source_target_pairs={{0,96},{4,28},{8,104},{12,4},{16,112},{20,12},{24,120},{28,20},{32... | collective-permute-start | bytes 3145736 | tf_op jit(solution)/shard_map/ppermute | solution.py:40
  165.2 10.6 %collective-permute-done.32 = bf16[128,4096]{1,0:T(8,128)(2,1)S(1)} collective-permute-done((bf16[128,4096]{1,0:T(8,128)(2,1)S(1)}, bf16[128,4096]{1,0:T(8,128)(2,1)S(1)}, u32[]{:S(2)}, u32[]{:S(2)}) %collective-permute-start.32) | collective-permute-done | bytes 1048608 | tf_op jit(solution)/shard_map/ppermute | solution.py:40
  176.2 9.8 %expert_rows.4 = (bf16[128,4096]{1,0:T(8,128)(2,1)S(1)}, bf16[128,4096]{1,0:T(8,128)(2,1)S(1)}) custom-call(bf16[128,4096]{1,0:T(8,128)(2,1)S(1)} %constant_dynamic-update-slice_fusion.2.refs_0_, bf16[128,4096]{1,0:T(8,128)(2,1)S(1)} %constant_dynamic-update-slice_fusion.7.refs_1_, bf16[448,4096]{1,0:T(8,128)(2,1)S(1)} %bitcast.32, ...), custom_call_target="tpu_custom_call" | custom-call | flops 5637144576 | bytes 22020096 | tf_op jit(solution)/shard_map/expert_rows/pallas_call | solution.py:215
  186.5 2.3 %collective-permute-start.35 = (bf16[64,4096]{1,0:T(8,128)(2,1)S(1)}, bf16[64,4096]{1,0:T(8,128)(2,1)S(1)}, u32[]{:S(2)}, u32[]{:S(2)}) collective-permute-start(bf16[64,4096]{1,0:T(8,128)(2,1)S(1)} %slice.68), channel_id=1, source_target_pairs={{0,24},{4,100},{8,0},{12,108},{16,8},{20,116},{24,16},{28,124},{32... | collective-permute-start | bytes 1572872 | tf_op jit(solution)/shard_map/ppermute | solution.py:40
  188.9 4.0 %collective-permute-done.33 = bf16[128,4096]{1,0:T(8,128)(2,1)S(1)} collective-permute-done((bf16[128,4096]{1,0:T(8,128)(2,1)S(1)}, bf16[128,4096]{1,0:T(8,128)(2,1)S(1)}, u32[]{:S(2)}, u32[]{:S(2)}) %collective-permute-start.33) | collective-permute-done | bytes 1048608 | tf_op jit(solution)/shard_map/ppermute | solution.py:40
  194.4 6.5 %collective-permute-start.38 = (bf16[64,4096]{1,0:T(8,128)(2,1)}, bf16[64,4096]{1,0:T(8,128)(2,1)}, u32[]{:S(2)}, u32[]{:S(2)}) collective-permute-start(bf16[64,4096]{1,0:T(8,128)(2,1)} %get-tuple-element.32), channel_id=1, source_target_pairs={{0,16},{4,68},{8,24},{12,76},{16,0},{20,84},{24,8},{28,92},{32,48}... | collective-permute-start | bytes 1572872 | tf_op jit(solution)/shard_map/ppermute | solution.py:40
  204.7 2.2 collective-permute-done.37
  206.9 7.1 %collective-permute-done.38 = bf16[64,4096]{1,0:T(8,128)(2,1)} collective-permute-done((bf16[64,4096]{1,0:T(8,128)(2,1)}, bf16[64,4096]{1,0:T(8,128)(2,1)}, u32[]{:S(2)}, u32[]{:S(2)}) %collective-permute-start.38) | collective-permute-done | bytes 524320 | tf_op jit(solution)/shard_map/ppermute | solution.py:40
  214.0 1.5 add_convert_fusion.4
  215.5 1.6 collective-permute-start.39
  217.1 6.2 %collective-permute-start.40 = (bf16[16,4096]{1,0:T(8,128)(2,1)S(1)}, bf16[16,4096]{1,0:T(8,128)(2,1)S(1)}, u32[]{:S(2)}, u32[]{:S(2)}) collective-permute-start(bf16[16,4096]{1,0:T(8,128)(2,1)S(1)} %get-tuple-element.35), channel_id=1, source_target_pairs={{0,2},{1,3},{2,0},{3,1},{4,6},{5,7},{6,4},{7,5},{8,10},{9,11},{10,... | collective-permute-start | bytes 393224 | tf_op jit(solution)/shard_map/ppermute | solution.py:48
  223.3 1.3 collective-permute-start.41
  224.8 1.5 collective-permute-done.40
  226.3 3.2 %collective-permute-done.41 = bf16[16,4096]{1,0:T(8,128)(2,1)S(1)} collective-permute-done((bf16[16,4096]{1,0:T(8,128)(2,1)S(1)}, bf16[16,4096]{1,0:T(8,128)(2,1)S(1)}, u32[]{:S(2)}, u32[]{:S(2)}) %collective-permute-start.41) | collective-permute-done | bytes 131104 | tf_op jit(solution)/shard_map/ppermute | solution.py:48
  (144 shorter events, 21.7 us)
Async XLA Ops:
  0.0 200.9 %copy-start = (f32[4096,4]{0,1:T(4,128)S(1)}, f32[4096,4]{0,1:T(4,128)}, u32[]{:S(2)}) copy-start(f32[4096,4]{0,1:T(4,128)} %param.27) | copy-start | bytes 196612
  1.7 7.8 %collective-permute-start = (bf16[128,512]{1,0:T(8,128)(2,1)S(1)}, bf16[128,512]{1,0:T(8,128)(2,1)S(1)}, u32[]{:S(2)}, u32[]{:S(2)}) collective-permute-start(bf16[128,512]{1,0:T(8,128)(2,1)S(1)} %constant_dynamic-update-slice_fusion), channel_id=1, source_target_pairs={{0,8},{4,36},{8,16},{12,44},{16,24},{20,52},{24,0},{28,60},{32,40}... | collective-permute-start | bytes 393224 | tf_op jit(solution)/shard_map/ppermute | solution.py:40
  3.3 6.2 %collective-permute-start.1 = (bf16[128,512]{1,0:T(8,128)(2,1)S(1)}, bf16[128,512]{1,0:T(8,128)(2,1)S(1)}, u32[]{:S(2)}, u32[]{:S(2)}) collective-permute-start(bf16[128,512]{1,0:T(8,128)(2,1)S(1)} %constant_dynamic-update-slice_fusion), channel_id=1, source_target_pairs={{0,24},{4,100},{8,0},{12,108},{16,8},{20,116},{24,16},{28,124},{32... | collective-permute-start | bytes 393224 | tf_op jit(solution)/shard_map/ppermute | solution.py:40
  5.0 6.5 %collective-permute-start.2 = (bf16[128,512]{1,0:T(8,128)(2,1)S(1)}, bf16[128,512]{1,0:T(8,128)(2,1)S(1)}, u32[]{:S(2)}, u32[]{:S(2)}) collective-permute-start(bf16[128,512]{1,0:T(8,128)(2,1)S(1)} %constant_dynamic-update-slice_fusion), channel_id=1, source_target_pairs={{0,16},{4,68},{8,24},{12,76},{16,0},{20,84},{24,8},{28,92},{32,48}... | collective-permute-start | bytes 393224 | tf_op jit(solution)/shard_map/ppermute | solution.py:40
  11.5 20.6 %copy-start.7 = (bf16[512,512]{1,0:T(8,128)(2,1)}, bf16[512,512]{1,0:T(8,128)(2,1)S(1)}, u32[]{:S(2)}) copy-start(bf16[512,512]{1,0:T(8,128)(2,1)S(1)} %pad_maximum_fusion.refs_0_) | copy-start | bytes 1572868
  11.5 11.4 %collective-permute-start.4 = (bf16[512,512]{1,0:T(8,128)(2,1)S(1)}, bf16[512,512]{1,0:T(8,128)(2,1)S(1)}, u32[]{:S(2)}, u32[]{:S(2)}) collective-permute-start(bf16[512,512]{1,0:T(8,128)(2,1)S(1)} %pad_maximum_fusion.refs_0_), channel_id=1, source_target_pairs={{0,32},{4,12},{8,40},{12,20},{16,48},{20,28},{24,56},{28,4},{32,64... | collective-permute-start | bytes 1572872 | tf_op jit(solution)/shard_map/ppermute | solution.py:40
  13.6 14.6 %collective-permute-start.6 = (bf16[512,512]{1,0:T(8,128)(2,1)S(1)}, bf16[512,512]{1,0:T(8,128)(2,1)S(1)}, u32[]{:S(2)}, u32[]{:S(2)}) collective-permute-start(bf16[512,512]{1,0:T(8,128)(2,1)S(1)} %pad_maximum_fusion.refs_0_), channel_id=1, source_target_pairs={{0,96},{4,28},{8,104},{12,4},{16,112},{20,12},{24,120},{28,20},{32... | collective-permute-start | bytes 1572872 | tf_op jit(solution)/shard_map/ppermute | solution.py:40
  15.8 14.2 %collective-permute-start.8 = (bf16[512,512]{1,0:T(8,128)(2,1)S(1)}, bf16[512,512]{1,0:T(8,128)(2,1)S(1)}, u32[]{:S(2)}, u32[]{:S(2)}) collective-permute-start(bf16[512,512]{1,0:T(8,128)(2,1)S(1)} %pad_maximum_fusion.refs_0_), channel_id=1, source_target_pairs={{0,64},{4,20},{8,72},{12,28},{16,80},{20,4},{24,88},{28,12},{32,96... | collective-permute-start | bytes 1572872 | tf_op jit(solution)/shard_map/ppermute | solution.py:40
  18.7 11.4 %collective-permute-start.3 = (bf16[512,512]{1,0:T(8,128)(2,1)S(1)}, bf16[512,512]{1,0:T(8,128)(2,1)S(1)}, u32[]{:S(2)}, u32[]{:S(2)}) collective-permute-start(bf16[512,512]{1,0:T(8,128)(2,1)S(1)} %pad_maximum_fusion.refs_0_), channel_id=1, source_target_pairs={{0,4},{4,0},{8,12},{12,8},{16,20},{20,16},{24,28},{28,24},{32,36},... | collective-permute-start | bytes 1572872 | tf_op jit(solution)/shard_map/ppermute | solution.py:44
  22.9 7.3 %collective-permute-start.5 = (bf16[512,512]{1,0:T(8,128)(2,1)S(1)}, bf16[512,512]{1,0:T(8,128)(2,1)}, u32[]{:S(2)}, u32[]{:S(2)}) collective-permute-start(bf16[512,512]{1,0:T(8,128)(2,1)S(1)} %collective-permute-done.4.refs_2_), channel_id=1, source_target_pairs={{0,4},{4,0},{8,12},{12,8},{16,20},{20,16},{24,28},{28,24},{32,36},... | collective-permute-start | bytes 1572872 | tf_op jit(solution)/shard_map/ppermute | solution.py:44
  28.1 2.0 collective-permute-start.7
  29.9 2.0 collective-permute-start.9
  33.1 17.7 %copy-start.10 = (s32[32,2]{0,1:T(2,128)S(1)}, s32[32,2]{0,1:T(2,128)}, u32[]{:S(2)}) copy-start(s32[32,2]{0,1:T(2,128)} %param.28) | copy-start | bytes 772
  33.1 27.1 %copy-start.8 = (bf16[32,4096]{1,0:T(8,128)(2,1)S(1)}, bf16[32,4096]{1,0:T(8,128)(2,1)}, u32[]{:S(2)}) copy-start(bf16[32,4096]{1,0:T(8,128)(2,1)} %param.23) | copy-start | bytes 786436
  33.1 27.4 %copy-start.9 = (f32[4096]{0:T(1024)S(1)}, f32[4096]{0:T(1024)}, u32[]{:S(2)}) copy-start(f32[4096]{0:T(1024)} %param.26) | copy-start | bytes 49156
  44.2 10.8 %collective-permute-start.10 = (bf16[32,4096]{1,0:T(8,128)(2,1)S(1)}, bf16[32,4096]{1,0:T(8,128)(2,1)S(1)}, u32[]{:S(2)}, u32[]{:S(2)}) collective-permute-start(bf16[32,4096]{1,0:T(8,128)(2,1)S(1)} %get-tuple-element.18), channel_id=1, source_target_pairs={{0,2},{1,3},{2,0},{3,1},{4,6},{5,7},{6,4},{7,5},{8,10},{9,11},{10,... | collective-permute-start | bytes 786440 | tf_op jit(solution)/shard_map/ppermute | solution.py:48
  47.5 12.3 %collective-permute-start.11 = (bf16[32,4096]{1,0:T(8,128)(2,1)S(1)}, bf16[32,4096]{1,0:T(8,128)(2,1)S(1)}, u32[]{:S(2)}, u32[]{:S(2)}) collective-permute-start(bf16[32,4096]{1,0:T(8,128)(2,1)S(1)} %get-tuple-element.19), channel_id=1, source_target_pairs={{0,1},{1,2},{2,3},{3,0},{4,5},{5,6},{6,7},{7,4},{8,9},{9,10},{10,1... | collective-permute-start | bytes 786440 | tf_op jit(solution)/shard_map/ppermute | solution.py:48
  48.2 12.0 %collective-permute-start.12 = (bf16[32,4096]{1,0:T(8,128)(2,1)S(1)}, bf16[32,4096]{1,0:T(8,128)(2,1)S(1)}, u32[]{:S(2)}, u32[]{:S(2)}) collective-permute-start(bf16[32,4096]{1,0:T(8,128)(2,1)S(1)} %get-tuple-element.20), channel_id=1, source_target_pairs={{0,3},{1,0},{2,1},{3,2},{4,7},{5,4},{6,5},{7,6},{8,11},{9,8},{10,9... | collective-permute-start | bytes 786440 | tf_op jit(solution)/shard_map/ppermute | solution.py:48
  60.9 6.4 %collective-permute-start.13 = (bf16[16,4096]{1,0:T(8,128)(2,1)S(1)}, bf16[16,4096]{1,0:T(8,128)(2,1)S(1)}, u32[]{:S(2)}, u32[]{:S(2)}) collective-permute-start(bf16[16,4096]{1,0:T(8,128)(2,1)S(1)} %get-tuple-element.41), channel_id=1, source_target_pairs={{0,1},{1,2},{2,3},{3,0},{4,5},{5,6},{6,7},{7,4},{8,9},{9,10},{10,1... | collective-permute-start | bytes 393224 | tf_op jit(solution)/shard_map/ppermute | solution.py:48
  62.3 8.9 %collective-permute-start.14 = (bf16[16,4096]{1,0:T(8,128)(2,1)S(1)}, bf16[16,4096]{1,0:T(8,128)(2,1)S(1)}, u32[]{:S(2)}, u32[]{:S(2)}) collective-permute-start(bf16[16,4096]{1,0:T(8,128)(2,1)S(1)} %get-tuple-element.40), channel_id=1, source_target_pairs={{0,2},{1,3},{2,0},{3,1},{4,6},{5,7},{6,4},{7,5},{8,10},{9,11},{10,... | collective-permute-start | bytes 393224 | tf_op jit(solution)/shard_map/ppermute | solution.py:48
  65.1 6.2 %collective-permute-start.15 = (bf16[16,4096]{1,0:T(8,128)(2,1)S(1)}, bf16[16,4096]{1,0:T(8,128)(2,1)S(1)}, u32[]{:S(2)}, u32[]{:S(2)}) collective-permute-start(bf16[16,4096]{1,0:T(8,128)(2,1)S(1)} %get-tuple-element.39), channel_id=1, source_target_pairs={{0,3},{1,0},{2,1},{3,2},{4,7},{5,4},{6,5},{7,6},{8,11},{9,8},{10,9... | collective-permute-start | bytes 393224 | tf_op jit(solution)/shard_map/ppermute | solution.py:48
  65.6 45.1 %collective-permute-start.20 = (bf16[448,4096]{1,0:T(8,128)(2,1)S(1)}, bf16[448,4096]{1,0:T(8,128)(2,1)S(1)}, u32[]{:S(2)}, u32[]{:S(2)}) collective-permute-start(bf16[448,4096]{1,0:T(8,128)(2,1)S(1)} %bitcast.28), channel_id=1, source_target_pairs={{0,4},{4,0},{8,12},{12,8},{16,20},{20,16},{24,28},{28,24},{32,36},... | collective-permute-start | bytes 11010056 | tf_op jit(solution)/shard_map/ppermute | solution.py:44
  65.6 45.9 %collective-permute-start.21 = (bf16[448,4096]{1,0:T(8,128)(2,1)}, bf16[448,4096]{1,0:T(8,128)(2,1)S(1)}, u32[]{:S(2)}, u32[]{:S(2)}) collective-permute-start(bf16[448,4096]{1,0:T(8,128)(2,1)} %bitcast.33), channel_id=1, source_target_pairs={{0,4},{4,0},{8,12},{12,8},{16,20},{20,16},{24,28},{28,24},{32,36},... | collective-permute-start | bytes 11010056 | tf_op jit(solution)/shard_map/ppermute | solution.py:44
  67.3 45.5 %collective-permute-start.22 = (bf16[448,4096]{1,0:T(8,128)(2,1)}, bf16[448,4096]{1,0:T(8,128)(2,1)S(1)}, u32[]{:S(2)}, u32[]{:S(2)}) collective-permute-start(bf16[448,4096]{1,0:T(8,128)(2,1)} %bitcast.38), channel_id=1, source_target_pairs={{0,4},{4,0},{8,12},{12,8},{16,20},{20,16},{24,28},{28,24},{32,36},... | collective-permute-start | bytes 11010056 | tf_op jit(solution)/shard_map/ppermute | solution.py:44
  71.3 12.1 %collective-permute-start.17 = (bf16[64,4096]{1,0:T(8,128)(2,1)S(1)}, bf16[64,4096]{1,0:T(8,128)(2,1)S(1)}, u32[]{:S(2)}, u32[]{:S(2)}) collective-permute-start(bf16[64,4096]{1,0:T(8,128)(2,1)S(1)} %pad_maximum_fusion.1), channel_id=1, source_target_pairs={{0,24},{4,100},{8,0},{12,108},{16,8},{20,116},{24,16},{28,124},{32... | collective-permute-start | bytes 1572872 | tf_op jit(solution)/shard_map/ppermute | solution.py:40
  72.9 10.4 %collective-permute-start.16 = (bf16[64,4096]{1,0:T(8,128)(2,1)S(1)}, bf16[64,4096]{1,0:T(8,128)(2,1)S(1)}, u32[]{:S(2)}, u32[]{:S(2)}) collective-permute-start(bf16[64,4096]{1,0:T(8,128)(2,1)S(1)} %pad_maximum_fusion.1), channel_id=1, source_target_pairs={{0,8},{4,36},{8,16},{12,44},{16,24},{20,52},{24,0},{28,60},{32,40}... | collective-permute-start | bytes 1572872 | tf_op jit(solution)/shard_map/ppermute | solution.py:40
  73.4 50.0 %copy-start.2 = (bf16[1,4096,448]{1,2,0:T(8,128)(2,1)S(1)}, bf16[1,4096,448]{1,2,0:T(8,128)(2,1)}, u32[]{:S(2)}) copy-start(bf16[1,4096,448]{1,2,0:T(8,128)(2,1)} %param.30) | copy-start | bytes 11010052
  83.3 7.7 %collective-permute-start.18 = (bf16[32,4096]{1,0:T(8,128)(2,1)S(1)}, bf16[32,4096]{1,0:T(8,128)(2,1)S(1)}, u32[]{:S(2)}, u32[]{:S(2)}) collective-permute-start(bf16[32,4096]{1,0:T(8,128)(2,1)S(1)} %slice.64), channel_id=1, source_target_pairs={{0,8},{4,36},{8,16},{12,44},{16,24},{20,52},{24,0},{28,60},{32,40}... | collective-permute-start | bytes 786440 | tf_op jit(solution)/shard_map/ppermute | solution.py:40
  83.5 9.6 %collective-permute-start.19 = (bf16[32,4096]{1,0:T(8,128)(2,1)S(1)}, bf16[32,4096]{1,0:T(8,128)(2,1)S(1)}, u32[]{:S(2)}, u32[]{:S(2)}) collective-permute-start(bf16[32,4096]{1,0:T(8,128)(2,1)S(1)} %slice.65), channel_id=1, source_target_pairs={{0,24},{4,100},{8,0},{12,108},{16,8},{20,116},{24,16},{28,124},{32... | collective-permute-start | bytes 786440 | tf_op jit(solution)/shard_map/ppermute | solution.py:40
  91.0 16.4 %collective-permute-start.23 = (bf16[128,4096]{1,0:T(8,128)(2,1)S(1)}, bf16[128,4096]{1,0:T(8,128)(2,1)S(1)}, u32[]{:S(2)}, u32[]{:S(2)}) collective-permute-start(bf16[128,4096]{1,0:T(8,128)(2,1)S(1)} %constant_dynamic-update-slice_fusion.2.refs_0_), channel_id=1, source_target_pairs={{0,32},{4,12},{8,40},{12,20},{16,48},{20,28},{24,56},{28,4},{32,64... | collective-permute-start | bytes 3145736 | tf_op jit(solution)/shard_map/ppermute | solution.py:40
  93.1 14.9 %collective-permute-start.24 = (bf16[128,4096]{1,0:T(8,128)(2,1)S(1)}, bf16[128,4096]{1,0:T(8,128)(2,1)S(1)}, u32[]{:S(2)}, u32[]{:S(2)}) collective-permute-start(bf16[128,4096]{1,0:T(8,128)(2,1)S(1)} %constant_dynamic-update-slice_fusion.7.refs_1_), channel_id=1, source_target_pairs={{0,96},{4,28},{8,104},{12,4},{16,112},{20,12},{24,120},{28,20},{32... | collective-permute-start | bytes 3145736 | tf_op jit(solution)/shard_map/ppermute | solution.py:40
  107.4 16.0 %collective-permute-start.25 = (bf16[128,4096]{1,0:T(8,128)(2,1)S(1)}, bf16[128,4096]{1,0:T(8,128)(2,1)S(1)}, u32[]{:S(2)}, u32[]{:S(2)}) collective-permute-start(bf16[128,4096]{1,0:T(8,128)(2,1)S(1)} %collective-permute-done.23.refs_0_), channel_id=1, source_target_pairs={{0,32},{4,12},{8,40},{12,20},{16,48},{20,28},{24,56},{28,4},{32,64... | collective-permute-start | bytes 3145736 | tf_op jit(solution)/shard_map/ppermute | solution.py:40
  107.9 15.5 %collective-permute-start.26 = (bf16[128,4096]{1,0:T(8,128)(2,1)S(1)}, bf16[128,4096]{1,0:T(8,128)(2,1)S(1)}, u32[]{:S(2)}, u32[]{:S(2)}) collective-permute-start(bf16[128,4096]{1,0:T(8,128)(2,1)S(1)} %collective-permute-done.24.refs_1_), channel_id=1, source_target_pairs={{0,96},{4,28},{8,104},{12,4},{16,112},{20,12},{24,120},{28,20},{32... | collective-permute-start | bytes 3145736 | tf_op jit(solution)/shard_map/ppermute | solution.py:40
  110.8 27.9 %collective-permute-start.30 = (bf16[128,4096]{1,0:T(8,128)(2,1)S(1)}, bf16[128,4096]{1,0:T(8,128)(2,1)S(1)}, u32[]{:S(2)}, u32[]{:S(2)}) collective-permute-start(bf16[128,4096]{1,0:T(8,128)(2,1)S(1)} %constant_dynamic-update-slice_fusion.2.refs_0_), channel_id=1, source_target_pairs={{0,96},{4,28},{8,104},{12,4},{16,112},{20,12},{24,120},{28,20},{32... | collective-permute-start | bytes 3145736 | tf_op jit(solution)/shard_map/ppermute | solution.py:40
  111.6 27.1 %collective-permute-start.29 = (bf16[128,4096]{1,0:T(8,128)(2,1)S(1)}, bf16[128,4096]{1,0:T(8,128)(2,1)S(1)}, u32[]{:S(2)}, u32[]{:S(2)}) collective-permute-start(bf16[128,4096]{1,0:T(8,128)(2,1)S(1)} %constant_dynamic-update-slice_fusion.7.refs_1_), channel_id=1, source_target_pairs={{0,32},{4,12},{8,40},{12,20},{16,48},{20,28},{24,56},{28,4},{32,64... | collective-permute-start | bytes 3145736 | tf_op jit(solution)/shard_map/ppermute | solution.py:40
  135.3 26.4 %collective-permute-start.27 = (bf16[128,4096]{1,0:T(8,128)(2,1)S(1)}, bf16[128,4096]{1,0:T(8,128)(2,1)S(1)}, u32[]{:S(2)}, u32[]{:S(2)}) collective-permute-start(bf16[128,4096]{1,0:T(8,128)(2,1)S(1)} %get-tuple-element.23), channel_id=1, source_target_pairs={{0,96},{4,28},{8,104},{12,4},{16,112},{20,12},{24,120},{28,20},{32... | collective-permute-start | bytes 3145736 | tf_op jit(solution)/shard_map/ppermute | solution.py:40
  148.5 37.5 %collective-permute-start.31 = (bf16[128,4096]{1,0:T(8,128)(2,1)S(1)}, bf16[128,4096]{1,0:T(8,128)(2,1)S(1)}, u32[]{:S(2)}, u32[]{:S(2)}) collective-permute-start(bf16[128,4096]{1,0:T(8,128)(2,1)S(1)} %get-tuple-element.24), channel_id=1, source_target_pairs={{0,32},{4,12},{8,40},{12,20},{16,48},{20,28},{24,56},{28,4},{32,64... | collective-permute-start | bytes 3145736 | tf_op jit(solution)/shard_map/ppermute | solution.py:40
  148.6 40.3 %collective-permute-start.36 = (bf16[128,4096]{1,0:T(8,128)(2,1)S(1)}, bf16[128,4096]{1,0:T(8,128)(2,1)S(1)}, u32[]{:S(2)}, u32[]{:S(2)}) collective-permute-start(bf16[128,4096]{1,0:T(8,128)(2,1)S(1)} %get-tuple-element.28), channel_id=1, source_target_pairs={{0,96},{4,28},{8,104},{12,4},{16,112},{20,12},{24,120},{28,20},{32... | collective-permute-start | bytes 3145736 | tf_op jit(solution)/shard_map/ppermute | solution.py:40
  151.8 24.0 %collective-permute-start.32 = (bf16[128,4096]{1,0:T(8,128)(2,1)S(1)}, bf16[128,4096]{1,0:T(8,128)(2,1)S(1)}, u32[]{:S(2)}, u32[]{:S(2)}) collective-permute-start(bf16[128,4096]{1,0:T(8,128)(2,1)S(1)} %get-tuple-element.26), channel_id=1, source_target_pairs={{0,32},{4,12},{8,40},{12,20},{16,48},{20,28},{24,56},{28,4},{32,64... | collective-permute-start | bytes 3145736 | tf_op jit(solution)/shard_map/ppermute | solution.py:40
  161.9 24.1 %collective-permute-start.28 = (bf16[128,4096]{1,0:T(8,128)(2,1)S(1)}, bf16[128,4096]{1,0:T(8,128)(2,1)S(1)}, u32[]{:S(2)}, u32[]{:S(2)}) collective-permute-start(bf16[128,4096]{1,0:T(8,128)(2,1)S(1)} %add_convert_fusion.3), channel_id=1, source_target_pairs={{0,96},{4,28},{8,104},{12,4},{16,112},{20,12},{24,120},{28,20},{32... | collective-permute-start | bytes 3145736 | tf_op jit(solution)/shard_map/ppermute | solution.py:40
  176.1 16.8 %collective-permute-start.33 = (bf16[128,4096]{1,0:T(8,128)(2,1)S(1)}, bf16[128,4096]{1,0:T(8,128)(2,1)S(1)}, u32[]{:S(2)}, u32[]{:S(2)}) collective-permute-start(bf16[128,4096]{1,0:T(8,128)(2,1)S(1)} %add_convert_fusion.1), channel_id=1, source_target_pairs={{0,32},{4,12},{8,40},{12,20},{16,48},{20,28},{24,56},{28,4},{32,64... | collective-permute-start | bytes 3145736 | tf_op jit(solution)/shard_map/ppermute | solution.py:40
  186.5 18.2 %collective-permute-start.35 = (bf16[64,4096]{1,0:T(8,128)(2,1)S(1)}, bf16[64,4096]{1,0:T(8,128)(2,1)S(1)}, u32[]{:S(2)}, u32[]{:S(2)}) collective-permute-start(bf16[64,4096]{1,0:T(8,128)(2,1)S(1)} %slice.68), channel_id=1, source_target_pairs={{0,24},{4,100},{8,0},{12,108},{16,8},{20,116},{24,16},{28,124},{32... | collective-permute-start | bytes 1572872 | tf_op jit(solution)/shard_map/ppermute | solution.py:40
  194.4 12.5 %collective-permute-start.37 = (bf16[64,4096]{1,0:T(8,128)(2,1)}, bf16[64,4096]{1,0:T(8,128)(2,1)}, u32[]{:S(2)}, u32[]{:S(2)}) collective-permute-start(bf16[64,4096]{1,0:T(8,128)(2,1)} %get-tuple-element.31), channel_id=1, source_target_pairs={{0,8},{4,36},{8,16},{12,44},{16,24},{20,52},{24,0},{28,60},{32,40}... | collective-permute-start | bytes 1572872 | tf_op jit(solution)/shard_map/ppermute | solution.py:40
  194.4 19.6 %collective-permute-start.38 = (bf16[64,4096]{1,0:T(8,128)(2,1)}, bf16[64,4096]{1,0:T(8,128)(2,1)}, u32[]{:S(2)}, u32[]{:S(2)}) collective-permute-start(bf16[64,4096]{1,0:T(8,128)(2,1)} %get-tuple-element.32), channel_id=1, source_target_pairs={{0,16},{4,68},{8,24},{12,76},{16,0},{20,84},{24,8},{28,92},{32,48}... | collective-permute-start | bytes 1572872 | tf_op jit(solution)/shard_map/ppermute | solution.py:40
  201.3 2.1 collective-permute-start.34
  215.5 9.2 %collective-permute-start.39 = (bf16[16,4096]{1,0:T(8,128)(2,1)S(1)}, bf16[16,4096]{1,0:T(8,128)(2,1)S(1)}, u32[]{:S(2)}, u32[]{:S(2)}) collective-permute-start(bf16[16,4096]{1,0:T(8,128)(2,1)S(1)} %get-tuple-element.36), channel_id=1, source_target_pairs={{0,3},{1,0},{2,1},{3,2},{4,7},{5,4},{6,5},{7,6},{8,11},{9,8},{10,9... | collective-permute-start | bytes 393224 | tf_op jit(solution)/shard_map/ppermute | solution.py:48
  217.1 9.2 %collective-permute-start.40 = (bf16[16,4096]{1,0:T(8,128)(2,1)S(1)}, bf16[16,4096]{1,0:T(8,128)(2,1)S(1)}, u32[]{:S(2)}, u32[]{:S(2)}) collective-permute-start(bf16[16,4096]{1,0:T(8,128)(2,1)S(1)} %get-tuple-element.35), channel_id=1, source_target_pairs={{0,2},{1,3},{2,0},{3,1},{4,6},{5,7},{6,4},{7,5},{8,10},{9,11},{10,... | collective-permute-start | bytes 393224 | tf_op jit(solution)/shard_map/ppermute | solution.py:48
  223.3 6.2 %collective-permute-start.41 = (bf16[16,4096]{1,0:T(8,128)(2,1)S(1)}, bf16[16,4096]{1,0:T(8,128)(2,1)S(1)}, u32[]{:S(2)}, u32[]{:S(2)}) collective-permute-start(bf16[16,4096]{1,0:T(8,128)(2,1)S(1)} %get-tuple-element.34), channel_id=1, source_target_pairs={{0,1},{1,2},{2,3},{3,0},{4,5},{5,6},{6,7},{7,4},{8,9},{9,10},{10,1... | collective-permute-start | bytes 393224 | tf_op jit(solution)/shard_map/ppermute | solution.py:48
  (9 other events, 57.2 us)

commit v5 on v4

--- a/solution.py
+++ b/solution.py
@@ -90,10 +90,17 @@
                 return pl.ds(pl.multiple_of(i * HEAD_SIZE, HEAD_SIZE), HEAD_SIZE)
 
             q_rows = jnp.concatenate([q_ref[:, column(h * cluster + g)] for g in range(cluster)], axis=0)
+
+            def score(kv):
+                contract = (((1,), (1,)), ((), ()))
+                return lax.dot_general(q_rows, kv[:, column(h)], contract, preferred_element_type=f32)
+
+            ahead = score(kv_refs[0])
             for n, kv in enumerate(kv_refs):
-                k = kv[:, column(h)]
+                s = ahead
+                if n + 1 < count:
+                    ahead = score(kv_refs[n + 1])
                 v = kv[:, column(kv_heads + h)]
-                s = lax.dot_general(q_rows, k, (((1,), (1,)), ((), ())), preferred_element_type=f32)
                 mask = jnp.where(kpos_ref[n : n + 1, :] <= qpos_ref[:, 0:1], 0.0, NEVER)
                 s = (s.reshape(cluster, tok, -1) * slope + mask[None]).reshape(rows, -1)
                 top = jnp.max(s, axis=1, keepdims=True)
@@ -331,7 +338,13 @@
     level = lax.ppermute(v1[:16, :128], "ctx", [(2 * i, 2 * i + 1) for i in range(16)])
     n0, n1 = total(n0, u0, v0), total(n1, u1, v1)
     part = rows.shape[0]
-    back = (shift(n0[part:], 1, -1), shift(n1[:part], 1, 1), shift(n1[part:], 1, 2))
+    half = part // 2
+    minus, plus = n0[part:], n1[:part]
+    q0 = shift(n1[part : part + half], 1, -1)
+    q1 = shift(n1[part + half :], 1, 1)
+    minus = total(minus, jnp.pad(q0, ((0, half), (0, 0))))
+    plus = total(plus, jnp.pad(q1, ((half, 0), (0, 0))))
+    back = (shift(minus, 1, -1), shift(plus, 1, 1))
     own_rows = total(n0[:part] + jnp.max(level) * 0, *back)
 
     r0, r1, r2, r3 = (own_rows[i * slot_count : (i + 1) * slot_count] for i in range(4))

time: 231 us -> 224 us (0.970); the launches traced: 231 us -> 221 us
  starting transfers between devices: 66.8 us -> 58.2 us
    ppermute x9, starting transfers between devices: 20.4 us -> 15 us  [shift_exp(): return lax.ppermute(a, 'exp', [(i, (i + step) % 4) for i in range(4)])]
    ppermute x25 -> x26, starting transfers between devices: 44.5 us -> 41.3 us  [shift(): return lax.ppermute(a, 'ctx', RINGS[phase, step])]
    ppermute x25 -> x26, waiting for transfers between devices: 74.3 us -> 74.2 us  [shift(): return lax.ppermute(a, 'ctx', RINGS[phase, step])]
  transfers between devices with their start and end apart: 42 -> 43, of which waited for: 22 -> 24; matrix products, arithmetic and copies ran while one was open for 4% -> 4% of each run, Pallas kernels for 17% -> 18%
where the time goes in v5:
time: 224 us; the launch traced here: 221 us
  waiting for transfers between devices  96.1 us (43%)
  starting transfers between devices  58.2 us (26%)
  Pallas kernels  49.7 us (22%)
  other arithmetic  7.56 us (3%)
  local copies, waits for them, and re-layouts  6.53 us (3%)
    ppermute x26, waiting for transfers between devices, shift(): return lax.ppermute(a, 'ctx', RINGS[phase, step])  74.2 us
    ppermute x26, starting transfers between devices, shift(): return lax.ppermute(a, 'ctx', RINGS[phase, step])  41.3 us
    pallas_call x4, Pallas kernels, expert_rows(): pl.pallas_call(kernel, out_shape=tuple((jax.ShapeDtypeStruct((size, width...  39.2 us
    ppermute x9, waiting for transfers between devices, shift_exp(): return lax.ppermute(a, 'exp', [(i, (i + step) % 4) for i in range(4)])  19.3 us
    ppermute x9, starting transfers between devices, shift_exp(): return lax.ppermute(a, 'exp', [(i, (i + step) % 4) for i in range(4)])  15 us
    pallas_call x1, Pallas kernels, attend(): pl.pallas_call(kernel, out_shape=tuple((jax.ShapeDtypeStruct((sub, width)...  10.5 us
  transfers between devices with their start and end apart: 43, of which 24 were waited for; matrix products, arithmetic and copies ran while one was open for 4% of the time, Pallas kernels for 18%

profile of v5, /device:TPU:0, one launch (start us, length us, event | category | flops | bytes accessed | tf_op | source)
XLA Modules:
  0.0 220.9 jit_solution(13383155397151232795)
XLA Ops:
  1.7 1.6 collective-permute-start
  3.3 1.6 collective-permute-start.1
  5.0 1.9 collective-permute-start.2
  9.5 1.9 collective-permute-done.2
  11.5 2.1 collective-permute-start.4
  13.6 2.2 collective-permute-start.6
  15.8 1.8 collective-permute-start.8
  18.8 4.0 %collective-permute-done.4.refs_2_ = bf16[512,512]{1,0:T(8,128)(2,1)S(1)} collective-permute-done((bf16[512,512]{1,0:T(8,128)(2,1)S(1)}, bf16[512,512]{1,0:T(8,128)(2,1)S(1)}, u32[]{:S(2)}, u32[]{:S(2)}) %collective-permute-start.4) | collective-permute-done | bytes 524320 | tf_op jit(solution)/shard_map/ppermute | solution.py:40
  22.9 5.3 %collective-permute-done.6.refs_4_ = bf16[512,512]{1,0:T(8,128)(2,1)S(1)} collective-permute-done((bf16[512,512]{1,0:T(8,128)(2,1)S(1)}, bf16[512,512]{1,0:T(8,128)(2,1)S(1)}, u32[]{:S(2)}, u32[]{:S(2)}) %collective-permute-start.6) | collective-permute-done | bytes 524320 | tf_op jit(solution)/shard_map/ppermute | solution.py:40
  28.1 1.8 collective-permute-done.8.refs_6_
  30.2 1.8 collective-permute-done.9.refs_7_
  33.1 10.5 %attend.1 = (f32[32,4096]{1,0:T(8,128)S(1)}, bf16[32,4096]{1,0:T(8,128)(2,1)S(1)}, bf16[32,4096]{1,0:T(8,128)(2,1)S(1)}, bf16[32,4096]{1,0:T(8,128)(2,1)S(1)}) custom-call(s32[1]{0:T(128)} %bitcast.mine_ref, bf16[128,1024]{1,0:T(8,128)(2,1)S(1)} %copy-done.4, s32[128,128]{1,0:T(8,128)S(1)} %broadcast_in_dim.125.qpos_ref, ...), custom_call_target="tpu_custom_call" | custom-call | flops 4294967296 | bytes 4194304 | tf_op jit(solution)/shard_map/attend/pallas_call | solution.py:136
  43.5 3.3 %collective-permute-start.10 = (bf16[32,4096]{1,0:T(8,128)(2,1)S(1)}, bf16[32,4096]{1,0:T(8,128)(2,1)S(1)}, u32[]{:S(2)}, u32[]{:S(2)}) collective-permute-start(bf16[32,4096]{1,0:T(8,128)(2,1)S(1)} %get-tuple-element.18), channel_id=1, source_target_pairs={{0,2},{1,3},{2,0},{3,1},{4,6},{5,7},{6,4},{7,5},{8,10},{9,11},{10,... | collective-permute-start | bytes 786440 | tf_op jit(solution)/shard_map/ppermute | solution.py:48
  47.5 2.6 %collective-permute-start.12 = (bf16[32,4096]{1,0:T(8,128)(2,1)S(1)}, bf16[32,4096]{1,0:T(8,128)(2,1)S(1)}, u32[]{:S(2)}, u32[]{:S(2)}) collective-permute-start(bf16[32,4096]{1,0:T(8,128)(2,1)S(1)} %get-tuple-element.20), channel_id=1, source_target_pairs={{0,3},{1,0},{2,1},{3,2},{4,7},{5,4},{6,5},{7,6},{8,11},{9,8},{10,9... | collective-permute-start | bytes 786440 | tf_op jit(solution)/shard_map/ppermute | solution.py:48
  50.6 3.8 %collective-permute-done.10 = bf16[32,4096]{1,0:T(8,128)(2,1)S(1)} collective-permute-done((bf16[32,4096]{1,0:T(8,128)(2,1)S(1)}, bf16[32,4096]{1,0:T(8,128)(2,1)S(1)}, u32[]{:S(2)}, u32[]{:S(2)}) %collective-permute-start.10) | collective-permute-done | bytes 262176 | tf_op jit(solution)/shard_map/ppermute | solution.py:48
  54.3 4.7 %collective-permute-done.11 = bf16[32,4096]{1,0:T(8,128)(2,1)S(1)} collective-permute-done((bf16[32,4096]{1,0:T(8,128)(2,1)S(1)}, bf16[32,4096]{1,0:T(8,128)(2,1)S(1)}, u32[]{:S(2)}, u32[]{:S(2)}) %collective-permute-start.11) | collective-permute-done | bytes 262176 | tf_op jit(solution)/shard_map/ppermute | solution.py:48
  60.2 1.4 collective-permute-start.13
  61.6 2.7 %collective-permute-start.14 = (bf16[16,4096]{1,0:T(8,128)(2,1)S(1)}, bf16[16,4096]{1,0:T(8,128)(2,1)S(1)}, u32[]{:S(2)}, u32[]{:S(2)}) collective-permute-start(bf16[16,4096]{1,0:T(8,128)(2,1)S(1)} %get-tuple-element.40), channel_id=1, source_target_pairs={{0,2},{1,3},{2,0},{3,1},{4,6},{5,7},{6,4},{7,5},{8,10},{9,11},{10,... | collective-permute-start | bytes 393224 | tf_op jit(solution)/shard_map/ppermute | solution.py:48
  66.6 4.0 %collective-permute-done.14 = bf16[16,4096]{1,0:T(8,128)(2,1)S(1)} collective-permute-done((bf16[16,4096]{1,0:T(8,128)(2,1)S(1)}, bf16[16,4096]{1,0:T(8,128)(2,1)S(1)}, u32[]{:S(2)}, u32[]{:S(2)}) %collective-permute-start.14) | collective-permute-done | bytes 131104 | tf_op jit(solution)/shard_map/ppermute | solution.py:48
  70.6 1.6 collective-permute-start.17
  72.8 9.8 %collective-permute-done.16 = bf16[64,4096]{1,0:T(8,128)(2,1)S(1)} collective-permute-done((bf16[64,4096]{1,0:T(8,128)(2,1)S(1)}, bf16[64,4096]{1,0:T(8,128)(2,1)S(1)}, u32[]{:S(2)}, u32[]{:S(2)}) %collective-permute-start.16) | collective-permute-done | bytes 524320 | tf_op jit(solution)/shard_map/ppermute | solution.py:40
  82.9 3.3 %collective-permute-start.19 = (bf16[32,4096]{1,0:T(8,128)(2,1)S(1)}, bf16[32,4096]{1,0:T(8,128)(2,1)S(1)}, u32[]{:S(2)}, u32[]{:S(2)}) collective-permute-start(bf16[32,4096]{1,0:T(8,128)(2,1)S(1)} %slice.69), channel_id=1, source_target_pairs={{0,24},{4,100},{8,0},{12,108},{16,8},{20,116},{24,16},{28,124},{32... | collective-permute-start | bytes 786440 | tf_op jit(solution)/shard_map/ppermute | solution.py:40
  86.3 4.2 %collective-permute-done.18 = bf16[32,4096]{1,0:T(8,128)(2,1)S(1)} collective-permute-done((bf16[32,4096]{1,0:T(8,128)(2,1)S(1)}, bf16[32,4096]{1,0:T(8,128)(2,1)S(1)}, u32[]{:S(2)}, u32[]{:S(2)}) %collective-permute-start.18) | collective-permute-done | bytes 262176 | tf_op jit(solution)/shard_map/ppermute | solution.py:40
  90.5 2.0 collective-permute-start.23
  92.6 1.7 collective-permute-start.24
  94.2 12.6 %collective-permute-done.23.refs_0_ = bf16[128,4096]{1,0:T(8,128)(2,1)S(1)} collective-permute-done((bf16[128,4096]{1,0:T(8,128)(2,1)S(1)}, bf16[128,4096]{1,0:T(8,128)(2,1)S(1)}, u32[]{:S(2)}, u32[]{:S(2)}) %collective-permute-start.23) | collective-permute-done | bytes 1048608 | tf_op jit(solution)/shard_map/ppermute | solution.py:40
  107.4 2.8 %collective-permute-start.26 = (bf16[128,4096]{1,0:T(8,128)(2,1)S(1)}, bf16[128,4096]{1,0:T(8,128)(2,1)S(1)}, u32[]{:S(2)}, u32[]{:S(2)}) collective-permute-start(bf16[128,4096]{1,0:T(8,128)(2,1)S(1)} %collective-permute-done.24.refs_1_), channel_id=1, source_target_pairs={{0,96},{4,28},{8,104},{12,4},{16,112},{20,12},{24,120},{28,20},{32... | collective-permute-start | bytes 3145736 | tf_op jit(solution)/shard_map/ppermute | solution.py:40
  112.3 10.6 %collective-permute-done.25.refs_0_ = bf16[128,4096]{1,0:T(8,128)(2,1)S(1)} collective-permute-done((bf16[128,4096]{1,0:T(8,128)(2,1)S(1)}, bf16[128,4096]{1,0:T(8,128)(2,1)S(1)}, u32[]{:S(2)}, u32[]{:S(2)}) %collective-permute-start.25) | collective-permute-done | bytes 1048608 | tf_op jit(solution)/shard_map/ppermute | solution.py:40
  122.9 2.0 copy-done.3
  125.0 9.8 %expert_rows.6 = (bf16[128,4096]{1,0:T(8,128)(2,1)S(1)}, bf16[128,4096]{1,0:T(8,128)(2,1)S(1)}) custom-call(bf16[128,4096]{1,0:T(8,128)(2,1)S(1)} %collective-permute-done.25.refs_0_, bf16[128,4096]{1,0:T(8,128)(2,1)S(1)} %collective-permute-done.26.refs_1_, bf16[448,4096]{1,0:T(8,128)(2,1)S(1)} %bitcast.29, bf16[448,4096]{1,0:T(8,128)(2,1)S(1)} %bitcast.34, ...), custom_call_target="tpu_custom_call" | custom-call | flops 5637144576 | bytes 22020096 | tf_op jit(solution)/shard_map/expert_rows/pallas_call | solution.py:222
  135.7 9.8 %expert_rows.7 = (bf16[128,4096]{1,0:T(8,128)(2,1)S(1)}, bf16[128,4096]{1,0:T(8,128)(2,1)S(1)}) custom-call(bf16[128,4096]{1,0:T(8,128)(2,1)S(1)} %collective-permute-done.29.refs_0_, bf16[128,4096]{1,0:T(8,128)(2,1)S(1)} %collective-permute-done.30.refs_1_, bf16[448,4096]{1,0:T(8,128)(2,1)S(1)} %bitcast.30, bf16[448,4096]{1,0:T(8,128)(2,1)S(1)} %bitcast.35, ...), custom_call_target="tpu_custom_call" | custom-call | flops 5637144576 | bytes 22020096 | tf_op jit(solution)/shard_map/expert_rows/pallas_call | solution.py:222
  145.5 1.6 collective-permute-start.31
  147.1 1.8 collective-permute-start.35
  148.8 9.8 %expert_rows.5 = (bf16[128,4096]{1,0:T(8,128)(2,1)S(1)}, bf16[128,4096]{1,0:T(8,128)(2,1)S(1)}) custom-call(bf16[128,4096]{1,0:T(8,128)(2,1)S(1)} %collective-permute-done.23.refs_0_, bf16[128,4096]{1,0:T(8,128)(2,1)S(1)} %collective-permute-done.24.refs_1_, bf16[448,4096]{1,0:T(8,128)(2,1)S(1)} %bitcast.31, bf16[448,4096]{1,0:T(8,128)(2,1)S(1)} %bitcast.36, ...), custom_call_target="tpu_custom_call" | custom-call | flops 5637144576 | bytes 22020096 | tf_op jit(solution)/shard_map/expert_rows/pallas_call | solution.py:222
  158.6 1.4 collective-permute-start.27
  161.3 9.8 %expert_rows.4 = (bf16[128,4096]{1,0:T(8,128)(2,1)S(1)}, bf16[128,4096]{1,0:T(8,128)(2,1)S(1)}) custom-call(bf16[128,4096]{1,0:T(8,128)(2,1)S(1)} %constant_dynamic-update-slice_fusion.2.refs_0_, bf16[128,4096]{1,0:T(8,128)(2,1)S(1)} %constant_dynamic-update-slice_fusion.7.refs_1_, bf16[448,4096]{1,0:T(8,128)(2,1)S(1)} %bitcast.32, ...), custom_call_target="tpu_custom_call" | custom-call | flops 5637144576 | bytes 22020096 | tf_op jit(solution)/shard_map/expert_rows/pallas_call | solution.py:222
  171.1 2.4 %collective-permute-done.27 = bf16[128,4096]{1,0:T(8,128)(2,1)S(1)} collective-permute-done((bf16[128,4096]{1,0:T(8,128)(2,1)S(1)}, bf16[128,4096]{1,0:T(8,128)(2,1)S(1)}, u32[]{:S(2)}, u32[]{:S(2)}) %collective-permute-start.27) | collective-permute-done | bytes 1048608 | tf_op jit(solution)/shard_map/ppermute | solution.py:40
  173.8 2.6 %collective-permute-start.28 = (bf16[128,4096]{1,0:T(8,128)(2,1)S(1)}, bf16[128,4096]{1,0:T(8,128)(2,1)S(1)}, u32[]{:S(2)}, u32[]{:S(2)}) collective-permute-start(bf16[128,4096]{1,0:T(8,128)(2,1)S(1)} %add_convert_fusion.3), channel_id=1, source_target_pairs={{0,96},{4,28},{8,104},{12,4},{16,112},{20,12},{24,120},{28,20},{32... | collective-permute-start | bytes 3145736 | tf_op jit(solution)/shard_map/ppermute | solution.py:40
  177.9 4.1 %collective-permute-start.36 = (bf16[32,4096]{1,0:T(8,128)(2,1)S(1)}, bf16[32,4096]{1,0:T(8,128)(2,1)S(1)}, u32[]{:S(2)}, u32[]{:S(2)}) collective-permute-start(bf16[32,4096]{1,0:T(8,128)(2,1)S(1)} %get-tuple-element.31), channel_id=1, source_target_pairs={{0,24},{4,100},{8,0},{12,108},{16,8},{20,116},{24,16},{28,124},{32... | collective-permute-start | bytes 786440 | tf_op jit(solution)/shard_map/ppermute | solution.py:40
  182.0 13.6 %collective-permute-done.28 = bf16[128,4096]{1,0:T(8,128)(2,1)S(1)} collective-permute-done((bf16[128,4096]{1,0:T(8,128)(2,1)S(1)}, bf16[128,4096]{1,0:T(8,128)(2,1)S(1)}, u32[]{:S(2)}, u32[]{:S(2)}) %collective-permute-start.28) | collective-permute-done | bytes 1048608 | tf_op jit(solution)/shard_map/ppermute | solution.py:40
  197.0 2.0 collective-permute-start.37
  200.3 1.3 collective-permute-start.34
  203.7 2.7 %collective-permute-done.37 = bf16[64,4096]{1,0:T(8,128)(2,1)S(1)} collective-permute-done((bf16[64,4096]{1,0:T(8,128)(2,1)}, bf16[64,4096]{1,0:T(8,128)(2,1)S(1)}, u32[]{:S(2)}, u32[]{:S(2)}) %collective-permute-start.37) | collective-permute-done | bytes 524320 | tf_op jit(solution)/shard_map/ppermute | solution.py:40
  206.4 4.1 %collective-permute-done.39 = bf16[64,4096]{1,0:T(8,128)(2,1)S(1)} collective-permute-done((bf16[64,4096]{1,0:T(8,128)(2,1)}, bf16[64,4096]{1,0:T(8,128)(2,1)S(1)}, u32[]{:S(2)}, u32[]{:S(2)}) %collective-permute-start.39) | collective-permute-done | bytes 524320 | tf_op jit(solution)/shard_map/ppermute | solution.py:40
  210.8 1.3 collective-permute-start.40
  213.2 1.3 collective-permute-start.42
  215.8 2.8 %collective-permute-done.41 = bf16[16,4096]{1,0:T(8,128)(2,1)S(1)} collective-permute-done((bf16[16,4096]{1,0:T(8,128)(2,1)S(1)}, bf16[16,4096]{1,0:T(8,128)(2,1)S(1)}, u32[]{:S(2)}, u32[]{:S(2)}) %collective-permute-start.41) | collective-permute-done | bytes 131104 | tf_op jit(solution)/shard_map/ppermute | solution.py:48
  218.6 1.4 collective-permute-done.42
  (147 shorter events, 26.5 us)
Async XLA Ops:
  0.0 199.9 %copy-start = (f32[4096,4]{0,1:T(4,128)S(1)}, f32[4096,4]{0,1:T(4,128)}, u32[]{:S(2)}) copy-start(f32[4096,4]{0,1:T(4,128)} %param.27) | copy-start | bytes 196612
  1.7 7.8 %collective-permute-start = (bf16[128,512]{1,0:T(8,128)(2,1)S(1)}, bf16[128,512]{1,0:T(8,128)(2,1)S(1)}, u32[]{:S(2)}, u32[]{:S(2)}) collective-permute-start(bf16[128,512]{1,0:T(8,128)(2,1)S(1)} %constant_dynamic-update-slice_fusion), channel_id=1, source_target_pairs={{0,8},{4,36},{8,16},{12,44},{16,24},{20,52},{24,0},{28,60},{32,40}... | collective-permute-start | bytes 393224 | tf_op jit(solution)/shard_map/ppermute | solution.py:40
  3.3 6.2 %collective-permute-start.1 = (bf16[128,512]{1,0:T(8,128)(2,1)S(1)}, bf16[128,512]{1,0:T(8,128)(2,1)S(1)}, u32[]{:S(2)}, u32[]{:S(2)}) collective-permute-start(bf16[128,512]{1,0:T(8,128)(2,1)S(1)} %constant_dynamic-update-slice_fusion), channel_id=1, source_target_pairs={{0,24},{4,100},{8,0},{12,108},{16,8},{20,116},{24,16},{28,124},{32... | collective-permute-start | bytes 393224 | tf_op jit(solution)/shard_map/ppermute | solution.py:40
  5.0 6.5 %collective-permute-start.2 = (bf16[128,512]{1,0:T(8,128)(2,1)S(1)}, bf16[128,512]{1,0:T(8,128)(2,1)S(1)}, u32[]{:S(2)}, u32[]{:S(2)}) collective-permute-start(bf16[128,512]{1,0:T(8,128)(2,1)S(1)} %constant_dynamic-update-slice_fusion), channel_id=1, source_target_pairs={{0,16},{4,68},{8,24},{12,76},{16,0},{20,84},{24,8},{28,92},{32,48}... | collective-permute-start | bytes 393224 | tf_op jit(solution)/shard_map/ppermute | solution.py:40
  11.5 20.6 %copy-start.7 = (bf16[512,512]{1,0:T(8,128)(2,1)}, bf16[512,512]{1,0:T(8,128)(2,1)S(1)}, u32[]{:S(2)}) copy-start(bf16[512,512]{1,0:T(8,128)(2,1)S(1)} %pad_maximum_fusion.refs_0_) | copy-start | bytes 1572868
  11.5 11.4 %collective-permute-start.4 = (bf16[512,512]{1,0:T(8,128)(2,1)S(1)}, bf16[512,512]{1,0:T(8,128)(2,1)S(1)}, u32[]{:S(2)}, u32[]{:S(2)}) collective-permute-start(bf16[512,512]{1,0:T(8,128)(2,1)S(1)} %pad_maximum_fusion.refs_0_), channel_id=1, source_target_pairs={{0,32},{4,12},{8,40},{12,20},{16,48},{20,28},{24,56},{28,4},{32,64... | collective-permute-start | bytes 1572872 | tf_op jit(solution)/shard_map/ppermute | solution.py:40
  13.6 14.6 %collective-permute-start.6 = (bf16[512,512]{1,0:T(8,128)(2,1)S(1)}, bf16[512,512]{1,0:T(8,128)(2,1)S(1)}, u32[]{:S(2)}, u32[]{:S(2)}) collective-permute-start(bf16[512,512]{1,0:T(8,128)(2,1)S(1)} %pad_maximum_fusion.refs_0_), channel_id=1, source_target_pairs={{0,96},{4,28},{8,104},{12,4},{16,112},{20,12},{24,120},{28,20},{32... | collective-permute-start | bytes 1572872 | tf_op jit(solution)/shard_map/ppermute | solution.py:40
  15.8 14.2 %collective-permute-start.8 = (bf16[512,512]{1,0:T(8,128)(2,1)S(1)}, bf16[512,512]{1,0:T(8,128)(2,1)S(1)}, u32[]{:S(2)}, u32[]{:S(2)}) collective-permute-start(bf16[512,512]{1,0:T(8,128)(2,1)S(1)} %pad_maximum_fusion.refs_0_), channel_id=1, source_target_pairs={{0,64},{4,20},{8,72},{12,28},{16,80},{20,4},{24,88},{28,12},{32,96... | collective-permute-start | bytes 1572872 | tf_op jit(solution)/shard_map/ppermute | solution.py:40
  18.7 11.4 %collective-permute-start.3 = (bf16[512,512]{1,0:T(8,128)(2,1)S(1)}, bf16[512,512]{1,0:T(8,128)(2,1)S(1)}, u32[]{:S(2)}, u32[]{:S(2)}) collective-permute-start(bf16[512,512]{1,0:T(8,128)(2,1)S(1)} %pad_maximum_fusion.refs_0_), channel_id=1, source_target_pairs={{0,4},{4,0},{8,12},{12,8},{16,20},{20,16},{24,28},{28,24},{32,36},... | collective-permute-start | bytes 1572872 | tf_op jit(solution)/shard_map/ppermute | solution.py:44
  22.9 7.3 %collective-permute-start.5 = (bf16[512,512]{1,0:T(8,128)(2,1)S(1)}, bf16[512,512]{1,0:T(8,128)(2,1)}, u32[]{:S(2)}, u32[]{:S(2)}) collective-permute-start(bf16[512,512]{1,0:T(8,128)(2,1)S(1)} %collective-permute-done.4.refs_2_), channel_id=1, source_target_pairs={{0,4},{4,0},{8,12},{12,8},{16,20},{20,16},{24,28},{28,24},{32,36},... | collective-permute-start | bytes 1572872 | tf_op jit(solution)/shard_map/ppermute | solution.py:44
  28.1 2.0 collective-permute-start.7
  29.9 2.0 collective-permute-start.9
  33.1 26.4 %copy-start.8 = (bf16[32,4096]{1,0:T(8,128)(2,1)S(1)}, bf16[32,4096]{1,0:T(8,128)(2,1)}, u32[]{:S(2)}) copy-start(bf16[32,4096]{1,0:T(8,128)(2,1)} %param.23) | copy-start | bytes 786436
  33.1 26.7 %copy-start.9 = (f32[4096]{0:T(1024)S(1)}, f32[4096]{0:T(1024)}, u32[]{:S(2)}) copy-start(f32[4096]{0:T(1024)} %param.26) | copy-start | bytes 49156
  43.5 10.8 %collective-permute-start.10 = (bf16[32,4096]{1,0:T(8,128)(2,1)S(1)}, bf16[32,4096]{1,0:T(8,128)(2,1)S(1)}, u32[]{:S(2)}, u32[]{:S(2)}) collective-permute-start(bf16[32,4096]{1,0:T(8,128)(2,1)S(1)} %get-tuple-element.18), channel_id=1, source_target_pairs={{0,2},{1,3},{2,0},{3,1},{4,6},{5,7},{6,4},{7,5},{8,10},{9,11},{10,... | collective-permute-start | bytes 786440 | tf_op jit(solution)/shard_map/ppermute | solution.py:48
  46.8 12.3 %collective-permute-start.11 = (bf16[32,4096]{1,0:T(8,128)(2,1)S(1)}, bf16[32,4096]{1,0:T(8,128)(2,1)S(1)}, u32[]{:S(2)}, u32[]{:S(2)}) collective-permute-start(bf16[32,4096]{1,0:T(8,128)(2,1)S(1)} %get-tuple-element.19), channel_id=1, source_target_pairs={{0,1},{1,2},{2,3},{3,0},{4,5},{5,6},{6,7},{7,4},{8,9},{9,10},{10,1... | collective-permute-start | bytes 786440 | tf_op jit(solution)/shard_map/ppermute | solution.py:48
  47.5 12.0 %collective-permute-start.12 = (bf16[32,4096]{1,0:T(8,128)(2,1)S(1)}, bf16[32,4096]{1,0:T(8,128)(2,1)S(1)}, u32[]{:S(2)}, u32[]{:S(2)}) collective-permute-start(bf16[32,4096]{1,0:T(8,128)(2,1)S(1)} %get-tuple-element.20), channel_id=1, source_target_pairs={{0,3},{1,0},{2,1},{3,2},{4,7},{5,4},{6,5},{7,6},{8,11},{9,8},{10,9... | collective-permute-start | bytes 786440 | tf_op jit(solution)/shard_map/ppermute | solution.py:48
  60.2 6.4 %collective-permute-start.13 = (bf16[16,4096]{1,0:T(8,128)(2,1)S(1)}, bf16[16,4096]{1,0:T(8,128)(2,1)S(1)}, u32[]{:S(2)}, u32[]{:S(2)}) collective-permute-start(bf16[16,4096]{1,0:T(8,128)(2,1)S(1)} %get-tuple-element.41), channel_id=1, source_target_pairs={{0,1},{1,2},{2,3},{3,0},{4,5},{5,6},{6,7},{7,4},{8,9},{9,10},{10,1... | collective-permute-start | bytes 393224 | tf_op jit(solution)/shard_map/ppermute | solution.py:48
  61.6 8.9 %collective-permute-start.14 = (bf16[16,4096]{1,0:T(8,128)(2,1)S(1)}, bf16[16,4096]{1,0:T(8,128)(2,1)S(1)}, u32[]{:S(2)}, u32[]{:S(2)}) collective-permute-start(bf16[16,4096]{1,0:T(8,128)(2,1)S(1)} %get-tuple-element.40), channel_id=1, source_target_pairs={{0,2},{1,3},{2,0},{3,1},{4,6},{5,7},{6,4},{7,5},{8,10},{9,11},{10,... | collective-permute-start | bytes 393224 | tf_op jit(solution)/shard_map/ppermute | solution.py:48
  64.4 6.2 %collective-permute-start.15 = (bf16[16,4096]{1,0:T(8,128)(2,1)S(1)}, bf16[16,4096]{1,0:T(8,128)(2,1)S(1)}, u32[]{:S(2)}, u32[]{:S(2)}) collective-permute-start(bf16[16,4096]{1,0:T(8,128)(2,1)S(1)} %get-tuple-element.39), channel_id=1, source_target_pairs={{0,3},{1,0},{2,1},{3,2},{4,7},{5,4},{6,5},{7,6},{8,11},{9,8},{10,9... | collective-permute-start | bytes 393224 | tf_op jit(solution)/shard_map/ppermute | solution.py:48
  64.9 45.3 %collective-permute-start.20 = (bf16[448,4096]{1,0:T(8,128)(2,1)S(1)}, bf16[448,4096]{1,0:T(8,128)(2,1)S(1)}, u32[]{:S(2)}, u32[]{:S(2)}) collective-permute-start(bf16[448,4096]{1,0:T(8,128)(2,1)S(1)} %bitcast.28), channel_id=1, source_target_pairs={{0,4},{4,0},{8,12},{12,8},{16,20},{20,16},{24,28},{28,24},{32,36},... | collective-permute-start | bytes 11010056 | tf_op jit(solution)/shard_map/ppermute | solution.py:44
  64.9 46.1 %collective-permute-start.21 = (bf16[448,4096]{1,0:T(8,128)(2,1)}, bf16[448,4096]{1,0:T(8,128)(2,1)S(1)}, u32[]{:S(2)}, u32[]{:S(2)}) collective-permute-start(bf16[448,4096]{1,0:T(8,128)(2,1)} %bitcast.33), channel_id=1, source_target_pairs={{0,4},{4,0},{8,12},{12,8},{16,20},{20,16},{24,28},{28,24},{32,36},... | collective-permute-start | bytes 11010056 | tf_op jit(solution)/shard_map/ppermute | solution.py:44
  66.6 45.7 %collective-permute-start.22 = (bf16[448,4096]{1,0:T(8,128)(2,1)}, bf16[448,4096]{1,0:T(8,128)(2,1)S(1)}, u32[]{:S(2)}, u32[]{:S(2)}) collective-permute-start(bf16[448,4096]{1,0:T(8,128)(2,1)} %bitcast.38), channel_id=1, source_target_pairs={{0,4},{4,0},{8,12},{12,8},{16,20},{20,16},{24,28},{28,24},{32,36},... | collective-permute-start | bytes 11010056 | tf_op jit(solution)/shard_map/ppermute | solution.py:44
  70.6 12.3 %collective-permute-start.17 = (bf16[64,4096]{1,0:T(8,128)(2,1)S(1)}, bf16[64,4096]{1,0:T(8,128)(2,1)S(1)}, u32[]{:S(2)}, u32[]{:S(2)}) collective-permute-start(bf16[64,4096]{1,0:T(8,128)(2,1)S(1)} %pad_maximum_fusion.1), channel_id=1, source_target_pairs={{0,24},{4,100},{8,0},{12,108},{16,8},{20,116},{24,16},{28,124},{32... | collective-permute-start | bytes 1572872 | tf_op jit(solution)/shard_map/ppermute | solution.py:40
  72.2 10.4 %collective-permute-start.16 = (bf16[64,4096]{1,0:T(8,128)(2,1)S(1)}, bf16[64,4096]{1,0:T(8,128)(2,1)S(1)}, u32[]{:S(2)}, u32[]{:S(2)}) collective-permute-start(bf16[64,4096]{1,0:T(8,128)(2,1)S(1)} %pad_maximum_fusion.1), channel_id=1, source_target_pairs={{0,8},{4,36},{8,16},{12,44},{16,24},{20,52},{24,0},{28,60},{32,40}... | collective-permute-start | bytes 1572872 | tf_op jit(solution)/shard_map/ppermute | solution.py:40
  72.8 50.1 %copy-start.2 = (bf16[1,4096,448]{1,2,0:T(8,128)(2,1)S(1)}, bf16[1,4096,448]{1,2,0:T(8,128)(2,1)}, u32[]{:S(2)}) copy-start(bf16[1,4096,448]{1,2,0:T(8,128)(2,1)} %param.30) | copy-start | bytes 11010052
  82.6 7.8 %collective-permute-start.18 = (bf16[32,4096]{1,0:T(8,128)(2,1)S(1)}, bf16[32,4096]{1,0:T(8,128)(2,1)S(1)}, u32[]{:S(2)}, u32[]{:S(2)}) collective-permute-start(bf16[32,4096]{1,0:T(8,128)(2,1)S(1)} %slice.68), channel_id=1, source_target_pairs={{0,8},{4,36},{8,16},{12,44},{16,24},{20,52},{24,0},{28,60},{32,40}... | collective-permute-start | bytes 786440 | tf_op jit(solution)/shard_map/ppermute | solution.py:40
  82.9 9.6 %collective-permute-start.19 = (bf16[32,4096]{1,0:T(8,128)(2,1)S(1)}, bf16[32,4096]{1,0:T(8,128)(2,1)S(1)}, u32[]{:S(2)}, u32[]{:S(2)}) collective-permute-start(bf16[32,4096]{1,0:T(8,128)(2,1)S(1)} %slice.69), channel_id=1, source_target_pairs={{0,24},{4,100},{8,0},{12,108},{16,8},{20,116},{24,16},{28,124},{32... | collective-permute-start | bytes 786440 | tf_op jit(solution)/shard_map/ppermute | solution.py:40
  90.5 16.4 %collective-permute-start.23 = (bf16[128,4096]{1,0:T(8,128)(2,1)S(1)}, bf16[128,4096]{1,0:T(8,128)(2,1)S(1)}, u32[]{:S(2)}, u32[]{:S(2)}) collective-permute-start(bf16[128,4096]{1,0:T(8,128)(2,1)S(1)} %constant_dynamic-update-slice_fusion.2.refs_0_), channel_id=1, source_target_pairs={{0,32},{4,12},{8,40},{12,20},{16,48},{20,28},{24,56},{28,4},{32,64... | collective-permute-start | bytes 3145736 | tf_op jit(solution)/shard_map/ppermute | solution.py:40
  92.6 14.9 %collective-permute-start.24 = (bf16[128,4096]{1,0:T(8,128)(2,1)S(1)}, bf16[128,4096]{1,0:T(8,128)(2,1)S(1)}, u32[]{:S(2)}, u32[]{:S(2)}) collective-permute-start(bf16[128,4096]{1,0:T(8,128)(2,1)S(1)} %constant_dynamic-update-slice_fusion.7.refs_1_), channel_id=1, source_target_pairs={{0,96},{4,28},{8,104},{12,4},{16,112},{20,12},{24,120},{28,20},{32... | collective-permute-start | bytes 3145736 | tf_op jit(solution)/shard_map/ppermute | solution.py:40
  106.9 16.0 %collective-permute-start.25 = (bf16[128,4096]{1,0:T(8,128)(2,1)S(1)}, bf16[128,4096]{1,0:T(8,128)(2,1)S(1)}, u32[]{:S(2)}, u32[]{:S(2)}) collective-permute-start(bf16[128,4096]{1,0:T(8,128)(2,1)S(1)} %collective-permute-done.23.refs_0_), channel_id=1, source_target_pairs={{0,32},{4,12},{8,40},{12,20},{16,48},{20,28},{24,56},{28,4},{32,64... | collective-permute-start | bytes 3145736 | tf_op jit(solution)/shard_map/ppermute | solution.py:40
  107.4 15.5 %collective-permute-start.26 = (bf16[128,4096]{1,0:T(8,128)(2,1)S(1)}, bf16[128,4096]{1,0:T(8,128)(2,1)S(1)}, u32[]{:S(2)}, u32[]{:S(2)}) collective-permute-start(bf16[128,4096]{1,0:T(8,128)(2,1)S(1)} %collective-permute-done.24.refs_1_), channel_id=1, source_target_pairs={{0,96},{4,28},{8,104},{12,4},{16,112},{20,12},{24,120},{28,20},{32... | collective-permute-start | bytes 3145736 | tf_op jit(solution)/shard_map/ppermute | solution.py:40
  110.3 25.4 %collective-permute-start.30 = (bf16[128,4096]{1,0:T(8,128)(2,1)S(1)}, bf16[128,4096]{1,0:T(8,128)(2,1)S(1)}, u32[]{:S(2)}, u32[]{:S(2)}) collective-permute-start(bf16[128,4096]{1,0:T(8,128)(2,1)S(1)} %constant_dynamic-update-slice_fusion.2.refs_0_), channel_id=1, source_target_pairs={{0,96},{4,28},{8,104},{12,4},{16,112},{20,12},{24,120},{28,20},{32... | collective-permute-start | bytes 3145736 | tf_op jit(solution)/shard_map/ppermute | solution.py:40
  111.1 24.6 %collective-permute-start.29 = (bf16[128,4096]{1,0:T(8,128)(2,1)S(1)}, bf16[128,4096]{1,0:T(8,128)(2,1)S(1)}, u32[]{:S(2)}, u32[]{:S(2)}) collective-permute-start(bf16[128,4096]{1,0:T(8,128)(2,1)S(1)} %constant_dynamic-update-slice_fusion.7.refs_1_), channel_id=1, source_target_pairs={{0,32},{4,12},{8,40},{12,20},{16,48},{20,28},{24,56},{28,4},{32,64... | collective-permute-start | bytes 3145736 | tf_op jit(solution)/shard_map/ppermute | solution.py:40
  134.8 25.3 %collective-permute-start.32 = (bf16[128,4096]{1,0:T(8,128)(2,1)S(1)}, bf16[128,4096]{1,0:T(8,128)(2,1)S(1)}, u32[]{:S(2)}, u32[]{:S(2)}) collective-permute-start(bf16[128,4096]{1,0:T(8,128)(2,1)S(1)} %get-tuple-element.26), channel_id=1, source_target_pairs={{0,32},{4,12},{8,40},{12,20},{16,48},{20,28},{24,56},{28,4},{32,64... | collective-permute-start | bytes 3145736 | tf_op jit(solution)/shard_map/ppermute | solution.py:40
  145.5 36.5 %collective-permute-start.31 = (bf16[128,4096]{1,0:T(8,128)(2,1)S(1)}, bf16[128,4096]{1,0:T(8,128)(2,1)S(1)}, u32[]{:S(2)}, u32[]{:S(2)}) collective-permute-start(bf16[128,4096]{1,0:T(8,128)(2,1)S(1)} %get-tuple-element.24), channel_id=1, source_target_pairs={{0,32},{4,12},{8,40},{12,20},{16,48},{20,28},{24,56},{28,4},{32,64... | collective-permute-start | bytes 3145736 | tf_op jit(solution)/shard_map/ppermute | solution.py:40
  147.1 29.3 %collective-permute-start.35 = (bf16[128,4096]{1,0:T(8,128)(2,1)S(1)}, bf16[128,4096]{1,0:T(8,128)(2,1)S(1)}, u32[]{:S(2)}, u32[]{:S(2)}) collective-permute-start(bf16[128,4096]{1,0:T(8,128)(2,1)S(1)} %get-tuple-element.28), channel_id=1, source_target_pairs={{0,96},{4,28},{8,104},{12,4},{16,112},{20,12},{24,120},{28,20},{32... | collective-permute-start | bytes 3145736 | tf_op jit(solution)/shard_map/ppermute | solution.py:40
  158.6 14.9 %collective-permute-start.27 = (bf16[128,4096]{1,0:T(8,128)(2,1)S(1)}, bf16[128,4096]{1,0:T(8,128)(2,1)S(1)}, u32[]{:S(2)}, u32[]{:S(2)}) collective-permute-start(bf16[128,4096]{1,0:T(8,128)(2,1)S(1)} %get-tuple-element.23), channel_id=1, source_target_pairs={{0,96},{4,28},{8,104},{12,4},{16,112},{20,12},{24,120},{28,20},{32... | collective-permute-start | bytes 3145736 | tf_op jit(solution)/shard_map/ppermute | solution.py:40
  160.3 17.0 %collective-permute-start.33 = (bf16[128,4096]{1,0:T(8,128)(2,1)S(1)}, bf16[128,4096]{1,0:T(8,128)(2,1)S(1)}, u32[]{:S(2)}, u32[]{:S(2)}) collective-permute-start(bf16[128,4096]{1,0:T(8,128)(2,1)S(1)} %add_convert_fusion.1), channel_id=1, source_target_pairs={{0,32},{4,12},{8,40},{12,20},{16,48},{20,28},{24,56},{28,4},{32,64... | collective-permute-start | bytes 3145736 | tf_op jit(solution)/shard_map/ppermute | solution.py:40
  173.8 21.8 %collective-permute-start.28 = (bf16[128,4096]{1,0:T(8,128)(2,1)S(1)}, bf16[128,4096]{1,0:T(8,128)(2,1)S(1)}, u32[]{:S(2)}, u32[]{:S(2)}) collective-permute-start(bf16[128,4096]{1,0:T(8,128)(2,1)S(1)} %add_convert_fusion.3), channel_id=1, source_target_pairs={{0,96},{4,28},{8,104},{12,4},{16,112},{20,12},{24,120},{28,20},{32... | collective-permute-start | bytes 3145736 | tf_op jit(solution)/shard_map/ppermute | solution.py:40
  177.9 18.2 %collective-permute-start.36 = (bf16[32,4096]{1,0:T(8,128)(2,1)S(1)}, bf16[32,4096]{1,0:T(8,128)(2,1)S(1)}, u32[]{:S(2)}, u32[]{:S(2)}) collective-permute-start(bf16[32,4096]{1,0:T(8,128)(2,1)S(1)} %get-tuple-element.31), channel_id=1, source_target_pairs={{0,24},{4,100},{8,0},{12,108},{16,8},{20,116},{24,16},{28,124},{32... | collective-permute-start | bytes 786440 | tf_op jit(solution)/shard_map/ppermute | solution.py:40
  182.0 17.0 %collective-permute-start.38 = (bf16[32,4096]{1,0:T(8,128)(2,1)S(1)}, bf16[32,4096]{1,0:T(8,128)(2,1)S(1)}, u32[]{:S(2)}, u32[]{:S(2)}) collective-permute-start(bf16[32,4096]{1,0:T(8,128)(2,1)S(1)} %get-tuple-element.32), channel_id=1, source_target_pairs={{0,8},{4,36},{8,16},{12,44},{16,24},{20,52},{24,0},{28,60},{32,40}... | collective-permute-start | bytes 786440 | tf_op jit(solution)/shard_map/ppermute | solution.py:40
  197.0 9.4 %collective-permute-start.37 = (bf16[64,4096]{1,0:T(8,128)(2,1)}, bf16[64,4096]{1,0:T(8,128)(2,1)S(1)}, u32[]{:S(2)}, u32[]{:S(2)}) collective-permute-start(bf16[64,4096]{1,0:T(8,128)(2,1)} %add_convert_fusion.6), channel_id=1, source_target_pairs={{0,24},{4,100},{8,0},{12,108},{16,8},{20,116},{24,16},{28,124},{32... | collective-permute-start | bytes 1572872 | tf_op jit(solution)/shard_map/ppermute | solution.py:40
  199.9 10.6 %collective-permute-start.39 = (bf16[64,4096]{1,0:T(8,128)(2,1)}, bf16[64,4096]{1,0:T(8,128)(2,1)S(1)}, u32[]{:S(2)}, u32[]{:S(2)}) collective-permute-start(bf16[64,4096]{1,0:T(8,128)(2,1)} %add_convert_fusion.5), channel_id=1, source_target_pairs={{0,8},{4,36},{8,16},{12,44},{16,24},{20,52},{24,0},{28,60},{32,40}... | collective-permute-start | bytes 1572872 | tf_op jit(solution)/shard_map/ppermute | solution.py:40
  200.3 2.1 collective-permute-start.34
  210.8 5.0 %collective-permute-start.40 = (bf16[16,4096]{1,0:T(8,128)(2,1)S(1)}, bf16[16,4096]{1,0:T(8,128)(2,1)S(1)}, u32[]{:S(2)}, u32[]{:S(2)}) collective-permute-start(bf16[16,4096]{1,0:T(8,128)(2,1)S(1)} %get-tuple-element.36), channel_id=1, source_target_pairs={{0,3},{1,0},{2,1},{3,2},{4,7},{5,4},{6,5},{7,6},{8,11},{9,8},{10,9... | collective-permute-start | bytes 393224 | tf_op jit(solution)/shard_map/ppermute | solution.py:48
  212.0 6.5 %collective-permute-start.41 = (bf16[16,4096]{1,0:T(8,128)(2,1)S(1)}, bf16[16,4096]{1,0:T(8,128)(2,1)S(1)}, u32[]{:S(2)}, u32[]{:S(2)}) collective-permute-start(bf16[16,4096]{1,0:T(8,128)(2,1)S(1)} %get-tuple-element.35), channel_id=1, source_target_pairs={{0,2},{1,3},{2,0},{3,1},{4,6},{5,7},{6,4},{7,5},{8,10},{9,11},{10,... | collective-permute-start | bytes 393224 | tf_op jit(solution)/shard_map/ppermute | solution.py:48
  213.2 6.7 %collective-permute-start.42 = (bf16[16,4096]{1,0:T(8,128)(2,1)S(1)}, bf16[16,4096]{1,0:T(8,128)(2,1)S(1)}, u32[]{:S(2)}, u32[]{:S(2)}) collective-permute-start(bf16[16,4096]{1,0:T(8,128)(2,1)S(1)} %get-tuple-element.34), channel_id=1, source_target_pairs={{0,1},{1,2},{2,3},{3,0},{4,5},{5,6},{6,7},{7,4},{8,9},{9,10},{10,1... | collective-permute-start | bytes 393224 | tf_op jit(solution)/shard_map/ppermute | solution.py:48
  (10 other events, 74.2 us)

commit v6 on v5

--- a/solution.py
+++ b/solution.py
@@ -262,7 +262,8 @@
     mine = lax.axis_index("exp").astype(i32)
     my_z, my_x, my_core = me // 8, (me // 2) % RING, me % 2
 
-    kv = jnp.concatenate((keys, values), axis=1)
+    beside = ((0, 0), (0, keys.shape[1]))
+    kv = jnp.pad(keys, beside) + jnp.pad(values, tuple(side[::-1] for side in beside))
     near = join(kv, shift(kv, 1, 1), shift(kv, 1, -1), shift(kv, 1, 2))
     left, right = shift(near, 2, 1), shift(near, 2, -1)
     far = shift(near, 2, 2)
@@ -338,13 +339,7 @@
     level = lax.ppermute(v1[:16, :128], "ctx", [(2 * i, 2 * i + 1) for i in range(16)])
     n0, n1 = total(n0, u0, v0), total(n1, u1, v1)
     part = rows.shape[0]
-    half = part // 2
-    minus, plus = n0[part:], n1[:part]
-    q0 = shift(n1[part : part + half], 1, -1)
-    q1 = shift(n1[part + half :], 1, 1)
-    minus = total(minus, jnp.pad(q0, ((0, half), (0, 0))))
-    plus = total(plus, jnp.pad(q1, ((half, 0), (0, 0))))
-    back = (shift(minus, 1, -1), shift(plus, 1, 1))
+    back = (shift(n0[part:], 1, -1), shift(n1[:part], 1, 1), shift(n1[part:], 1, 2))
     own_rows = total(n0[:part] + jnp.max(level) * 0, *back)
 
     r0, r1, r2, r3 = (own_rows[i * slot_count : (i + 1) * slot_count] for i in range(4))

time: 224 us -> 230 us (1.027); the launches traced: 221 us -> 229 us
  starting transfers between devices: 58.2 us -> 67.3 us
    ppermute x9, starting transfers between devices: 15 us -> 20.4 us  [shift_exp(): return lax.ppermute(a, 'exp', [(i, (i + step) % 4) for i in range(4)])]
    ppermute x26 -> x25, starting transfers between devices: 41.3 us -> 45 us  [shift(): return lax.ppermute(a, 'ctx', RINGS[phase, step])]
    ppermute x26 -> x25, waiting for transfers between devices: 74.2 us -> 74.2 us  [shift(): return lax.ppermute(a, 'ctx', RINGS[phase, step])]
  transfers between devices with their start and end apart: 43 -> 42, of which waited for: 24 -> 22; matrix products, arithmetic and copies ran while one was open for 4% -> 4% of each run, Pallas kernels for 18% -> 17%
where the time goes in v6:
time: 230 us; the launch traced here: 229 us
  waiting for transfers between devices  95.6 us (42%)
  starting transfers between devices  67.3 us (29%)
  Pallas kernels  49.7 us (22%)
  other arithmetic  8 us (3%)
  local copies, waits for them, and re-layouts  5.89 us (3%)
    ppermute x25, waiting for transfers between devices, shift(): return lax.ppermute(a, 'ctx', RINGS[phase, step])  74.2 us
    ppermute x25, starting transfers between devices, shift(): return lax.ppermute(a, 'ctx', RINGS[phase, step])  45 us
    pallas_call x4, Pallas kernels, expert_rows(): pl.pallas_call(kernel, out_shape=tuple((jax.ShapeDtypeStruct((size, width...  39.2 us
    ppermute x9, starting transfers between devices, shift_exp(): return lax.ppermute(a, 'exp', [(i, (i + step) % 4) for i in range(4)])  20.4 us
    ppermute x9, waiting for transfers between devices, shift_exp(): return lax.ppermute(a, 'exp', [(i, (i + step) % 4) for i in range(4)])  18.8 us
    pallas_call x1, Pallas kernels, attend(): pl.pallas_call(kernel, out_shape=tuple((jax.ShapeDtypeStruct((sub, width)...  10.4 us
  transfers between devices with their start and end apart: 42, of which 22 were waited for; matrix products, arithmetic and copies ran while one was open for 4% of the time, Pallas kernels for 17%

profile of v6, /device:TPU:0, one launch (start us, length us, event | category | flops | bytes accessed | tf_op | source)
XLA Modules:
  0.0 229.3 jit_solution(9302515928550810574)
XLA Ops:
  0.9 1.7 collective-permute-start
  2.6 1.6 collective-permute-start.1
  4.2 1.9 collective-permute-start.2
  8.8 1.9 collective-permute-done.2
  10.7 2.1 collective-permute-start.4
  12.8 2.2 collective-permute-start.6
  15.0 1.8 collective-permute-start.8
  18.1 4.0 %collective-permute-done.4.refs_2_ = bf16[512,512]{1,0:T(8,128)(2,1)S(1)} collective-permute-done((bf16[512,512]{1,0:T(8,128)(2,1)S(1)}, bf16[512,512]{1,0:T(8,128)(2,1)S(1)}, u32[]{:S(2)}, u32[]{:S(2)}) %collective-permute-start.4) | collective-permute-done | bytes 524320 | tf_op jit(solution)/shard_map/ppermute | solution.py:40
  22.1 5.3 %collective-permute-done.6.refs_4_ = bf16[512,512]{1,0:T(8,128)(2,1)S(1)} collective-permute-done((bf16[512,512]{1,0:T(8,128)(2,1)S(1)}, bf16[512,512]{1,0:T(8,128)(2,1)S(1)}, u32[]{:S(2)}, u32[]{:S(2)}) %collective-permute-start.6) | collective-permute-done | bytes 524320 | tf_op jit(solution)/shard_map/ppermute | solution.py:40
  27.4 1.8 collective-permute-done.8.refs_6_
  29.4 1.8 collective-permute-done.9.refs_7_
  32.3 10.4 %attend.1 = (f32[32,4096]{1,0:T(8,128)S(1)}, bf16[32,4096]{1,0:T(8,128)(2,1)S(1)}, bf16[32,4096]{1,0:T(8,128)(2,1)S(1)}, bf16[32,4096]{1,0:T(8,128)(2,1)S(1)}) custom-call(s32[1]{0:T(128)} %bitcast.mine_ref, bf16[128,1024]{1,0:T(8,128)(2,1)S(1)} %copy-done.4, s32[128,128]{1,0:T(8,128)S(1)} %broadcast_in_dim.125.qpos_ref, ...), custom_call_target="tpu_custom_call" | custom-call | flops 4294967296 | bytes 4194304 | tf_op jit(solution)/shard_map/attend/pallas_call | solution.py:136
  42.8 3.3 %collective-permute-start.10 = (bf16[32,4096]{1,0:T(8,128)(2,1)S(1)}, bf16[32,4096]{1,0:T(8,128)(2,1)S(1)}, u32[]{:S(2)}, u32[]{:S(2)}) collective-permute-start(bf16[32,4096]{1,0:T(8,128)(2,1)S(1)} %get-tuple-element.18), channel_id=1, source_target_pairs={{0,2},{1,3},{2,0},{3,1},{4,6},{5,7},{6,4},{7,5},{8,10},{9,11},{10,... | collective-permute-start | bytes 786440 | tf_op jit(solution)/shard_map/ppermute | solution.py:48
  46.7 2.6 %collective-permute-start.12 = (bf16[32,4096]{1,0:T(8,128)(2,1)S(1)}, bf16[32,4096]{1,0:T(8,128)(2,1)S(1)}, u32[]{:S(2)}, u32[]{:S(2)}) collective-permute-start(bf16[32,4096]{1,0:T(8,128)(2,1)S(1)} %get-tuple-element.20), channel_id=1, source_target_pairs={{0,3},{1,0},{2,1},{3,2},{4,7},{5,4},{6,5},{7,6},{8,11},{9,8},{10,9... | collective-permute-start | bytes 786440 | tf_op jit(solution)/shard_map/ppermute | solution.py:48
  49.8 3.8 %collective-permute-done.10 = bf16[32,4096]{1,0:T(8,128)(2,1)S(1)} collective-permute-done((bf16[32,4096]{1,0:T(8,128)(2,1)S(1)}, bf16[32,4096]{1,0:T(8,128)(2,1)S(1)}, u32[]{:S(2)}, u32[]{:S(2)}) %collective-permute-start.10) | collective-permute-done | bytes 262176 | tf_op jit(solution)/shard_map/ppermute | solution.py:48
  53.6 4.7 %collective-permute-done.11 = bf16[32,4096]{1,0:T(8,128)(2,1)S(1)} collective-permute-done((bf16[32,4096]{1,0:T(8,128)(2,1)S(1)}, bf16[32,4096]{1,0:T(8,128)(2,1)S(1)}, u32[]{:S(2)}, u32[]{:S(2)}) %collective-permute-start.11) | collective-permute-done | bytes 262176 | tf_op jit(solution)/shard_map/ppermute | solution.py:48
  59.4 1.4 collective-permute-start.13
  60.9 2.7 %collective-permute-start.14 = (bf16[16,4096]{1,0:T(8,128)(2,1)S(1)}, bf16[16,4096]{1,0:T(8,128)(2,1)S(1)}, u32[]{:S(2)}, u32[]{:S(2)}) collective-permute-start(bf16[16,4096]{1,0:T(8,128)(2,1)S(1)} %get-tuple-element.40), channel_id=1, source_target_pairs={{0,2},{1,3},{2,0},{3,1},{4,6},{5,7},{6,4},{7,5},{8,10},{9,11},{10,... | collective-permute-start | bytes 393224 | tf_op jit(solution)/shard_map/ppermute | solution.py:48
  65.8 4.0 %collective-permute-done.14 = bf16[16,4096]{1,0:T(8,128)(2,1)S(1)} collective-permute-done((bf16[16,4096]{1,0:T(8,128)(2,1)S(1)}, bf16[16,4096]{1,0:T(8,128)(2,1)S(1)}, u32[]{:S(2)}, u32[]{:S(2)}) %collective-permute-start.14) | collective-permute-done | bytes 131104 | tf_op jit(solution)/shard_map/ppermute | solution.py:48
  69.9 1.6 collective-permute-start.17
  72.0 9.8 %collective-permute-done.16 = bf16[64,4096]{1,0:T(8,128)(2,1)S(1)} collective-permute-done((bf16[64,4096]{1,0:T(8,128)(2,1)S(1)}, bf16[64,4096]{1,0:T(8,128)(2,1)S(1)}, u32[]{:S(2)}, u32[]{:S(2)}) %collective-permute-start.16) | collective-permute-done | bytes 524320 | tf_op jit(solution)/shard_map/ppermute | solution.py:40
  82.2 3.3 %collective-permute-start.19 = (bf16[32,4096]{1,0:T(8,128)(2,1)S(1)}, bf16[32,4096]{1,0:T(8,128)(2,1)S(1)}, u32[]{:S(2)}, u32[]{:S(2)}) collective-permute-start(bf16[32,4096]{1,0:T(8,128)(2,1)S(1)} %slice.65), channel_id=1, source_target_pairs={{0,24},{4,100},{8,0},{12,108},{16,8},{20,116},{24,16},{28,124},{32... | collective-permute-start | bytes 786440 | tf_op jit(solution)/shard_map/ppermute | solution.py:40
  85.5 4.2 %collective-permute-done.18 = bf16[32,4096]{1,0:T(8,128)(2,1)S(1)} collective-permute-done((bf16[32,4096]{1,0:T(8,128)(2,1)S(1)}, bf16[32,4096]{1,0:T(8,128)(2,1)S(1)}, u32[]{:S(2)}, u32[]{:S(2)}) %collective-permute-start.18) | collective-permute-done | bytes 262176 | tf_op jit(solution)/shard_map/ppermute | solution.py:40
  89.7 2.0 collective-permute-start.23
  91.8 1.7 collective-permute-start.24
  93.5 12.6 %collective-permute-done.23.refs_0_ = bf16[128,4096]{1,0:T(8,128)(2,1)S(1)} collective-permute-done((bf16[128,4096]{1,0:T(8,128)(2,1)S(1)}, bf16[128,4096]{1,0:T(8,128)(2,1)S(1)}, u32[]{:S(2)}, u32[]{:S(2)}) %collective-permute-start.23) | collective-permute-done | bytes 1048608 | tf_op jit(solution)/shard_map/ppermute | solution.py:40
  106.7 2.8 %collective-permute-start.26 = (bf16[128,4096]{1,0:T(8,128)(2,1)S(1)}, bf16[128,4096]{1,0:T(8,128)(2,1)S(1)}, u32[]{:S(2)}, u32[]{:S(2)}) collective-permute-start(bf16[128,4096]{1,0:T(8,128)(2,1)S(1)} %collective-permute-done.24.refs_1_), channel_id=1, source_target_pairs={{0,96},{4,28},{8,104},{12,4},{16,112},{20,12},{24,120},{28,20},{32... | collective-permute-start | bytes 3145736 | tf_op jit(solution)/shard_map/ppermute | solution.py:40
  111.5 10.6 %collective-permute-done.25.refs_0_ = bf16[128,4096]{1,0:T(8,128)(2,1)S(1)} collective-permute-done((bf16[128,4096]{1,0:T(8,128)(2,1)S(1)}, bf16[128,4096]{1,0:T(8,128)(2,1)S(1)}, u32[]{:S(2)}, u32[]{:S(2)}) %collective-permute-start.25) | collective-permute-done | bytes 1048608 | tf_op jit(solution)/shard_map/ppermute | solution.py:40
  122.2 2.0 copy-done.3
  124.2 9.8 %expert_rows.6 = (bf16[128,4096]{1,0:T(8,128)(2,1)S(1)}, bf16[128,4096]{1,0:T(8,128)(2,1)S(1)}) custom-call(bf16[128,4096]{1,0:T(8,128)(2,1)S(1)} %collective-permute-done.25.refs_0_, bf16[128,4096]{1,0:T(8,128)(2,1)S(1)} %collective-permute-done.26.refs_1_, bf16[448,4096]{1,0:T(8,128)(2,1)S(1)} %bitcast.29, bf16[448,4096]{1,0:T(8,128)(2,1)S(1)} %bitcast.34, ...), custom_call_target="tpu_custom_call" | custom-call | flops 5637144576 | bytes 22020096 | tf_op jit(solution)/shard_map/expert_rows/pallas_call | solution.py:222
  134.0 3.4 %collective-permute-start.27 = (bf16[128,4096]{1,0:T(8,128)(2,1)S(1)}, bf16[128,4096]{1,0:T(8,128)(2,1)S(1)}, u32[]{:S(2)}, u32[]{:S(2)}) collective-permute-start(bf16[128,4096]{1,0:T(8,128)(2,1)S(1)} %get-tuple-element.23), channel_id=1, source_target_pairs={{0,96},{4,28},{8,104},{12,4},{16,112},{20,12},{24,120},{28,20},{32... | collective-permute-start | bytes 3145736 | tf_op jit(solution)/shard_map/ppermute | solution.py:40
  137.5 9.8 %expert_rows.7 = (bf16[128,4096]{1,0:T(8,128)(2,1)S(1)}, bf16[128,4096]{1,0:T(8,128)(2,1)S(1)}) custom-call(bf16[128,4096]{1,0:T(8,128)(2,1)S(1)} %collective-permute-done.29.refs_0_, bf16[128,4096]{1,0:T(8,128)(2,1)S(1)} %collective-permute-done.30.refs_1_, bf16[448,4096]{1,0:T(8,128)(2,1)S(1)} %bitcast.30, bf16[448,4096]{1,0:T(8,128)(2,1)S(1)} %bitcast.35, ...), custom_call_target="tpu_custom_call" | custom-call | flops 5637144576 | bytes 22020096 | tf_op jit(solution)/shard_map/expert_rows/pallas_call | solution.py:222
  147.4 3.2 %collective-permute-start.36 = (bf16[128,4096]{1,0:T(8,128)(2,1)S(1)}, bf16[128,4096]{1,0:T(8,128)(2,1)S(1)}, u32[]{:S(2)}, u32[]{:S(2)}) collective-permute-start(bf16[128,4096]{1,0:T(8,128)(2,1)S(1)} %get-tuple-element.28), channel_id=1, source_target_pairs={{0,96},{4,28},{8,104},{12,4},{16,112},{20,12},{24,120},{28,20},{32... | collective-permute-start | bytes 3145736 | tf_op jit(solution)/shard_map/ppermute | solution.py:40
  150.6 9.8 %expert_rows.5 = (bf16[128,4096]{1,0:T(8,128)(2,1)S(1)}, bf16[128,4096]{1,0:T(8,128)(2,1)S(1)}) custom-call(bf16[128,4096]{1,0:T(8,128)(2,1)S(1)} %collective-permute-done.23.refs_0_, bf16[128,4096]{1,0:T(8,128)(2,1)S(1)} %collective-permute-done.24.refs_1_, bf16[448,4096]{1,0:T(8,128)(2,1)S(1)} %bitcast.31, bf16[448,4096]{1,0:T(8,128)(2,1)S(1)} %bitcast.36, ...), custom_call_target="tpu_custom_call" | custom-call | flops 5637144576 | bytes 22020096 | tf_op jit(solution)/shard_map/expert_rows/pallas_call | solution.py:222
  160.7 3.5 %collective-permute-start.28 = (bf16[128,4096]{1,0:T(8,128)(2,1)S(1)}, bf16[128,4096]{1,0:T(8,128)(2,1)S(1)}, u32[]{:S(2)}, u32[]{:S(2)}) collective-permute-start(bf16[128,4096]{1,0:T(8,128)(2,1)S(1)} %add_convert_fusion.3), channel_id=1, source_target_pairs={{0,96},{4,28},{8,104},{12,4},{16,112},{20,12},{24,120},{28,20},{32... | collective-permute-start | bytes 3145736 | tf_op jit(solution)/shard_map/ppermute | solution.py:40
  164.2 10.4 %collective-permute-done.32 = bf16[128,4096]{1,0:T(8,128)(2,1)S(1)} collective-permute-done((bf16[128,4096]{1,0:T(8,128)(2,1)S(1)}, bf16[128,4096]{1,0:T(8,128)(2,1)S(1)}, u32[]{:S(2)}, u32[]{:S(2)}) %collective-permute-start.32) | collective-permute-done | bytes 1048608 | tf_op jit(solution)/shard_map/ppermute | solution.py:40
  174.9 9.8 %expert_rows.4 = (bf16[128,4096]{1,0:T(8,128)(2,1)S(1)}, bf16[128,4096]{1,0:T(8,128)(2,1)S(1)}) custom-call(bf16[128,4096]{1,0:T(8,128)(2,1)S(1)} %constant_dynamic-update-slice_fusion.refs_0_, bf16[128,4096]{1,0:T(8,128)(2,1)S(1)} %constant_dynamic-update-slice_fusion.5.refs_1_, bf16[448,4096]{1,0:T(8,128)(2,1)S(1)} %bitcast.32, ...), custom_call_target="tpu_custom_call" | custom-call | flops 5637144576 | bytes 22020096 | tf_op jit(solution)/shard_map/expert_rows/pallas_call | solution.py:222
  185.3 2.3 %collective-permute-start.35 = (bf16[64,4096]{1,0:T(8,128)(2,1)S(1)}, bf16[64,4096]{1,0:T(8,128)(2,1)S(1)}, u32[]{:S(2)}, u32[]{:S(2)}) collective-permute-start(bf16[64,4096]{1,0:T(8,128)(2,1)S(1)} %slice.68), channel_id=1, source_target_pairs={{0,24},{4,100},{8,0},{12,108},{16,8},{20,116},{24,16},{28,124},{32... | collective-permute-start | bytes 1572872 | tf_op jit(solution)/shard_map/ppermute | solution.py:40
  187.6 4.0 %collective-permute-done.33 = bf16[128,4096]{1,0:T(8,128)(2,1)S(1)} collective-permute-done((bf16[128,4096]{1,0:T(8,128)(2,1)S(1)}, bf16[128,4096]{1,0:T(8,128)(2,1)S(1)}, u32[]{:S(2)}, u32[]{:S(2)}) %collective-permute-start.33) | collective-permute-done | bytes 1048608 | tf_op jit(solution)/shard_map/ppermute | solution.py:40
  193.2 6.4 %collective-permute-start.38 = (bf16[64,4096]{1,0:T(8,128)(2,1)}, bf16[64,4096]{1,0:T(8,128)(2,1)}, u32[]{:S(2)}, u32[]{:S(2)}) collective-permute-start(bf16[64,4096]{1,0:T(8,128)(2,1)} %get-tuple-element.32), channel_id=1, source_target_pairs={{0,16},{4,68},{8,24},{12,76},{16,0},{20,84},{24,8},{28,92},{32,48}... | collective-permute-start | bytes 1572872 | tf_op jit(solution)/shard_map/ppermute | solution.py:40
  203.4 2.2 collective-permute-done.37
  205.6 7.1 %collective-permute-done.38 = bf16[64,4096]{1,0:T(8,128)(2,1)} collective-permute-done((bf16[64,4096]{1,0:T(8,128)(2,1)}, bf16[64,4096]{1,0:T(8,128)(2,1)}, u32[]{:S(2)}, u32[]{:S(2)}) %collective-permute-start.38) | collective-permute-done | bytes 524320 | tf_op jit(solution)/shard_map/ppermute | solution.py:40
  212.7 1.5 add_convert_fusion.4
  214.3 1.6 collective-permute-start.39
  215.9 6.2 %collective-permute-start.40 = (bf16[16,4096]{1,0:T(8,128)(2,1)S(1)}, bf16[16,4096]{1,0:T(8,128)(2,1)S(1)}, u32[]{:S(2)}, u32[]{:S(2)}) collective-permute-start(bf16[16,4096]{1,0:T(8,128)(2,1)S(1)} %get-tuple-element.35), channel_id=1, source_target_pairs={{0,2},{1,3},{2,0},{3,1},{4,6},{5,7},{6,4},{7,5},{8,10},{9,11},{10,... | collective-permute-start | bytes 393224 | tf_op jit(solution)/shard_map/ppermute | solution.py:48
  222.1 1.3 collective-permute-start.41
  223.5 1.5 collective-permute-done.40
  225.0 3.2 %collective-permute-done.41 = bf16[16,4096]{1,0:T(8,128)(2,1)S(1)} collective-permute-done((bf16[16,4096]{1,0:T(8,128)(2,1)S(1)}, bf16[16,4096]{1,0:T(8,128)(2,1)S(1)}, u32[]{:S(2)}, u32[]{:S(2)}) %collective-permute-start.41) | collective-permute-done | bytes 131104 | tf_op jit(solution)/shard_map/ppermute | solution.py:48
  (143 shorter events, 21.1 us)
Async XLA Ops:
  0.0 199.6 %copy-start = (f32[4096,4]{0,1:T(4,128)S(1)}, f32[4096,4]{0,1:T(4,128)}, u32[]{:S(2)}) copy-start(f32[4096,4]{0,1:T(4,128)} %param.27) | copy-start | bytes 196612
  0.9 7.8 %collective-permute-start = (bf16[128,512]{1,0:T(8,128)(2,1)S(1)}, bf16[128,512]{1,0:T(8,128)(2,1)S(1)}, u32[]{:S(2)}, u32[]{:S(2)}) collective-permute-start(bf16[128,512]{1,0:T(8,128)(2,1)S(1)} %pad_add_fusion), channel_id=1, source_target_pairs={{0,8},{4,36},{8,16},{12,44},{16,24},{20,52},{24,0},{28,60},{32,40}... | collective-permute-start | bytes 393224 | tf_op jit(solution)/shard_map/ppermute | solution.py:40
  2.6 6.2 %collective-permute-start.1 = (bf16[128,512]{1,0:T(8,128)(2,1)S(1)}, bf16[128,512]{1,0:T(8,128)(2,1)S(1)}, u32[]{:S(2)}, u32[]{:S(2)}) collective-permute-start(bf16[128,512]{1,0:T(8,128)(2,1)S(1)} %pad_add_fusion), channel_id=1, source_target_pairs={{0,24},{4,100},{8,0},{12,108},{16,8},{20,116},{24,16},{28,124},{32... | collective-permute-start | bytes 393224 | tf_op jit(solution)/shard_map/ppermute | solution.py:40
  4.2 6.5 %collective-permute-start.2 = (bf16[128,512]{1,0:T(8,128)(2,1)S(1)}, bf16[128,512]{1,0:T(8,128)(2,1)S(1)}, u32[]{:S(2)}, u32[]{:S(2)}) collective-permute-start(bf16[128,512]{1,0:T(8,128)(2,1)S(1)} %pad_add_fusion), channel_id=1, source_target_pairs={{0,16},{4,68},{8,24},{12,76},{16,0},{20,84},{24,8},{28,92},{32,48}... | collective-permute-start | bytes 393224 | tf_op jit(solution)/shard_map/ppermute | solution.py:40
  10.7 20.6 %copy-start.7 = (bf16[512,512]{1,0:T(8,128)(2,1)}, bf16[512,512]{1,0:T(8,128)(2,1)S(1)}, u32[]{:S(2)}) copy-start(bf16[512,512]{1,0:T(8,128)(2,1)S(1)} %pad_maximum_fusion.refs_0_) | copy-start | bytes 1572868
  10.7 11.4 %collective-permute-start.4 = (bf16[512,512]{1,0:T(8,128)(2,1)S(1)}, bf16[512,512]{1,0:T(8,128)(2,1)S(1)}, u32[]{:S(2)}, u32[]{:S(2)}) collective-permute-start(bf16[512,512]{1,0:T(8,128)(2,1)S(1)} %pad_maximum_fusion.refs_0_), channel_id=1, source_target_pairs={{0,32},{4,12},{8,40},{12,20},{16,48},{20,28},{24,56},{28,4},{32,64... | collective-permute-start | bytes 1572872 | tf_op jit(solution)/shard_map/ppermute | solution.py:40
  12.8 14.6 %collective-permute-start.6 = (bf16[512,512]{1,0:T(8,128)(2,1)S(1)}, bf16[512,512]{1,0:T(8,128)(2,1)S(1)}, u32[]{:S(2)}, u32[]{:S(2)}) collective-permute-start(bf16[512,512]{1,0:T(8,128)(2,1)S(1)} %pad_maximum_fusion.refs_0_), channel_id=1, source_target_pairs={{0,96},{4,28},{8,104},{12,4},{16,112},{20,12},{24,120},{28,20},{32... | collective-permute-start | bytes 1572872 | tf_op jit(solution)/shard_map/ppermute | solution.py:40
  15.0 14.2 %collective-permute-start.8 = (bf16[512,512]{1,0:T(8,128)(2,1)S(1)}, bf16[512,512]{1,0:T(8,128)(2,1)S(1)}, u32[]{:S(2)}, u32[]{:S(2)}) collective-permute-start(bf16[512,512]{1,0:T(8,128)(2,1)S(1)} %pad_maximum_fusion.refs_0_), channel_id=1, source_target_pairs={{0,64},{4,20},{8,72},{12,28},{16,80},{20,4},{24,88},{28,12},{32,96... | collective-permute-start | bytes 1572872 | tf_op jit(solution)/shard_map/ppermute | solution.py:40
  18.0 11.4 %collective-permute-start.3 = (bf16[512,512]{1,0:T(8,128)(2,1)S(1)}, bf16[512,512]{1,0:T(8,128)(2,1)S(1)}, u32[]{:S(2)}, u32[]{:S(2)}) collective-permute-start(bf16[512,512]{1,0:T(8,128)(2,1)S(1)} %pad_maximum_fusion.refs_0_), channel_id=1, source_target_pairs={{0,4},{4,0},{8,12},{12,8},{16,20},{20,16},{24,28},{28,24},{32,36},... | collective-permute-start | bytes 1572872 | tf_op jit(solution)/shard_map/ppermute | solution.py:44
  22.1 7.3 %collective-permute-start.5 = (bf16[512,512]{1,0:T(8,128)(2,1)S(1)}, bf16[512,512]{1,0:T(8,128)(2,1)}, u32[]{:S(2)}, u32[]{:S(2)}) collective-permute-start(bf16[512,512]{1,0:T(8,128)(2,1)S(1)} %collective-permute-done.4.refs_2_), channel_id=1, source_target_pairs={{0,4},{4,0},{8,12},{12,8},{16,20},{20,16},{24,28},{28,24},{32,36},... | collective-permute-start | bytes 1572872 | tf_op jit(solution)/shard_map/ppermute | solution.py:44
  27.4 2.0 collective-permute-start.7
  29.2 2.0 collective-permute-start.9
  32.3 17.0 %copy-start.10 = (s32[32,2]{0,1:T(2,128)S(1)}, s32[32,2]{0,1:T(2,128)}, u32[]{:S(2)}) copy-start(s32[32,2]{0,1:T(2,128)} %param.28) | copy-start | bytes 772
  32.3 26.4 %copy-start.8 = (bf16[32,4096]{1,0:T(8,128)(2,1)S(1)}, bf16[32,4096]{1,0:T(8,128)(2,1)}, u32[]{:S(2)}) copy-start(bf16[32,4096]{1,0:T(8,128)(2,1)} %param.23) | copy-start | bytes 786436
  32.3 26.7 %copy-start.9 = (f32[4096]{0:T(1024)S(1)}, f32[4096]{0:T(1024)}, u32[]{:S(2)}) copy-start(f32[4096]{0:T(1024)} %param.26) | copy-start | bytes 49156
  42.8 10.8 %collective-permute-start.10 = (bf16[32,4096]{1,0:T(8,128)(2,1)S(1)}, bf16[32,4096]{1,0:T(8,128)(2,1)S(1)}, u32[]{:S(2)}, u32[]{:S(2)}) collective-permute-start(bf16[32,4096]{1,0:T(8,128)(2,1)S(1)} %get-tuple-element.18), channel_id=1, source_target_pairs={{0,2},{1,3},{2,0},{3,1},{4,6},{5,7},{6,4},{7,5},{8,10},{9,11},{10,... | collective-permute-start | bytes 786440 | tf_op jit(solution)/shard_map/ppermute | solution.py:48
  46.1 12.3 %collective-permute-start.11 = (bf16[32,4096]{1,0:T(8,128)(2,1)S(1)}, bf16[32,4096]{1,0:T(8,128)(2,1)S(1)}, u32[]{:S(2)}, u32[]{:S(2)}) collective-permute-start(bf16[32,4096]{1,0:T(8,128)(2,1)S(1)} %get-tuple-element.19), channel_id=1, source_target_pairs={{0,1},{1,2},{2,3},{3,0},{4,5},{5,6},{6,7},{7,4},{8,9},{9,10},{10,1... | collective-permute-start | bytes 786440 | tf_op jit(solution)/shard_map/ppermute | solution.py:48
  46.7 12.0 %collective-permute-start.12 = (bf16[32,4096]{1,0:T(8,128)(2,1)S(1)}, bf16[32,4096]{1,0:T(8,128)(2,1)S(1)}, u32[]{:S(2)}, u32[]{:S(2)}) collective-permute-start(bf16[32,4096]{1,0:T(8,128)(2,1)S(1)} %get-tuple-element.20), channel_id=1, source_target_pairs={{0,3},{1,0},{2,1},{3,2},{4,7},{5,4},{6,5},{7,6},{8,11},{9,8},{10,9... | collective-permute-start | bytes 786440 | tf_op jit(solution)/shard_map/ppermute | solution.py:48
  59.4 6.4 %collective-permute-start.13 = (bf16[16,4096]{1,0:T(8,128)(2,1)S(1)}, bf16[16,4096]{1,0:T(8,128)(2,1)S(1)}, u32[]{:S(2)}, u32[]{:S(2)}) collective-permute-start(bf16[16,4096]{1,0:T(8,128)(2,1)S(1)} %get-tuple-element.41), channel_id=1, source_target_pairs={{0,1},{1,2},{2,3},{3,0},{4,5},{5,6},{6,7},{7,4},{8,9},{9,10},{10,1... | collective-permute-start | bytes 393224 | tf_op jit(solution)/shard_map/ppermute | solution.py:48
  60.9 8.9 %collective-permute-start.14 = (bf16[16,4096]{1,0:T(8,128)(2,1)S(1)}, bf16[16,4096]{1,0:T(8,128)(2,1)S(1)}, u32[]{:S(2)}, u32[]{:S(2)}) collective-permute-start(bf16[16,4096]{1,0:T(8,128)(2,1)S(1)} %get-tuple-element.40), channel_id=1, source_target_pairs={{0,2},{1,3},{2,0},{3,1},{4,6},{5,7},{6,4},{7,5},{8,10},{9,11},{10,... | collective-permute-start | bytes 393224 | tf_op jit(solution)/shard_map/ppermute | solution.py:48
  63.6 6.2 %collective-permute-start.15 = (bf16[16,4096]{1,0:T(8,128)(2,1)S(1)}, bf16[16,4096]{1,0:T(8,128)(2,1)S(1)}, u32[]{:S(2)}, u32[]{:S(2)}) collective-permute-start(bf16[16,4096]{1,0:T(8,128)(2,1)S(1)} %get-tuple-element.39), channel_id=1, source_target_pairs={{0,3},{1,0},{2,1},{3,2},{4,7},{5,4},{6,5},{7,6},{8,11},{9,8},{10,9... | collective-permute-start | bytes 393224 | tf_op jit(solution)/shard_map/ppermute | solution.py:48
  64.2 45.3 %collective-permute-start.20 = (bf16[448,4096]{1,0:T(8,128)(2,1)S(1)}, bf16[448,4096]{1,0:T(8,128)(2,1)S(1)}, u32[]{:S(2)}, u32[]{:S(2)}) collective-permute-start(bf16[448,4096]{1,0:T(8,128)(2,1)S(1)} %bitcast.28), channel_id=1, source_target_pairs={{0,4},{4,0},{8,12},{12,8},{16,20},{20,16},{24,28},{28,24},{32,36},... | collective-permute-start | bytes 11010056 | tf_op jit(solution)/shard_map/ppermute | solution.py:44
  64.2 46.1 %collective-permute-start.21 = (bf16[448,4096]{1,0:T(8,128)(2,1)}, bf16[448,4096]{1,0:T(8,128)(2,1)S(1)}, u32[]{:S(2)}, u32[]{:S(2)}) collective-permute-start(bf16[448,4096]{1,0:T(8,128)(2,1)} %bitcast.33), channel_id=1, source_target_pairs={{0,4},{4,0},{8,12},{12,8},{16,20},{20,16},{24,28},{28,24},{32,36},... | collective-permute-start | bytes 11010056 | tf_op jit(solution)/shard_map/ppermute | solution.py:44
  65.8 45.7 %collective-permute-start.22 = (bf16[448,4096]{1,0:T(8,128)(2,1)}, bf16[448,4096]{1,0:T(8,128)(2,1)S(1)}, u32[]{:S(2)}, u32[]{:S(2)}) collective-permute-start(bf16[448,4096]{1,0:T(8,128)(2,1)} %bitcast.38), channel_id=1, source_target_pairs={{0,4},{4,0},{8,12},{12,8},{16,20},{20,16},{24,28},{28,24},{32,36},... | collective-permute-start | bytes 11010056 | tf_op jit(solution)/shard_map/ppermute | solution.py:44
  69.9 12.3 %collective-permute-start.17 = (bf16[64,4096]{1,0:T(8,128)(2,1)S(1)}, bf16[64,4096]{1,0:T(8,128)(2,1)S(1)}, u32[]{:S(2)}, u32[]{:S(2)}) collective-permute-start(bf16[64,4096]{1,0:T(8,128)(2,1)S(1)} %pad_maximum_fusion.1), channel_id=1, source_target_pairs={{0,24},{4,100},{8,0},{12,108},{16,8},{20,116},{24,16},{28,124},{32... | collective-permute-start | bytes 1572872 | tf_op jit(solution)/shard_map/ppermute | solution.py:40
  71.5 10.4 %collective-permute-start.16 = (bf16[64,4096]{1,0:T(8,128)(2,1)S(1)}, bf16[64,4096]{1,0:T(8,128)(2,1)S(1)}, u32[]{:S(2)}, u32[]{:S(2)}) collective-permute-start(bf16[64,4096]{1,0:T(8,128)(2,1)S(1)} %pad_maximum_fusion.1), channel_id=1, source_target_pairs={{0,8},{4,36},{8,16},{12,44},{16,24},{20,52},{24,0},{28,60},{32,40}... | collective-permute-start | bytes 1572872 | tf_op jit(solution)/shard_map/ppermute | solution.py:40
  72.0 50.2 %copy-start.2 = (bf16[1,4096,448]{1,2,0:T(8,128)(2,1)S(1)}, bf16[1,4096,448]{1,2,0:T(8,128)(2,1)}, u32[]{:S(2)}) copy-start(bf16[1,4096,448]{1,2,0:T(8,128)(2,1)} %param.30) | copy-start | bytes 11010052
  81.9 7.8 %collective-permute-start.18 = (bf16[32,4096]{1,0:T(8,128)(2,1)S(1)}, bf16[32,4096]{1,0:T(8,128)(2,1)S(1)}, u32[]{:S(2)}, u32[]{:S(2)}) collective-permute-start(bf16[32,4096]{1,0:T(8,128)(2,1)S(1)} %slice.64), channel_id=1, source_target_pairs={{0,8},{4,36},{8,16},{12,44},{16,24},{20,52},{24,0},{28,60},{32,40}... | collective-permute-start | bytes 786440 | tf_op jit(solution)/shard_map/ppermute | solution.py:40
  82.2 9.6 %collective-permute-start.19 = (bf16[32,4096]{1,0:T(8,128)(2,1)S(1)}, bf16[32,4096]{1,0:T(8,128)(2,1)S(1)}, u32[]{:S(2)}, u32[]{:S(2)}) collective-permute-start(bf16[32,4096]{1,0:T(8,128)(2,1)S(1)} %slice.65), channel_id=1, source_target_pairs={{0,24},{4,100},{8,0},{12,108},{16,8},{20,116},{24,16},{28,124},{32... | collective-permute-start | bytes 786440 | tf_op jit(solution)/shard_map/ppermute | solution.py:40
  89.7 16.4 %collective-permute-start.23 = (bf16[128,4096]{1,0:T(8,128)(2,1)S(1)}, bf16[128,4096]{1,0:T(8,128)(2,1)S(1)}, u32[]{:S(2)}, u32[]{:S(2)}) collective-permute-start(bf16[128,4096]{1,0:T(8,128)(2,1)S(1)} %constant_dynamic-update-slice_fusion.refs_0_), channel_id=1, source_target_pairs={{0,32},{4,12},{8,40},{12,20},{16,48},{20,28},{24,56},{28,4},{32,64... | collective-permute-start | bytes 3145736 | tf_op jit(solution)/shard_map/ppermute | solution.py:40
  91.8 14.9 %collective-permute-start.24 = (bf16[128,4096]{1,0:T(8,128)(2,1)S(1)}, bf16[128,4096]{1,0:T(8,128)(2,1)S(1)}, u32[]{:S(2)}, u32[]{:S(2)}) collective-permute-start(bf16[128,4096]{1,0:T(8,128)(2,1)S(1)} %constant_dynamic-update-slice_fusion.5.refs_1_), channel_id=1, source_target_pairs={{0,96},{4,28},{8,104},{12,4},{16,112},{20,12},{24,120},{28,20},{32... | collective-permute-start | bytes 3145736 | tf_op jit(solution)/shard_map/ppermute | solution.py:40
  106.1 16.0 %collective-permute-start.25 = (bf16[128,4096]{1,0:T(8,128)(2,1)S(1)}, bf16[128,4096]{1,0:T(8,128)(2,1)S(1)}, u32[]{:S(2)}, u32[]{:S(2)}) collective-permute-start(bf16[128,4096]{1,0:T(8,128)(2,1)S(1)} %collective-permute-done.23.refs_0_), channel_id=1, source_target_pairs={{0,32},{4,12},{8,40},{12,20},{16,48},{20,28},{24,56},{28,4},{32,64... | collective-permute-start | bytes 3145736 | tf_op jit(solution)/shard_map/ppermute | solution.py:40
  106.7 15.5 %collective-permute-start.26 = (bf16[128,4096]{1,0:T(8,128)(2,1)S(1)}, bf16[128,4096]{1,0:T(8,128)(2,1)S(1)}, u32[]{:S(2)}, u32[]{:S(2)}) collective-permute-start(bf16[128,4096]{1,0:T(8,128)(2,1)S(1)} %collective-permute-done.24.refs_1_), channel_id=1, source_target_pairs={{0,96},{4,28},{8,104},{12,4},{16,112},{20,12},{24,120},{28,20},{32... | collective-permute-start | bytes 3145736 | tf_op jit(solution)/shard_map/ppermute | solution.py:40
  109.5 27.9 %collective-permute-start.30 = (bf16[128,4096]{1,0:T(8,128)(2,1)S(1)}, bf16[128,4096]{1,0:T(8,128)(2,1)S(1)}, u32[]{:S(2)}, u32[]{:S(2)}) collective-permute-start(bf16[128,4096]{1,0:T(8,128)(2,1)S(1)} %constant_dynamic-update-slice_fusion.refs_0_), channel_id=1, source_target_pairs={{0,96},{4,28},{8,104},{12,4},{16,112},{20,12},{24,120},{28,20},{32... | collective-permute-start | bytes 3145736 | tf_op jit(solution)/shard_map/ppermute | solution.py:40
  110.3 27.1 %collective-permute-start.29 = (bf16[128,4096]{1,0:T(8,128)(2,1)S(1)}, bf16[128,4096]{1,0:T(8,128)(2,1)S(1)}, u32[]{:S(2)}, u32[]{:S(2)}) collective-permute-start(bf16[128,4096]{1,0:T(8,128)(2,1)S(1)} %constant_dynamic-update-slice_fusion.5.refs_1_), channel_id=1, source_target_pairs={{0,32},{4,12},{8,40},{12,20},{16,48},{20,28},{24,56},{28,4},{32,64... | collective-permute-start | bytes 3145736 | tf_op jit(solution)/shard_map/ppermute | solution.py:40
  134.0 26.4 %collective-permute-start.27 = (bf16[128,4096]{1,0:T(8,128)(2,1)S(1)}, bf16[128,4096]{1,0:T(8,128)(2,1)S(1)}, u32[]{:S(2)}, u32[]{:S(2)}) collective-permute-start(bf16[128,4096]{1,0:T(8,128)(2,1)S(1)} %get-tuple-element.23), channel_id=1, source_target_pairs={{0,96},{4,28},{8,104},{12,4},{16,112},{20,12},{24,120},{28,20},{32... | collective-permute-start | bytes 3145736 | tf_op jit(solution)/shard_map/ppermute | solution.py:40
  147.3 37.5 %collective-permute-start.31 = (bf16[128,4096]{1,0:T(8,128)(2,1)S(1)}, bf16[128,4096]{1,0:T(8,128)(2,1)S(1)}, u32[]{:S(2)}, u32[]{:S(2)}) collective-permute-start(bf16[128,4096]{1,0:T(8,128)(2,1)S(1)} %get-tuple-element.24), channel_id=1, source_target_pairs={{0,32},{4,12},{8,40},{12,20},{16,48},{20,28},{24,56},{28,4},{32,64... | collective-permute-start | bytes 3145736 | tf_op jit(solution)/shard_map/ppermute | solution.py:40
  147.4 40.2 %collective-permute-start.36 = (bf16[128,4096]{1,0:T(8,128)(2,1)S(1)}, bf16[128,4096]{1,0:T(8,128)(2,1)S(1)}, u32[]{:S(2)}, u32[]{:S(2)}) collective-permute-start(bf16[128,4096]{1,0:T(8,128)(2,1)S(1)} %get-tuple-element.28), channel_id=1, source_target_pairs={{0,96},{4,28},{8,104},{12,4},{16,112},{20,12},{24,120},{28,20},{32... | collective-permute-start | bytes 3145736 | tf_op jit(solution)/shard_map/ppermute | solution.py:40
  150.6 24.0 %collective-permute-start.32 = (bf16[128,4096]{1,0:T(8,128)(2,1)S(1)}, bf16[128,4096]{1,0:T(8,128)(2,1)S(1)}, u32[]{:S(2)}, u32[]{:S(2)}) collective-permute-start(bf16[128,4096]{1,0:T(8,128)(2,1)S(1)} %get-tuple-element.26), channel_id=1, source_target_pairs={{0,32},{4,12},{8,40},{12,20},{16,48},{20,28},{24,56},{28,4},{32,64... | collective-permute-start | bytes 3145736 | tf_op jit(solution)/shard_map/ppermute | solution.py:40
  160.7 24.1 %collective-permute-start.28 = (bf16[128,4096]{1,0:T(8,128)(2,1)S(1)}, bf16[128,4096]{1,0:T(8,128)(2,1)S(1)}, u32[]{:S(2)}, u32[]{:S(2)}) collective-permute-start(bf16[128,4096]{1,0:T(8,128)(2,1)S(1)} %add_convert_fusion.3), channel_id=1, source_target_pairs={{0,96},{4,28},{8,104},{12,4},{16,112},{20,12},{24,120},{28,20},{32... | collective-permute-start | bytes 3145736 | tf_op jit(solution)/shard_map/ppermute | solution.py:40
  174.8 16.8 %collective-permute-start.33 = (bf16[128,4096]{1,0:T(8,128)(2,1)S(1)}, bf16[128,4096]{1,0:T(8,128)(2,1)S(1)}, u32[]{:S(2)}, u32[]{:S(2)}) collective-permute-start(bf16[128,4096]{1,0:T(8,128)(2,1)S(1)} %add_convert_fusion.1), channel_id=1, source_target_pairs={{0,32},{4,12},{8,40},{12,20},{16,48},{20,28},{24,56},{28,4},{32,64... | collective-permute-start | bytes 3145736 | tf_op jit(solution)/shard_map/ppermute | solution.py:40
  185.3 18.2 %collective-permute-start.35 = (bf16[64,4096]{1,0:T(8,128)(2,1)S(1)}, bf16[64,4096]{1,0:T(8,128)(2,1)S(1)}, u32[]{:S(2)}, u32[]{:S(2)}) collective-permute-start(bf16[64,4096]{1,0:T(8,128)(2,1)S(1)} %slice.68), channel_id=1, source_target_pairs={{0,24},{4,100},{8,0},{12,108},{16,8},{20,116},{24,16},{28,124},{32... | collective-permute-start | bytes 1572872 | tf_op jit(solution)/shard_map/ppermute | solution.py:40
  193.2 12.4 %collective-permute-start.37 = (bf16[64,4096]{1,0:T(8,128)(2,1)}, bf16[64,4096]{1,0:T(8,128)(2,1)}, u32[]{:S(2)}, u32[]{:S(2)}) collective-permute-start(bf16[64,4096]{1,0:T(8,128)(2,1)} %get-tuple-element.31), channel_id=1, source_target_pairs={{0,8},{4,36},{8,16},{12,44},{16,24},{20,52},{24,0},{28,60},{32,40}... | collective-permute-start | bytes 1572872 | tf_op jit(solution)/shard_map/ppermute | solution.py:40
  193.2 19.5 %collective-permute-start.38 = (bf16[64,4096]{1,0:T(8,128)(2,1)}, bf16[64,4096]{1,0:T(8,128)(2,1)}, u32[]{:S(2)}, u32[]{:S(2)}) collective-permute-start(bf16[64,4096]{1,0:T(8,128)(2,1)} %get-tuple-element.32), channel_id=1, source_target_pairs={{0,16},{4,68},{8,24},{12,76},{16,0},{20,84},{24,8},{28,92},{32,48}... | collective-permute-start | bytes 1572872 | tf_op jit(solution)/shard_map/ppermute | solution.py:40
  200.1 2.1 collective-permute-start.34
  214.3 9.2 %collective-permute-start.39 = (bf16[16,4096]{1,0:T(8,128)(2,1)S(1)}, bf16[16,4096]{1,0:T(8,128)(2,1)S(1)}, u32[]{:S(2)}, u32[]{:S(2)}) collective-permute-start(bf16[16,4096]{1,0:T(8,128)(2,1)S(1)} %get-tuple-element.36), channel_id=1, source_target_pairs={{0,3},{1,0},{2,1},{3,2},{4,7},{5,4},{6,5},{7,6},{8,11},{9,8},{10,9... | collective-permute-start | bytes 393224 | tf_op jit(solution)/shard_map/ppermute | solution.py:48
  215.9 9.1 %collective-permute-start.40 = (bf16[16,4096]{1,0:T(8,128)(2,1)S(1)}, bf16[16,4096]{1,0:T(8,128)(2,1)S(1)}, u32[]{:S(2)}, u32[]{:S(2)}) collective-permute-start(bf16[16,4096]{1,0:T(8,128)(2,1)S(1)} %get-tuple-element.35), channel_id=1, source_target_pairs={{0,2},{1,3},{2,0},{3,1},{4,6},{5,7},{6,4},{7,5},{8,10},{9,11},{10,... | collective-permute-start | bytes 393224 | tf_op jit(solution)/shard_map/ppermute | solution.py:48
  222.1 6.2 %collective-permute-start.41 = (bf16[16,4096]{1,0:T(8,128)(2,1)S(1)}, bf16[16,4096]{1,0:T(8,128)(2,1)S(1)}, u32[]{:S(2)}, u32[]{:S(2)}) collective-permute-start(bf16[16,4096]{1,0:T(8,128)(2,1)S(1)} %get-tuple-element.34), channel_id=1, source_target_pairs={{0,1},{1,2},{2,3},{3,0},{4,5},{5,6},{6,7},{7,4},{8,9},{9,10},{10,1... | collective-permute-start | bytes 393224 | tf_op jit(solution)/shard_map/ppermute | solution.py:48
  (9 other events, 57.2 us)
